TPU v7x, 32 devices: a whole 2x2x4 slice. The times are simulated.
32 devices in a mesh: dp: 8 (over z, x), tensor: 4 (over y, core).
Axes of the slice: x: 2, y: 2, z: 4, core: 2. Of those that a mesh axis runs over, the one named last changes fastest.
Arguments:
- tokens: bfloat16 [2, 512, 4096], P(None, 'dp', 'tensor'), may hold values from -6 to 6
- routes: int32 [2, 512, 2], P(None, 'dp'), may hold values from 0 to 7, all different within a row; in each aligned block of 64 rows (0 to 63, 64 to 127, ..., all dimensions but the last counted through in order) at most 20 rows name the same one
- probs: float32 [2, 512, 8], P(None, 'dp'), may hold values from 0 to 1, as said below
- w_gate: bfloat16 [8, 4096, 14336], P('dp', None, 'tensor'), may hold values from -0.09375 to 0.09375
- w_up: bfloat16 [8, 4096, 14336], P('dp', None, 'tensor'), may hold values from -0.09375 to 0.09375
- w_down: bfloat16 [8, 14336, 4096], P('dp', 'tensor'), may hold values from -0.046875 to 0.046875
Outputs:
- mixed: bfloat16 [2, 512, 4096], P(None, 'dp', 'tensor')
- aux_loss: float32 [2, 8], replicated
Inputs may be any that keep to these rules, and one draw needn't show every extreme that they name: `routes`: in each aligned block of 64 rows (the rows of one index of dp in one micro-batch) no expert is named in more than 20 entries; the 2 experts of a row differ. `probs`: each row is positive and sums to one.
All inputs are finite; a program needn't handle non-finite values.
Results may differ from a plain program's by a relative error of at most 0.012.
Values may be sent and summed in bfloat16 or wider, within the bound.
No kernel may reach another device: no remote copies, remote signals or barrier semaphores. Data moves between devices by JAX's collectives and lax.ppermute only.
A program may use at most 192 MiB of HBM per device.

v0:
```python
import jax
import jax.numpy as jnp
from jax import lax
from jax.sharding import PartitionSpec as P

MICRO = 2
CAP = 20


def slot_tables(route, prob):
    rows_count = route.shape[0]
    experts = prob.shape[-1]
    capacity = CAP
    flat = route.reshape(-1)
    onehot = (flat[:, None] == jnp.arange(experts, dtype=jnp.int32)[None, :]).astype(jnp.int32)
    before = jnp.cumsum(onehot, axis=0) - onehot
    place = jnp.sum(before * onehot, axis=1)
    slot = flat * capacity + place
    picked = jnp.take_along_axis(prob, route, axis=1)
    weights = picked / jnp.sum(picked, axis=1, keepdims=True)
    grid = (slot[:, None] == jnp.arange(experts * capacity, dtype=jnp.int32)[None, :]).astype(
        jnp.float32
    )
    grid = grid.reshape(rows_count, route.shape[1], experts * capacity)
    dispatch = jnp.sum(grid, axis=1).T.astype(jnp.bfloat16)
    combine = jnp.sum(grid * weights[:, :, None], axis=1)
    counts = jnp.sum(onehot, axis=0).astype(jnp.float32)
    return (dispatch, combine, counts)


def spread_slots(slots, experts, copies_per, capacity):
    width = slots.shape[-1]
    wide = jnp.broadcast_to(
        slots.reshape(experts, 1, capacity, width), (experts, copies_per, capacity, width)
    )
    return wide.reshape(experts * copies_per, capacity, width)


def local(tokens, routes, probs, w_gate, w_up, w_down):
    groups = lax.axis_size("dp")
    experts = probs.shape[-1]
    copies_per = groups // experts
    capacity = CAP
    gate_local = w_gate[0]
    up_local = w_up[0]
    down_local = w_down[0]
    rows_local = tokens.shape[1]
    total_rows = rows_local * groups
    top_count = routes.shape[-1]
    tables = [slot_tables(routes[index], probs[index]) for index in range(MICRO)]
    prob_local = [jnp.sum(probs[index], axis=0) for index in range(MICRO)]
    outputs = []
    loss_terms = []
    for micro_index in range(MICRO):
        dispatch, combine, counts = tables[micro_index]
        count_all, prob_all = lax.psum((counts, prob_local[micro_index]), "dp")
        width_local = tokens.shape[2]
        slots = jnp.dot(dispatch, tokens[micro_index], preferred_element_type=jnp.float32).astype(
            jnp.bfloat16
        )
        arrived = lax.all_to_all(
            spread_slots(slots, experts, copies_per, capacity),
            "dp",
            split_axis=0,
            concat_axis=0,
            tiled=True,
        )
        piece = lax.all_gather(arrived, "tensor", axis=2, tiled=True)
        piece_rows = piece.reshape(-1, piece.shape[2])
        gate = jnp.dot(piece_rows, gate_local, preferred_element_type=jnp.float32)
        up = jnp.dot(piece_rows, up_local, preferred_element_type=jnp.float32)
        hidden = (jax.nn.silu(gate) * up).astype(jnp.bfloat16)
        part = jnp.dot(hidden, down_local, preferred_element_type=jnp.float32).astype(jnp.bfloat16)
        reduced = lax.psum_scatter(part, "tensor", scatter_dimension=1, tiled=True).astype(
            jnp.float32
        )
        returned = lax.all_to_all(
            reduced.reshape(groups, capacity, width_local).astype(jnp.bfloat16),
            "dp",
            split_axis=0,
            concat_axis=0,
            tiled=True,
        ).astype(jnp.float32)
        summed = jnp.sum(returned.reshape(experts, copies_per, capacity, width_local), axis=1)
        mixed = jnp.dot(
            combine,
            summed.reshape(experts * capacity, width_local),
            precision=lax.Precision.HIGHEST,
            preferred_element_type=jnp.float32,
        )
        outputs.append(mixed.astype(jnp.bfloat16))
        loss_terms.append(
            experts * (count_all / (total_rows * top_count)) * (prob_all / total_rows)
        )
    return (jnp.stack(outputs), jnp.stack(loss_terms))


def solution(mesh):
    in_specs = (
        P(None, "dp", "tensor"),
        P(None, "dp", None),
        P(None, "dp", None),
        P("dp", None, "tensor"),
        P("dp", None, "tensor"),
        P("dp", "tensor", None),
    )
    out_specs = (P(None, "dp", "tensor"), P())
    return jax.shard_map(local, mesh=mesh, in_specs=in_specs, out_specs=out_specs, check_vma=False)
```

profile of v0, /device:TPU:0, one launch (start us, length us, event | category | flops | bytes accessed | tf_op | source)
XLA Modules:
  0.0 197.0 jit_solution(15916981015399917968)
XLA Ops:
  7.2 0.7 fusion.64
  7.9 0.7 bitcast_or_fusion.1
  8.6 0.1 copy.32
  8.7 0.1 eq.58
  8.8 0.1 fusion.53
  8.9 0.2 reduce_window_sum.17
  9.1 0.2 fusion.54
  9.3 0.1 reduce_sum.121
  9.4 0.1 copy.33
  9.5 0.1 copy.36
  9.6 0.2 eq.65
  9.8 0.1 fusion.52
  9.9 0.2 reduce_window_sum.18
  10.0 0.2 fusion.55
  10.2 0.1 reduce_sum.126
  10.4 0.1 copy.37
  10.4 0.9 slice_reduce_fusion.1
  11.3 0.1 copy.34
  11.4 0.1 reshape.106
  11.5 1.0 gather_fusion
  12.6 0.1 reshape.109
  12.8 0.1 copy.38
  12.9 0.2 reshape.111
  13.0 1.0 gather_fusion.1
  14.1 0.1 reshape.114
  14.3 0.1 convert_reduce_fusion
  14.5 0.3 convolution_convert_fusion
  14.8 19.2 %all_to_all.20 = bf16[8,20,1024]{2,1,0:T(8,128)(2,1)} all-to-all(bf16[8,20,1024]{2,1,0:T(8,128)(2,1)S(1)} %reshape_reshape.7), channel_id=1, replica_groups=mesh['dp'=8,'tensor'=4] {'dp'}, dimensions={0} | all-to-all | bytes 655360 | tf_op jit(solution)/shard_map/all_to_all | solution.py:61
  34.2 0.3 convolution_convert_fusion.1
  34.5 15.1 %all_to_all.21 = bf16[8,20,1024]{2,1,0:T(8,128)(2,1)} all-to-all(bf16[8,20,1024]{2,1,0:T(8,128)(2,1)S(1)} %reshape_reshape.6), channel_id=1, replica_groups=mesh['dp'=8,'tensor'=4] {'dp'}, dimensions={0} | all-to-all | bytes 655360 | tf_op jit(solution)/shard_map/all_to_all | solution.py:61
  49.7 2.9 %all-gather.5.cloned.1.call-done = bf16[8,20,4096]{2,1,0:T(8,128)(2,1)} async-done(((bf16[8,20,1024]{2,1,0:T(8,128)(2,1)}), bf16[8,20,4096]{2,1,0:T(8,128)(2,1)}) %all-gather.5.cloned.1.call-update) | async-done | bytes 1310736 | tf_op jit(solution)/shard_map/all_gather | solution.py:68
  52.6 1.5 reshape.80
  54.1 13.8 %fusion.8 = f32[160,3584]{1,0:T(8,128)} fusion(bf16[160,4096]{1,0:T(8,128)(2,1)S(1)} %reshape.80, bf16[1,4096,3584]{2,1,0:T(8,128)(2,1)} %param.11), kind=kOutput, calls=%fused_computation.10 | convolution fusion | flops 4697620480 | bytes 32964608 | tf_op jit(solution)/shard_map/dot_general | solution.py:70
  68.0 24.3 %fusion.27 = bf16[160,4096]{1,0:T(8,128)(2,1)} fusion(bf16[1,3584,4096]{2,1,0:T(8,128)(2,1)} %param.13, bf16[160,4096]{1,0:T(8,128)(2,1)S(1)} %reshape.80, bf16[1,4096,3584]{2,1,0:T(8,128)(2,1)} %param.12, f32[160,3584]{1,0:T(8,128)} %fusion.8), kind=kOutput, calls=%fused_computation.19 | convolution fusion | flops 9399336960 | bytes 63635456 | tf_op jit(solution)/shard_map/dot_general | solution.py:73
  92.3 0.2 reduce-scatter.3.cloned.1.call-start
  92.5 1.5 reshape.78
  94.0 14.0 %fusion.10 = f32[160,3584]{1,0:T(8,128)} fusion(bf16[160,4096]{1,0:T(8,128)(2,1)S(1)} %reshape.78, bf16[1,4096,3584]{2,1,0:T(8,128)(2,1)} %param.11), kind=kOutput, calls=%fused_computation.12 | convolution fusion | flops 4697620480 | bytes 32964608 | tf_op jit(solution)/shard_map/dot_general | solution.py:70
  108.0 24.5 %fusion.24 = bf16[160,4096]{1,0:T(8,128)(2,1)} fusion(bf16[1,3584,4096]{2,1,0:T(8,128)(2,1)} %param.13, bf16[160,4096]{1,0:T(8,128)(2,1)S(1)} %reshape.78, bf16[1,4096,3584]{2,1,0:T(8,128)(2,1)} %param.12, f32[160,3584]{1,0:T(8,128)} %fusion.10), kind=kOutput, calls=%fused_computation.18 | convolution fusion | flops 9399336960 | bytes 63635456 | tf_op jit(solution)/shard_map/dot_general | solution.py:73
  132.5 1.8 convert_element_type.78
  134.3 5.6 %all-to-all-start.3 = ((bf16[8,20,1024]{2,1,0:T(8,128)(2,1)}), bf16[8,20,1024]{2,1,0:T(8,128)(2,1)S(1)}, u32[]{:S(2)}, u32[]{:S(2)}) async-start(bf16[8,20,1024]{2,1,0:T(8,128)(2,1)} %convert_element_type.78), calls=%async_computation.5 | async-start | bytes 786432 | tf_op jit(solution)/shard_map/all_to_all | solution.py:77
  139.9 19.3 %reduce-scatter.3.cloned.1.call-done = bf16[160,1024]{1,0:T(8,128)(2,1)} async-done(((bf16[160,4096]{1,0:T(8,128)(2,1)}), bf16[160,1024]{1,0:T(8,128)(2,1)}) %reduce-scatter.3.cloned.1.call-update) | async-done | bytes 327696 | tf_op jit(solution)/shard_map/reduce_scatter | solution.py:74
  159.2 1.8 convert_element_type.70
  160.9 5.5 %all-to-all-start.1 = ((bf16[8,20,1024]{2,1,0:T(8,128)(2,1)}), bf16[8,20,1024]{2,1,0:T(8,128)(2,1)S(1)}, u32[]{:S(2)}, u32[]{:S(2)}) async-start(bf16[8,20,1024]{2,1,0:T(8,128)(2,1)} %convert_element_type.70), calls=%async_computation.2 | async-start | bytes 786432 | tf_op jit(solution)/shard_map/all_to_all | solution.py:77
  166.5 21.9 %all-reduce = (f32[8]{0:T(128)S(1)}, f32[8]{0:T(128)S(1)}, f32[8]{0:T(128)S(1)}, f32[8]{0:T(128)S(1)}) all-reduce(f32[8]{0:T(128)S(1)} %get-tuple-element.4, f32[8]{0:T(128)S(1)} %convert_element_type.81, f32[8]{0:T(128)S(1)} %get-tuple-element.3, f32[8]{0:T(128)S(1)} %convert_element_type.80), channel_id=1, replica_groups=mesh['dp'=8,'tensor'=4] {'dp'}, use_global_device_ids=true, to_apply=%region_19.21 | all-reduce | flops 32 | bytes 256 | tf_op jit(solution)/shard_map/psum | solution.py:56
  188.4 0.6 pad_maximum_fusion.1
  189.1 0.3 fusion.47
  189.5 0.3 fusion.46
  189.7 0.7 pad_maximum_fusion
  (28 shorter events, 0.7 us)
Async XLA Ops:
  7.2 45.4 %all-gather.5.cloned.1.call-start = ((), (), s32[]{:S(2)}) async-start(), calls=%async_computation.8 | async-start | bytes 1966080 | tf_op jit(solution)/shard_map/all_gather | solution.py:68
  13.0 1.3 copy-start.1
  13.0 1.5 copy-start
  34.1 58.4 %all-gather.3.cloned.1.call-start = ((), (), s32[]{:S(2)}) async-start(), calls=%async_computation.6 | async-start | bytes 1966080 | tf_op jit(solution)/shard_map/all_gather | solution.py:68
  49.6 82.9 %reduce-scatter.5.cloned.1.call-start = ((), (), s32[]{:S(2)}) async-start(), calls=%async_computation.9 | async-start | bytes 1638400 | tf_op jit(solution)/shard_map/reduce_scatter | solution.py:74
  92.3 66.9 %reduce-scatter.3.cloned.1.call-start = ((), (), s32[]{:S(2)}) async-start(), calls=%async_computation.7 | async-start | bytes 1638400 | tf_op jit(solution)/shard_map/reduce_scatter | solution.py:74
  134.3 26.6 %all-to-all-start.3 = ((bf16[8,20,1024]{2,1,0:T(8,128)(2,1)}), bf16[8,20,1024]{2,1,0:T(8,128)(2,1)S(1)}, u32[]{:S(2)}, u32[]{:S(2)}) async-start(bf16[8,20,1024]{2,1,0:T(8,128)(2,1)} %convert_element_type.78), calls=%async_computation.5 | async-start | bytes 786432 | tf_op jit(solution)/shard_map/all_to_all | solution.py:77
  160.9 28.4 %all-to-all-start.1 = ((bf16[8,20,1024]{2,1,0:T(8,128)(2,1)}), bf16[8,20,1024]{2,1,0:T(8,128)(2,1)S(1)}, u32[]{:S(2)}, u32[]{:S(2)}) async-start(bf16[8,20,1024]{2,1,0:T(8,128)(2,1)} %convert_element_type.70), calls=%async_computation.2 | async-start | bytes 786432 | tf_op jit(solution)/shard_map/all_to_all | solution.py:77
Sparse Core Ops, SparseCore 0:
  34.2 18.3 all-gather.4
  54.2 19.6 all-gather.2
  92.4 26.4 reduce-scatter.4
  132.6 26.4 reduce-scatter.2
where the time goes:
time: 198 us; the launch traced here: 197 us
  matrix products  77.6 us (39%)
  blocking collectives  56.3 us (28%)
  waiting for transfers between devices  22.3 us (11%)
  between operations  14 us (7%)
  starting transfers between devices  11.5 us (6%)
  local copies, waits for them, and re-layouts  11.4 us (6%)
  other arithmetic  3.94 us (2%)
    dot_general x2, matrix products, local(): jnp.dot(hidden, down_local, preferred_element_type=jnp.float32)  48.7 us
    all_to_all x2, blocking collectives, local(): lax.all_to_all(spread_slots(slots, experts, copies_per, capacity), 'dp',...  34.3 us
    dot_general x2, matrix products, local(): gate = jnp.dot(piece_rows, gate_local, preferred_element_type=jnp.float32)  27.8 us
    psum x1, blocking collectives, local(): count_all, prob_all = lax.psum((counts, prob_local[micro_index]), 'dp')  21.9 us
    reduce_scatter x2, waiting for transfers between devices, local(): lax.psum_scatter(part, 'tensor', scatter_dimension=1, tiled=True)  19.3 us
    all_to_all x2, starting transfers between devices, local(): lax.all_to_all(reduced.reshape(groups, capacity, width_local).astype(jnp....  11.1 us
  transfers between devices with their start and end apart: 6, of which 2 were waited for; matrix products, arithmetic and copies ran while one was open for 43% of the time, Pallas kernels for 0%

commit v1 on v0

v1 whole, which is shorter than its diff:
```python
import functools

import jax
import jax.numpy as jnp
from jax import lax
from jax.experimental import pallas as pl
from jax.experimental.pallas import tpu as pltpu
from jax.sharding import PartitionSpec as P


CAP = 20
LANES = 128
PAIR_KEY = 64
IN_CHUNKS = 2
OUT_CHUNKS = 2
DOWN_PARTS = 7


def tile_of(size, most):
    return max(d for d in range(LANES, most + 1, LANES) if size % d == 0)


def places(dims, routes_ref, m):
    dp, cap2, experts = dims
    rows = routes_ref.shape[2]
    at = lax.broadcasted_iota(jnp.int32, (dp * cap2, rows), 0).astype(jnp.float32)
    device = jnp.floor((at + 0.5) * (1.0 / cap2))
    keys = jnp.floor((device + 0.5) * (experts / dp)) * PAIR_KEY + (at - device * cap2)
    earlier = lax.broadcasted_iota(jnp.int32, (rows, rows), 0) < lax.broadcasted_iota(
        jnp.int32, (rows, rows), 1
    )
    ids = lax.broadcasted_iota(jnp.int32, (experts, rows), 0)
    route = routes_ref[m]
    hits = [(route[k : k + 1, :] == ids).astype(jnp.float32) for k in range(2)]
    named = hits[0] + hits[1]
    before = jnp.dot(named, earlier.astype(jnp.float32), preferred_element_type=jnp.float32)
    here = []
    for k in range(2):
        place = jnp.sum(before * hits[k], axis=0, keepdims=True)
        own_key = route[k : k + 1, :].astype(jnp.float32) * PAIR_KEY + (m * CAP + place)
        here.append((keys == own_key).astype(jnp.float32))
    return hits, named, here


def tables_kernel(dims, routes_ref, probs_ref, tokens_ref, sent_ref, aux_ref):
    dp, cap2, experts = dims
    micro = routes_ref.shape[0]
    blocks = tokens_ref.shape[2] // LANES
    aux_ref[...] = jnp.zeros_like(aux_ref)
    slots = jnp.zeros((dp * cap2, tokens_ref.shape[2]), jnp.float32)
    for m in range(micro):
        _, named, here = places(dims, routes_ref, m)
        pick = (here[0] + here[1]).astype(jnp.bfloat16)
        slots = slots + jnp.dot(pick, tokens_ref[m], preferred_element_type=jnp.float32)
        sums = jnp.sum(probs_ref[m], axis=1, keepdims=True)
        aux_ref[0:experts, m : m + 1] = jnp.sum(named, axis=1, keepdims=True)
        for piece in range(3):
            part = sums.astype(jnp.bfloat16).astype(jnp.float32)
            column = (piece + 1) * micro + m
            aux_ref[0:experts, column : column + 1] = part
            sums = sums - part
    slots = slots.astype(jnp.bfloat16)
    aux = aux_ref[...].astype(jnp.bfloat16)
    for d in range(dp):
        for b in range(blocks):
            sent_ref[d, b * cap2 : (b + 1) * cap2, :] = slots[
                d * cap2 : (d + 1) * cap2, b * LANES : (b + 1) * LANES
            ]
        sent_ref[d, blocks * cap2 :, :] = aux


def weights_kernel(dims, routes_ref, probs_ref, combine_ref):
    for m in range(routes_ref.shape[0]):
        hits, _, here = places(dims, routes_ref, m)
        picked = [jnp.sum(probs_ref[m] * hit, axis=0, keepdims=True) for hit in hits]
        total = picked[0] + picked[1]
        combine_ref[m] = here[0] * (picked[0] / total) + here[1] * (picked[1] / total)


def repack_kernel(dims, arrived_ref, *refs):
    dp, cap2, blocks, micro, experts, tokens_all = dims
    xs, loss_ref = refs[:-1], refs[-1]
    per = blocks // len(xs)
    total = jnp.zeros((experts, LANES), jnp.float32)
    for d in range(dp):
        for b in range(blocks):
            xs[b // per][
                d * cap2 : (d + 1) * cap2, b % per * LANES : (b % per + 1) * LANES
            ] = arrived_ref[d, b * cap2 : (b + 1) * cap2, :]
        total = total + arrived_ref[d, blocks * cap2 :, :].astype(jnp.float32)
    count = total[:, 0:micro]
    prob = total[:, 3 * micro : 4 * micro] + total[:, 2 * micro : 3 * micro]
    prob = prob + total[:, micro : 2 * micro]
    loss_ref[...] = experts * (count / (tokens_all * 2)) * (prob / tokens_all)


def gate_up_copies(pieces, here, sources, targets, sems):
    copies = []
    depth = targets[0].shape[0] // len(pieces)
    half = depth // 2
    for i, (quarter, c) in enumerate(pieces):
        start = ((here ^ quarter) * IN_CHUNKS + c) * depth
        for k, (source, target) in enumerate(zip(sources, targets)):
            for part in range(2):
                at = pl.multiple_of(start + part * half, half)
                copies.append(
                    pltpu.make_async_copy(
                        source.at[0, pl.ds(at, half), :],
                        target.at[pl.ds(i * depth + part * half, half), :],
                        sems.at[k, 2 * i + part],
                    )
                )
    return copies


def down_copies(side, parts, here, source, targets, sems):
    copies = []
    half, columns = targets[0].shape
    at = pl.multiple_of(((here >> 1) ^ side) * columns, columns)
    step = half // DOWN_PARTS
    for i, target in zip(parts, targets):
        for part in range(DOWN_PARTS):
            copies.append(
                pltpu.make_async_copy(
                    source.at[0, pl.ds(i * half + part * step, step), pl.ds(at, columns)],
                    target.at[pl.ds(part * step, step), :],
                    sems.at[i, part],
                )
            )
    return copies


def run_copies(copies):
    for copy in copies:
        copy.start()

    def finish():
        for copy in copies:
            copy.wait()

    return finish


def first_kernel(pieces, where_ref, after_ref, w_gate, w_up, gate_ref, up_ref, sems):
    sources, targets = (w_gate, w_up), (gate_ref, up_ref)
    run_copies(gate_up_copies(pieces, where_ref[0], sources, targets, sems))()


def gate_up_kernel(plan, where_ref, *refs):
    count, first, following, tile = plan
    last = following is None
    xs, refs = refs[:count], refs[count:]
    gate_w, up_w, refs = refs[0], refs[1], refs[2:]
    if not first:
        gate_in, up_in, refs = refs[0], refs[1], refs[2:]
    here = where_ref[0]
    if last:
        w_down, out_ref, next_a, next_b, sems = refs
        copies = down_copies(1, (0, 1), here, w_down, (next_a, next_b), sems)
    else:
        w_gate, w_up, gate_out, up_out, next_a, next_b, sems = refs
        copies = gate_up_copies(following, here, (w_gate, w_up), (next_a, next_b), sems)
    finish = run_copies(copies)
    depth = gate_w.shape[0] // count

    def step(j, carry):
        columns = pl.ds(pl.multiple_of(j * tile, tile), tile)
        if first:
            gate = up = 0.0
        else:
            gate, up = gate_in[:, columns], up_in[:, columns]
        for i, x in enumerate(xs):
            rows = slice(i * depth, (i + 1) * depth)
            gate = gate + jnp.dot(
                x[...], gate_w[rows, columns], preferred_element_type=jnp.float32
            )
            up = up + jnp.dot(x[...], up_w[rows, columns], preferred_element_type=jnp.float32)
        if last:
            out_ref[:, columns] = (gate / (1.0 + jnp.exp(-gate)) * up).astype(jnp.bfloat16)
        else:
            gate_out[:, columns] = gate
            up_out[:, columns] = up
        return carry

    lax.fori_loop(0, gate_w.shape[1] // tile, step, 0)
    finish()


VMEM = pl.BlockSpec(memory_space=pltpu.VMEM)
SMEM = pl.BlockSpec(memory_space=pltpu.SMEM)
HBM = pl.BlockSpec(memory_space=pltpu.HBM)


def first_weights(where, pieces, after, w_gate, w_up, depth):
    width = w_gate.shape[2]
    return pl.pallas_call(
        functools.partial(first_kernel, pieces),
        in_specs=[SMEM, HBM, HBM, HBM],
        out_specs=[VMEM] * 2,
        out_shape=[pltpu.VMEM((depth, width), jnp.bfloat16)] * 2,
        scratch_shapes=[pltpu.SemaphoreType.DMA((2, 2 * len(pieces)))],
        compiler_params=pltpu.CompilerParams(vmem_limit_bytes=1 << 20),
        name="first",
    )(where, after, w_gate, w_up)


def gate_up(where, xs, weights, totals, following, w_gate, w_up, w_down):
    rows = xs[0].shape[0]
    depth, width = weights[0].shape
    last = following is None
    if last:
        sources = [w_down]
        out_shape = [pltpu.VMEM((rows, width), jnp.bfloat16)]
        out_shape += [pltpu.VMEM((width // 2, w_down.shape[2] // 2), jnp.bfloat16)] * 2
    else:
        sources = [w_gate, w_up]
        out_shape = [pltpu.VMEM((rows, width), jnp.float32)] * 2
        out_shape += [pltpu.VMEM((depth, width), jnp.bfloat16)] * 2
    plan = (len(xs), totals is None, following, tile_of(width, 512))
    totals = totals or []
    at = 1 + len(xs) + 2
    return pl.pallas_call(
        functools.partial(gate_up_kernel, plan),
        in_specs=[SMEM] + [VMEM] * (len(xs) + 2 + len(totals)) + [HBM] * len(sources),
        out_specs=[VMEM] * len(out_shape),
        out_shape=out_shape,
        scratch_shapes=[pltpu.SemaphoreType.DMA((2, max(4, DOWN_PARTS)))],
        input_output_aliases={} if last or not totals else {at + i: i for i in range(2)},
        compiler_params=pltpu.CompilerParams(vmem_limit_bytes=8 << 20),
        cost_estimate=pl.CostEstimate(
            flops=4 * rows * depth * width, transcendentals=0, bytes_accessed=4 * depth * width
        ),
    )(where, *xs, *weights, *totals, *sources)


def down_kernel(plan, where_ref, h_ref, w_a, w_b, after_ref, *refs):
    c, part, tile, columns = plan
    here = where_ref[0]
    if part is None:
        keep_ref, send_ref, token_ref = refs
        finish = None
    else:
        w_down, keep_ref, send_ref, token_ref, next_ref, sems = refs
        finish = run_copies(down_copies(0, (part,), here, w_down, (next_ref,), sems))
    quarter = columns * OUT_CHUNKS
    half = w_a.shape[0]
    for p, out_ref in enumerate((keep_ref, send_ref)):
        start = ((here & 1) ^ p) * quarter + c * columns
        for j in range(columns // tile):
            at = pl.ds(pl.multiple_of(start + j * tile, tile), tile)
            total = jnp.dot(h_ref[:, :half], w_a[:, at], preferred_element_type=jnp.float32)
            total = total + jnp.dot(
                h_ref[:, half:], w_b[:, at], preferred_element_type=jnp.float32
            )
            out_ref[:, j * tile : (j + 1) * tile] = total.astype(out_ref.dtype)
    token_ref[...] = jnp.zeros_like(token_ref)
    if finish is not None:
        finish()


def down(where, c, h, weights, after, part, w_down):
    rows, depth = h.shape
    half, both = weights[0].shape
    columns = both // 2 // OUT_CHUNKS
    out_shape = [
        pltpu.VMEM((rows, columns), jnp.float32),
        pltpu.VMEM((rows, columns), jnp.bfloat16),
        jax.ShapeDtypeStruct((8, LANES), jnp.float32),
    ]
    more = part is not None
    if more:
        out_shape.append(pltpu.VMEM((half, both), jnp.bfloat16))
    return pl.pallas_call(
        functools.partial(down_kernel, (c, part, tile_of(columns, 512), columns)),
        in_specs=[SMEM, VMEM, VMEM, VMEM, HBM] + [HBM] * more,
        out_specs=[VMEM] * len(out_shape),
        out_shape=out_shape,
        scratch_shapes=[pltpu.SemaphoreType.DMA((2, DOWN_PARTS))] * more,
        compiler_params=pltpu.CompilerParams(vmem_limit_bytes=8 << 20),
        cost_estimate=pl.CostEstimate(
            flops=4 * rows * depth * columns, transcendentals=0, bytes_accessed=4 * depth * columns
        ),
    )(where, h, *weights, after, *([w_down] * more))


def combine_kernel(combine_ref, *refs):
    parts, out_ref = refs[:-1], refs[-1]
    micro, _, rows = combine_ref.shape
    left = jnp.concatenate([combine_ref[m].T for m in range(micro)], axis=0)
    pieces = []
    for _ in range(3):
        piece = left.astype(jnp.bfloat16)
        pieces.append(piece)
        left = left - piece.astype(jnp.float32)
    pieces = jnp.concatenate(pieces, axis=0)
    each = micro * rows
    for at, part in enumerate(parts):
        width = part.shape[1]
        total = jnp.dot(pieces, part[...], preferred_element_type=jnp.float32)
        total = (total[2 * each :] + total[each : 2 * each]) + total[:each]
        total = total.astype(jnp.bfloat16)
        for m in range(micro):
            out_ref[m, :, at * width : (at + 1) * width] = total[m * rows : (m + 1) * rows]


def local(dp, tensor, tokens, routes, probs, w_gate, w_up, w_down):
    micro, rows, features = tokens.shape
    experts = probs.shape[-1]
    cap2 = micro * CAP
    blocks = features // LANES
    slots_all = dp * cap2
    where = lax.axis_index("tensor")[None]
    w_gate, w_up, w_down = (
        pltpu.with_memory_space_constraint(w, pltpu.HBM) for w in (w_gate, w_up, w_down)
    )
    core = [(t, t ^ 1) for t in range(tensor)]
    row = [(t, t ^ 2) for t in range(tensor)]

    width = features // IN_CHUNKS
    dims = (dp, cap2, experts)
    routes, probs = routes.transpose(0, 2, 1), probs.transpose(0, 2, 1)
    sent = pl.pallas_call(
        functools.partial(tables_kernel, dims),
        out_shape=pltpu.VMEM((dp, blocks * cap2 + experts, LANES), jnp.bfloat16),
        scratch_shapes=[pltpu.VMEM((experts, LANES), jnp.float32)],
        compiler_params=pltpu.CompilerParams(vmem_limit_bytes=24 << 20),
        name="tables",
    )(*(pltpu.with_memory_space_constraint(a, pltpu.HBM) for a in (routes, probs, tokens)))
    arrived = lax.all_to_all(sent, "dp", split_axis=0, concat_axis=0, tiled=True)
    combine = pl.pallas_call(
        functools.partial(weights_kernel, dims),
        out_shape=jax.ShapeDtypeStruct((micro, slots_all, rows), jnp.float32),
        compiler_params=pltpu.CompilerParams(vmem_limit_bytes=8 << 20),
        name="weights",
    )(routes, probs)
    *xs, loss = pl.pallas_call(
        functools.partial(repack_kernel, (dp, cap2, blocks, micro, experts, rows * dp)),
        out_shape=[pltpu.VMEM((slots_all, width), jnp.bfloat16)] * IN_CHUNKS
        + [jax.ShapeDtypeStruct((experts, micro), jnp.float32)],
        compiler_params=pltpu.CompilerParams(vmem_limit_bytes=4 << 20),
        name="repack",
    )(pltpu.with_memory_space_constraint(arrived, pltpu.VMEM))
    paired, crossed = [], []
    for x in xs:
        paired.append(lax.ppermute(x, "tensor", core))
        crossed.append(lax.ppermute(x, "tensor", row))
    chunks = range(IN_CHUNKS)
    stages = [[(q, c) for c in chunks] for q in range(2)] + [[(2, c), (3, c)] for c in chunks]
    operands = [xs, paired]
    for c in chunks:
        operands.append([crossed[c], lax.ppermute(crossed[c], "tensor", core)])
    weights = first_weights(where, stages[0], loss, w_gate, w_up, features)
    totals = None
    for at, pieces in enumerate(operands):
        following = stages[at + 1] if at + 1 < len(stages) else None
        made = gate_up(where, pieces, weights, totals, following, w_gate, w_up, w_down)
        totals, weights = made[:-2], made[-2:]
    hidden = totals[0]

    returned = []
    kept = {}
    width = features // OUT_CHUNKS
    token = loss
    for side in (1, 0):
        upcoming = []
        for c in range(OUT_CHUNKS):
            keep, send, token, *more = down(
                where, c, hidden, weights, token, c if side else None, w_down
            )
            upcoming += more
            kept[side, c] = (keep, lax.ppermute(send, "tensor", core))
        weights = upcoming
    crossed = []
    for c in range(OUT_CHUNKS):
        keep, got = kept[1, c]
        total = (keep + got.astype(jnp.float32)).astype(jnp.bfloat16)
        crossed.append(lax.ppermute(total, "tensor", row))
    for c in range(OUT_CHUNKS):
        keep, got = kept[0, c]
        total = keep + got.astype(jnp.float32) + crossed[c].astype(jnp.float32)
        total = total.astype(jnp.bfloat16).reshape(dp, cap2, width)
        back = lax.all_to_all(total, "dp", split_axis=0, concat_axis=0, tiled=True)
        back = pltpu.with_memory_space_constraint(back.reshape(slots_all, width), pltpu.VMEM)
        returned.append(back)
    mixed = pl.pallas_call(
        combine_kernel,
        out_shape=jax.ShapeDtypeStruct((micro, rows, features), jnp.bfloat16),
        compiler_params=pltpu.CompilerParams(vmem_limit_bytes=16 << 20),
        name="combine",
    )(combine, *returned)
    return mixed, loss.T


def solution(mesh):
    dp, tensor = mesh.shape["dp"], mesh.shape["tensor"]
    in_specs = (
        P(None, "dp", "tensor"),
        P(None, "dp", None),
        P(None, "dp", None),
        P("dp", None, "tensor"),
        P("dp", None, "tensor"),
        P("dp", "tensor", None),
    )
    out_specs = (P(None, "dp", "tensor"), P())


    def body(*args):
        return local(dp, tensor, *args)

    return jax.shard_map(
        body, mesh=mesh, in_specs=in_specs, out_specs=out_specs, check_vma=False
    )
```

time: 198 us -> 125 us (0.63)
  matrix products: 77.6 us -> 0 us
  blocking collectives: 56.3 us -> 0 us
  Pallas kernels: 0 us -> 49.8 us
  waiting for transfers between devices: 22.3 us -> 45.5 us
  between operations: 14 us -> 0.79 us
  starting transfers between devices: 11.5 us -> 20.2 us
  local copies, waits for them, and re-layouts: 11.4 us -> 6.65 us
    dot_general x8 -> x0, matrix products: 77.6 us -> none  [the longest x2 48.7 us: local(): jnp.dot(hidden, down_local, preferred_element_type=jnp.float32)]
    pallas_call x0 -> x13, Pallas kernels: none -> 49.8 us  [the longest x4 25.4 us: gate_up(): pl.pallas_call(functools.partial(gate_up_kernel, plan), in_specs=[SMEM] +...]
    all_to_all x2 -> x0, blocking collectives: 34.3 us -> none  [local(): lax.all_to_all(spread_slots(slots, experts, copies_per, capacity), 'dp',...]
    all_to_all x2 -> x3, waiting for transfers between devices: 0.01 us -> 32.2 us  [the longest x1 17.6 us: local(): lax.all_to_all(sent, 'dp', split_axis=0, concat_axis=0, tiled=True)]
    psum x1 -> x0, blocking collectives: 21.9 us -> none  [local(): count_all, prob_all = lax.psum((counts, prob_local[micro_index]), 'dp')]
    reduce_scatter x2 -> x0, waiting for transfers between devices: 19.3 us -> none  [local(): lax.psum_scatter(part, 'tensor', scatter_dimension=1, tiled=True)]
    ppermute x0 -> x12, waiting for transfers between devices: none -> 13.3 us  [the longest x2 9.98 us: local(): crossed.append(lax.ppermute(total, 'tensor', row))]
    unnamed x4 -> x9, local copies, waits for them, and re-layouts: 0.01 us -> 6.65 us
  transfers between devices with their start and end apart: 6 -> 15, of which waited for: 2 -> 6; matrix products, arithmetic and copies ran while one was open for 43% -> 2% of each run, Pallas kernels for 0% -> 24%
where the time goes in v1:
time: 125 us
  Pallas kernels  49.8 us (40%)
  waiting for transfers between devices  45.5 us (36%)
  starting transfers between devices  20.2 us (16%)
  local copies, waits for them, and re-layouts  6.65 us (5%)
  other arithmetic  1.99 us (2%)
    pallas_call x4, Pallas kernels, gate_up(): pl.pallas_call(functools.partial(gate_up_kernel, plan), in_specs=[SMEM] +...  25.4 us
    all_to_all x1, waiting for transfers between devices, local(): lax.all_to_all(sent, 'dp', split_axis=0, concat_axis=0, tiled=True)  17.6 us
    pallas_call x4, Pallas kernels, down(): pl.pallas_call(functools.partial(down_kernel, (c, part, tile_of(columns,...  14.9 us
    all_to_all x2, waiting for transfers between devices, local(): back = lax.all_to_all(total, 'dp', split_axis=0, concat_axis=0, tiled=True)  14.5 us
    ppermute x2, waiting for transfers between devices, local(): crossed.append(lax.ppermute(total, 'tensor', row))  9.98 us
    all_to_all x1, starting transfers between devices, local(): lax.all_to_all(sent, 'dp', split_axis=0, concat_axis=0, tiled=True)  7.28 us
    all_to_all x2, starting transfers between devices, local(): back = lax.all_to_all(total, 'dp', split_axis=0, concat_axis=0, tiled=True)  7.24 us
    unnamed x9, local copies, waits for them, and re-layouts  6.65 us
  transfers between devices with their start and end apart: 15, of which 6 were waited for; matrix products, arithmetic and copies ran while one was open for 2% of the time, Pallas kernels for 24%

profile of v1, /device:TPU:0, one launch (start us, length us, event | category | flops | bytes accessed | tf_op | source)
XLA Modules:
  0.0 124.9 jit_solution(15112988800997411451)
XLA Ops:
  0.6 2.4 %tables.1 = bf16[8,328,128]{2,1,0:T(8,128)(2,1)} custom-call(s32[2,2,64]{2,1,0:T(2,128)} %bitcast.13, f32[2,8,64]{2,1,0:T(8,128)} %bitcast.11, bf16[2,64,1024]{2,1,0:T(8,128)(2,1)} %tokens_ref.1), custom_call_target="tpu_custom_call" | custom-call | tf_op jit(solution)/shard_map/tables/pallas_call | solution.py:322
  3.1 7.3 %all-to-all-start = ((bf16[8,328,128]{2,1,0:T(8,128)(2,1)}), bf16[8,328,128]{2,1,0:T(8,128)(2,1)S(1)}, u32[]{:S(2)}, u32[]{:S(2)}) async-start(bf16[8,328,128]{2,1,0:T(8,128)(2,1)} %tables.1), calls=%async_computation | async-start | bytes 1343488 | tf_op jit(solution)/shard_map/all_to_all | solution.py:329
  10.3 17.6 %all-to-all-done.arrived_ref = bf16[8,328,128]{2,1,0:T(8,128)(2,1)S(1)} async-done(((bf16[8,328,128]{2,1,0:T(8,128)(2,1)}), bf16[8,328,128]{2,1,0:T(8,128)(2,1)S(1)}, u32[]{:S(2)}, u32[]{:S(2)}) %all-to-all-start) | async-done | bytes 671776 | tf_op jit(solution)/shard_map/all_to_all | solution.py:329
  28.0 0.2 repack.1
  28.1 0.0 collective-permute-start.4
  28.2 1.6 %collective-permute-start.2 = (bf16[320,512]{1,0:T(8,128)(2,1)S(1)}, bf16[320,512]{1,0:T(8,128)(2,1)S(1)}, u32[]{:S(2)}, u32[]{:S(2)}) collective-permute-start(bf16[320,512]{1,0:T(8,128)(2,1)S(1)} %get-tuple-element.36.refs_0_), channel_id=1, source_target_pairs={{0,2},{1,3},{2,0},{3,1},{4,6},{5,7},{6,4},{7,5},{8,10},{9,11},{10,... | collective-permute-start | bytes 983048 | tf_op jit(solution)/shard_map/ppermute | solution.py:346
  29.8 0.2 collective-permute-start.5
  29.9 0.5 collective-permute-start
  30.4 5.3 %first.1 = (bf16[1024,3584]{1,0:T(8,128)(2,1)S(1)}, bf16[1024,3584]{1,0:T(8,128)(2,1)S(1)}) custom-call(s32[1]{0:T(128)} %bitcast.2.where_ref, f32[8,2]{1,0:T(8,128)S(1)} %get-tuple-element.37.after_ref, bf16[1,4096,3584]{2,1,0:T(8,128)(2,1)} %refs_6_.4, bf16[1,4096,3584]{2,1,0:T(8,128)(2,1)} %refs_7_.3), custom_call_target="tpu_custom_call" | custom-call | tf_op jit(solution)/shard_map/first/pallas_call | solution.py:196
  35.8 6.1 %shard_map.77 = (f32[320,3584]{1,0:T(8,128)S(1)}, f32[320,3584]{1,0:T(8,128)S(1)}, bf16[1024,3584]{1,0:T(8,128)(2,1)S(1)}, bf16[1024,3584]{1,0:T(8,128)(2,1)S(1)}) custom-call(s32[1]{0:T(128)} %bitcast.2.where_ref, bf16[320,512]{1,0:T(8,128)(2,1)S(1)} %get-tuple-element.36.refs_0_, bf16[320,512]{1,0:T(8,128)(2,1)S(1)} %get-tuple-element.35.refs_1_, ...), custom_call_target="tpu_custom_call" | custom-call | flops 4697620480 | bytes 14680064 | tf_op jit(solution)/shard_map/pallas_call | solution.py:222
  41.8 0.1 collective-permute-start.3
  42.0 3.3 %collective-permute-done.refs_0_ = bf16[320,512]{1,0:T(8,128)(2,1)S(1)} collective-permute-done((bf16[320,512]{1,0:T(8,128)(2,1)S(1)}, bf16[320,512]{1,0:T(8,128)(2,1)S(1)}, u32[]{:S(2)}, u32[]{:S(2)}) %collective-permute-start) | collective-permute-done | bytes 327712 | tf_op jit(solution)/shard_map/ppermute | solution.py:346
  45.3 0.0 collective-permute-start.1
  45.3 0.0 collective-permute-done.4.refs_0_
  45.3 0.0 collective-permute-done.5.refs_1_
  45.3 6.5 %shard_map.78 = (f32[320,3584]{1,0:T(8,128)S(1)}, f32[320,3584]{1,0:T(8,128)S(1)}, bf16[1024,3584]{1,0:T(8,128)(2,1)S(1)}, bf16[1024,3584]{1,0:T(8,128)(2,1)S(1)}) custom-call(s32[1]{0:T(128)} %bitcast.2.where_ref, bf16[320,512]{1,0:T(8,128)(2,1)S(1)} %collective-permute-done.4.refs_0_, ...), custom_call_target="tpu_custom_call", output_to_operand_aliasing={{0}: (5, {}), {1}: (6, {})} | custom-call | flops 4697620480 | bytes 14680064 | tf_op jit(solution)/shard_map/pallas_call | solution.py:222
  51.8 0.0 collective-permute-done.3.refs_1_
  51.8 6.5 %shard_map.79 = (f32[320,3584]{1,0:T(8,128)S(1)}, f32[320,3584]{1,0:T(8,128)S(1)}, bf16[1024,3584]{1,0:T(8,128)(2,1)S(1)}, bf16[1024,3584]{1,0:T(8,128)(2,1)S(1)}) custom-call(s32[1]{0:T(128)} %bitcast.2.where_ref, bf16[320,512]{1,0:T(8,128)(2,1)S(1)} %collective-permute-done.2.refs_0_, ...), custom_call_target="tpu_custom_call", output_to_operand_aliasing={{0}: (5, {}), {1}: (6, {})} | custom-call | flops 4697620480 | bytes 14680064 | tf_op jit(solution)/shard_map/pallas_call | solution.py:222
  58.3 2.9 %copy-done = bf16[1024,3584]{1,0:T(8,128)(2,1)} copy-done((bf16[1024,3584]{1,0:T(8,128)(2,1)}, bf16[1024,3584]{1,0:T(8,128)(2,1)S(1)}, u32[]{:S(2)}) %copy-start) | copy-done | bytes 7340056
  61.2 3.1 %copy-done.1 = bf16[1024,3584]{1,0:T(8,128)(2,1)S(1)} copy-done((bf16[1024,3584]{1,0:T(8,128)(2,1)S(1)}, bf16[1024,3584]{1,0:T(8,128)(2,1)}, u32[]{:S(2)}) %copy-start.1) | copy-done | bytes 7340056
  64.3 6.4 %shard_map.80 = (bf16[320,3584]{1,0:T(8,128)(2,1)S(1)}, bf16[1792,2048]{1,0:T(8,128)(2,1)S(1)}, bf16[1792,2048]{1,0:T(8,128)(2,1)S(1)}) custom-call(s32[1]{0:T(128)} %bitcast.2.where_ref, bf16[320,512]{1,0:T(8,128)(2,1)S(1)} %collective-permute-done.refs_0_, bf16[320,512]{1,0:T(8,128)(2,1)S(1)} %collective-permute-done.1.refs_1_, ...), custom_call_target="tpu_custom_call" | custom-call | flops 4697620480 | bytes 14680064 | tf_op jit(solution)/shard_map/pallas_call | solution.py:222
  70.7 4.7 %shard_map.81 = (f32[320,512]{1,0:T(8,128)S(1)}, bf16[320,512]{1,0:T(8,128)(2,1)S(1)}, f32[8,128]{1,0:T(8,128)S(1)}, bf16[1792,2048]{1,0:T(8,128)(2,1)S(1)}) custom-call(s32[1]{0:T(128)} %bitcast.2.where_ref, bf16[320,3584]{1,0:T(8,128)(2,1)S(1)} %get-tuple-element.52.h_ref, bf16[1792,2048]{1,0:T(8,128)(2,1)S(1)} %get-tuple-element.53.w_a, ...), custom_call_target="tpu_custom_call" | custom-call | flops 2348810240 | bytes 7340032 | tf_op jit(solution)/shard_map/pallas_call | solution.py:273
  75.4 4.8 %shard_map.82 = (f32[320,512]{1,0:T(8,128)S(1)}, bf16[320,512]{1,0:T(8,128)(2,1)S(1)}, f32[8,128]{1,0:T(8,128)S(1)}, bf16[1792,2048]{1,0:T(8,128)(2,1)S(1)}) custom-call(s32[1]{0:T(128)} %bitcast.2.where_ref, bf16[320,3584]{1,0:T(8,128)(2,1)S(1)} %get-tuple-element.52.h_ref, bf16[1792,2048]{1,0:T(8,128)(2,1)S(1)} %get-tuple-element.53.w_a, ...), custom_call_target="tpu_custom_call" | custom-call | flops 2348810240 | bytes 7340032 | tf_op jit(solution)/shard_map/pallas_call | solution.py:273
  80.1 0.5 collective-permute-start.10
  80.7 0.1 collective-permute-start.7
  80.8 2.5 %shard_map.83 = (f32[320,512]{1,0:T(8,128)S(1)}, bf16[320,512]{1,0:T(8,128)(2,1)S(1)}, f32[8,128]{1,0:T(8,128)S(1)}) custom-call(s32[1]{0:T(128)} %bitcast.2.where_ref, bf16[320,3584]{1,0:T(8,128)(2,1)S(1)} %get-tuple-element.52.h_ref, bf16[1792,2048]{1,0:T(8,128)(2,1)S(1)} %get-tuple-element.55.w_a, bf16[1792,2048]{1,0:T(8,128)(2,1)S(1)} %get-tuple-element.57.w_b, ...), custom_call_target="tpu_custom_call" | custom-call | flops 2348810240 | bytes 7340032 | tf_op jit(solution)/shard_map/pallas_call | solution.py:273
  83.3 0.0 copy-start.2
  83.3 0.0 copy-start.3
  83.3 3.0 %shard_map.84 = (f32[320,512]{1,0:T(8,128)S(1)}, bf16[320,512]{1,0:T(8,128)(2,1)S(1)}, f32[8,128]{1,0:T(8,128)}) custom-call(s32[1]{0:T(128)} %bitcast.2.where_ref, bf16[320,3584]{1,0:T(8,128)(2,1)S(1)} %get-tuple-element.52.h_ref, bf16[1792,2048]{1,0:T(8,128)(2,1)S(1)} %get-tuple-element.55.w_a, bf16[1792,2048]{1,0:T(8,128)(2,1)S(1)} %get-tuple-element.57.w_b, ...), custom_call_target="tpu_custom_call" | custom-call | flops 2348810240 | bytes 7340032 | tf_op jit(solution)/shard_map/pallas_call | solution.py:273
  86.3 0.4 collective-permute-start.9
  86.7 0.1 add_convert_fusion.1
  86.8 1.6 %collective-permute-start.11 = (bf16[320,512]{1,0:T(8,128)(2,1)S(1)}, bf16[320,512]{1,0:T(8,128)(2,1)S(1)}, u32[]{:S(2)}, u32[]{:S(2)}) collective-permute-start(bf16[320,512]{1,0:T(8,128)(2,1)S(1)} %add_convert_fusion.1), channel_id=1, source_target_pairs={{0,2},{1,3},{2,0},{3,1},{4,6},{5,7},{6,4},{7,5},{8,10},{9,11},{10,... | collective-permute-start | bytes 983048 | tf_op jit(solution)/shard_map/ppermute | solution.py:377
  88.4 0.0 collective-permute-start.6
  88.4 0.0 collective-permute-done.7
  88.4 0.1 add_convert_fusion.3
  88.5 0.6 collective-permute-start.8
  89.1 8.4 %collective-permute-done.11 = bf16[320,512]{1,0:T(8,128)(2,1)S(1)} collective-permute-done((bf16[320,512]{1,0:T(8,128)(2,1)S(1)}, bf16[320,512]{1,0:T(8,128)(2,1)S(1)}, u32[]{:S(2)}, u32[]{:S(2)}) %collective-permute-start.11) | collective-permute-done | bytes 327712 | tf_op jit(solution)/shard_map/ppermute | solution.py:377
  97.5 0.9 add_convert_fusion
  98.4 3.6 %all-to-all-start.2 = ((bf16[8,40,512]{2,1,0:T(8,128)(2,1)}), bf16[8,40,512]{2,1,0:T(8,128)(2,1)S(1)}, u32[]{:S(2)}, u32[]{:S(2)}) async-start(bf16[8,40,512]{2,1,0:T(8,128)(2,1)} %bitcast.5), calls=%async_computation.2 | async-start | bytes 655360 | tf_op jit(solution)/shard_map/all_to_all | solution.py:382
  102.0 0.0 collective-permute-done.6
  102.0 1.6 %collective-permute-done.8 = bf16[320,512]{1,0:T(8,128)(2,1)S(1)} collective-permute-done((bf16[320,512]{1,0:T(8,128)(2,1)S(1)}, bf16[320,512]{1,0:T(8,128)(2,1)S(1)}, u32[]{:S(2)}, u32[]{:S(2)}) %collective-permute-start.8) | collective-permute-done | bytes 327712 | tf_op jit(solution)/shard_map/ppermute | solution.py:377
  103.6 0.9 add_convert_fusion.2
  104.5 6.3 %all-to-all-done.2 = bf16[8,40,512]{2,1,0:T(8,128)(2,1)S(1)} async-done(((bf16[8,40,512]{2,1,0:T(8,128)(2,1)}), bf16[8,40,512]{2,1,0:T(8,128)(2,1)S(1)}, u32[]{:S(2)}, u32[]{:S(2)}) %all-to-all-start.2) | async-done | bytes 327712 | tf_op jit(solution)/shard_map/all_to_all | solution.py:382
  110.8 3.6 %all-to-all-start.1 = ((bf16[8,40,512]{2,1,0:T(8,128)(2,1)}), bf16[8,40,512]{2,1,0:T(8,128)(2,1)S(1)}, u32[]{:S(2)}, u32[]{:S(2)}) async-start(bf16[8,40,512]{2,1,0:T(8,128)(2,1)} %bitcast.3), calls=%async_computation.1 | async-start | bytes 655360 | tf_op jit(solution)/shard_map/all_to_all | solution.py:382
  114.4 0.2 weights.1.combine_ref
  114.7 0.6 copy.12
  115.3 8.2 %all-to-all-done.1 = bf16[8,40,512]{2,1,0:T(8,128)(2,1)S(1)} async-done(((bf16[8,40,512]{2,1,0:T(8,128)(2,1)}), bf16[8,40,512]{2,1,0:T(8,128)(2,1)S(1)}, u32[]{:S(2)}, u32[]{:S(2)}) %all-to-all-start.1) | async-done | bytes 327712 | tf_op jit(solution)/shard_map/all_to_all | solution.py:382
  123.5 1.3 %combine.1 = bf16[2,64,1024]{2,1,0:T(8,128)(2,1)} custom-call(f32[2,320,64]{2,1,0:T(8,128)S(1)} %weights.1.combine_ref, bf16[320,512]{1,0:T(8,128)(2,1)S(1)} %bitcast.9, bf16[320,512]{1,0:T(8,128)(2,1)S(1)} %bitcast.8), custom_call_target="tpu_custom_call" | custom-call | tf_op jit(solution)/shard_map/combine/pallas_call | solution.py:385
  (8 shorter events, 0.0 us)
Async XLA Ops:
  3.1 24.9 %all-to-all-start = ((bf16[8,328,128]{2,1,0:T(8,128)(2,1)}), bf16[8,328,128]{2,1,0:T(8,128)(2,1)S(1)}, u32[]{:S(2)}, u32[]{:S(2)}) async-start(bf16[8,328,128]{2,1,0:T(8,128)(2,1)} %tables.1), calls=%async_computation | async-start | bytes 1343488 | tf_op jit(solution)/shard_map/all_to_all | solution.py:329
  28.1 17.2 %collective-permute-start.4 = (bf16[320,512]{1,0:T(8,128)(2,1)S(1)}, bf16[320,512]{1,0:T(8,128)(2,1)S(1)}, u32[]{:S(2)}, u32[]{:S(2)}) collective-permute-start(bf16[320,512]{1,0:T(8,128)(2,1)S(1)} %get-tuple-element.36.refs_0_), channel_id=1, source_target_pairs={{0,1},{1,0},{2,3},{3,2},{4,5},{5,4},{6,7},{7,6},{8,9},{9,8},{10,11... | collective-permute-start | bytes 983048 | tf_op jit(solution)/shard_map/ppermute | solution.py:345
  28.2 13.6 %collective-permute-start.2 = (bf16[320,512]{1,0:T(8,128)(2,1)S(1)}, bf16[320,512]{1,0:T(8,128)(2,1)S(1)}, u32[]{:S(2)}, u32[]{:S(2)}) collective-permute-start(bf16[320,512]{1,0:T(8,128)(2,1)S(1)} %get-tuple-element.36.refs_0_), channel_id=1, source_target_pairs={{0,2},{1,3},{2,0},{3,1},{4,6},{5,7},{6,4},{7,5},{8,10},{9,11},{10,... | collective-permute-start | bytes 983048 | tf_op jit(solution)/shard_map/ppermute | solution.py:346
  29.8 15.6 %collective-permute-start.5 = (bf16[320,512]{1,0:T(8,128)(2,1)S(1)}, bf16[320,512]{1,0:T(8,128)(2,1)S(1)}, u32[]{:S(2)}, u32[]{:S(2)}) collective-permute-start(bf16[320,512]{1,0:T(8,128)(2,1)S(1)} %get-tuple-element.35.refs_1_), channel_id=1, source_target_pairs={{0,1},{1,0},{2,3},{3,2},{4,5},{5,4},{6,7},{7,6},{8,9},{9,8},{10,11... | collective-permute-start | bytes 983048 | tf_op jit(solution)/shard_map/ppermute | solution.py:345
  29.9 15.4 %collective-permute-start = (bf16[320,512]{1,0:T(8,128)(2,1)S(1)}, bf16[320,512]{1,0:T(8,128)(2,1)S(1)}, u32[]{:S(2)}, u32[]{:S(2)}) collective-permute-start(bf16[320,512]{1,0:T(8,128)(2,1)S(1)} %get-tuple-element.35.refs_1_), channel_id=1, source_target_pairs={{0,2},{1,3},{2,0},{3,1},{4,6},{5,7},{6,4},{7,5},{8,10},{9,11},{10,... | collective-permute-start | bytes 983048 | tf_op jit(solution)/shard_map/ppermute | solution.py:346
  41.8 10.0 %collective-permute-start.3 = (bf16[320,512]{1,0:T(8,128)(2,1)S(1)}, bf16[320,512]{1,0:T(8,128)(2,1)S(1)}, u32[]{:S(2)}, u32[]{:S(2)}) collective-permute-start(bf16[320,512]{1,0:T(8,128)(2,1)S(1)} %collective-permute-done.2.refs_0_), channel_id=1, source_target_pairs={{0,1},{1,0},{2,3},{3,2},{4,5},{5,4},{6,7},{7,6},{8,9},{9,8},{10,11... | collective-permute-start | bytes 983048 | tf_op jit(solution)/shard_map/ppermute | solution.py:351
  45.3 15.9 %collective-permute-start.1 = (bf16[320,512]{1,0:T(8,128)(2,1)S(1)}, bf16[320,512]{1,0:T(8,128)(2,1)S(1)}, u32[]{:S(2)}, u32[]{:S(2)}) collective-permute-start(bf16[320,512]{1,0:T(8,128)(2,1)S(1)} %collective-permute-done.refs_0_), channel_id=1, source_target_pairs={{0,1},{1,0},{2,3},{3,2},{4,5},{5,4},{6,7},{7,6},{8,9},{9,8},{10,11... | collective-permute-start | bytes 983048 | tf_op jit(solution)/shard_map/ppermute | solution.py:351
  58.3 2.9 %copy-start = (bf16[1024,3584]{1,0:T(8,128)(2,1)}, bf16[1024,3584]{1,0:T(8,128)(2,1)S(1)}, u32[]{:S(2)}) copy-start(bf16[1024,3584]{1,0:T(8,128)(2,1)S(1)} %get-tuple-element.48.refs_2_) | copy-start | bytes 22020100
  61.2 3.1 %copy-start.1 = (bf16[1024,3584]{1,0:T(8,128)(2,1)S(1)}, bf16[1024,3584]{1,0:T(8,128)(2,1)}, u32[]{:S(2)}) copy-start(bf16[1024,3584]{1,0:T(8,128)(2,1)} %copy-done) | copy-start | bytes 22020100
  80.1 6.6 %collective-permute-start.10 = (bf16[320,512]{1,0:T(8,128)(2,1)S(1)}, bf16[320,512]{1,0:T(8,128)(2,1)S(1)}, u32[]{:S(2)}, u32[]{:S(2)}) collective-permute-start(bf16[320,512]{1,0:T(8,128)(2,1)S(1)} %get-tuple-element.67), channel_id=1, source_target_pairs={{0,1},{1,0},{2,3},{3,2},{4,5},{5,4},{6,7},{7,6},{8,9},{9,8},{10,11... | collective-permute-start | bytes 983048 | tf_op jit(solution)/shard_map/ppermute | solution.py:371
  80.7 7.8 %collective-permute-start.7 = (bf16[320,512]{1,0:T(8,128)(2,1)S(1)}, bf16[320,512]{1,0:T(8,128)(2,1)S(1)}, u32[]{:S(2)}, u32[]{:S(2)}) collective-permute-start(bf16[320,512]{1,0:T(8,128)(2,1)S(1)} %get-tuple-element.62), channel_id=1, source_target_pairs={{0,1},{1,0},{2,3},{3,2},{4,5},{5,4},{6,7},{7,6},{8,9},{9,8},{10,11... | collective-permute-start | bytes 983048 | tf_op jit(solution)/shard_map/ppermute | solution.py:371
  83.3 31.1 %copy-start.2 = (f32[2,64,8]{1,2,0:T(8,128)S(1)}, f32[2,64,8]{1,2,0:T(8,128)}, u32[]{:S(2)}) copy-start(f32[2,64,8]{1,2,0:T(8,128)} %param.8) | copy-start | bytes 12292
  83.3 31.1 %copy-start.3 = (s32[2,64,2]{1,2,0:T(2,128)S(1)}, s32[2,64,2]{1,2,0:T(2,128)}, u32[]{:S(2)}) copy-start(s32[2,64,2]{1,2,0:T(2,128)} %param.7) | copy-start | bytes 3076
  86.3 2.8 %collective-permute-start.9 = (bf16[320,512]{1,0:T(8,128)(2,1)S(1)}, bf16[320,512]{1,0:T(8,128)(2,1)S(1)}, u32[]{:S(2)}, u32[]{:S(2)}) collective-permute-start(bf16[320,512]{1,0:T(8,128)(2,1)S(1)} %get-tuple-element.65), channel_id=1, source_target_pairs={{0,1},{1,0},{2,3},{3,2},{4,5},{5,4},{6,7},{7,6},{8,9},{9,8},{10,11... | collective-permute-start | bytes 983048 | tf_op jit(solution)/shard_map/ppermute | solution.py:371
  86.8 10.6 %collective-permute-start.11 = (bf16[320,512]{1,0:T(8,128)(2,1)S(1)}, bf16[320,512]{1,0:T(8,128)(2,1)S(1)}, u32[]{:S(2)}, u32[]{:S(2)}) collective-permute-start(bf16[320,512]{1,0:T(8,128)(2,1)S(1)} %add_convert_fusion.1), channel_id=1, source_target_pairs={{0,2},{1,3},{2,0},{3,1},{4,6},{5,7},{6,4},{7,5},{8,10},{9,11},{10,... | collective-permute-start | bytes 983048 | tf_op jit(solution)/shard_map/ppermute | solution.py:377
  88.4 13.6 %collective-permute-start.6 = (bf16[320,512]{1,0:T(8,128)(2,1)S(1)}, bf16[320,512]{1,0:T(8,128)(2,1)S(1)}, u32[]{:S(2)}, u32[]{:S(2)}) collective-permute-start(bf16[320,512]{1,0:T(8,128)(2,1)S(1)} %get-tuple-element.60), channel_id=1, source_target_pairs={{0,1},{1,0},{2,3},{3,2},{4,5},{5,4},{6,7},{7,6},{8,9},{9,8},{10,11... | collective-permute-start | bytes 983048 | tf_op jit(solution)/shard_map/ppermute | solution.py:371
  88.5 15.1 %collective-permute-start.8 = (bf16[320,512]{1,0:T(8,128)(2,1)S(1)}, bf16[320,512]{1,0:T(8,128)(2,1)S(1)}, u32[]{:S(2)}, u32[]{:S(2)}) collective-permute-start(bf16[320,512]{1,0:T(8,128)(2,1)S(1)} %add_convert_fusion.3), channel_id=1, source_target_pairs={{0,2},{1,3},{2,0},{3,1},{4,6},{5,7},{6,4},{7,5},{8,10},{9,11},{10,... | collective-permute-start | bytes 983048 | tf_op jit(solution)/shard_map/ppermute | solution.py:377
  98.4 12.4 %all-to-all-start.2 = ((bf16[8,40,512]{2,1,0:T(8,128)(2,1)}), bf16[8,40,512]{2,1,0:T(8,128)(2,1)S(1)}, u32[]{:S(2)}, u32[]{:S(2)}) async-start(bf16[8,40,512]{2,1,0:T(8,128)(2,1)} %bitcast.5), calls=%async_computation.2 | async-start | bytes 655360 | tf_op jit(solution)/shard_map/all_to_all | solution.py:382
  110.8 12.7 %all-to-all-start.1 = ((bf16[8,40,512]{2,1,0:T(8,128)(2,1)}), bf16[8,40,512]{2,1,0:T(8,128)(2,1)S(1)}, u32[]{:S(2)}, u32[]{:S(2)}) async-start(bf16[8,40,512]{2,1,0:T(8,128)(2,1)} %bitcast.3), calls=%async_computation.1 | async-start | bytes 655360 | tf_op jit(solution)/shard_map/all_to_all | solution.py:382

commit v2 on v1

--- a/solution.py
+++ b/solution.py
@@ -13,19 +13,29 @@
 PAIR_KEY = 64
 IN_CHUNKS = 2
 OUT_CHUNKS = 2
-DOWN_PARTS = 7
+DOWN_PARTS = 1
 
 
 def tile_of(size, most):
-    return max(d for d in range(LANES, most + 1, LANES) if size % d == 0)
-
-
-def places(dims, routes_ref, m):
+    return max(d for d in range(LANES, max(most, LANES) + 1, LANES) if size % d == 0)
+
+
+def block_device(dims, rows, first):
+    dp, cap2, _ = dims
+    device = lax.broadcasted_iota(jnp.int32, (dp * cap2, rows), 0).astype(jnp.float32)
+    device = jnp.floor((device + 0.5) * (1.0 / cap2))
+    if first is None:
+        return device
+    device = device + first.astype(jnp.float32)
+    return device - jnp.floor((device + 0.5) * (1.0 / dp)) * dp
+
+
+def places(dims, device, routes_ref, m):
     dp, cap2, experts = dims
     rows = routes_ref.shape[2]
     at = lax.broadcasted_iota(jnp.int32, (dp * cap2, rows), 0).astype(jnp.float32)
-    device = jnp.floor((at + 0.5) * (1.0 / cap2))
-    keys = jnp.floor((device + 0.5) * (experts / dp)) * PAIR_KEY + (at - device * cap2)
+    at = at - jnp.floor((at + 0.5) * (1.0 / cap2)) * cap2
+    keys = jnp.floor((device + 0.5) * (experts / dp)) * PAIR_KEY + at
     earlier = lax.broadcasted_iota(jnp.int32, (rows, rows), 0) < lax.broadcasted_iota(
         jnp.int32, (rows, rows), 1
     )
@@ -42,14 +52,16 @@
     return hits, named, here
 
 
-def tables_kernel(dims, routes_ref, probs_ref, tokens_ref, sent_ref, aux_ref):
+def tables_kernel(dims, where_ref, routes_ref, probs_ref, tokens_ref, *refs):
     dp, cap2, experts = dims
+    sent, aux_ref = refs[:dp], refs[dp]
+    device = block_device(dims, routes_ref.shape[2], where_ref[0])
     micro = routes_ref.shape[0]
     blocks = tokens_ref.shape[2] // LANES
     aux_ref[...] = jnp.zeros_like(aux_ref)
     slots = jnp.zeros((dp * cap2, tokens_ref.shape[2]), jnp.float32)
     for m in range(micro):
-        _, named, here = places(dims, routes_ref, m)
+        _, named, here = places(dims, device, routes_ref, m)
         pick = (here[0] + here[1]).astype(jnp.bfloat16)
         slots = slots + jnp.dot(pick, tokens_ref[m], preferred_element_type=jnp.float32)
         sums = jnp.sum(probs_ref[m], axis=1, keepdims=True)
@@ -63,31 +75,46 @@
     aux = aux_ref[...].astype(jnp.bfloat16)
     for d in range(dp):
         for b in range(blocks):
-            sent_ref[d, b * cap2 : (b + 1) * cap2, :] = slots[
+            sent[d][b * cap2 : (b + 1) * cap2, :] = slots[
                 d * cap2 : (d + 1) * cap2, b * LANES : (b + 1) * LANES
             ]
-        sent_ref[d, blocks * cap2 :, :] = aux
-
-
-def weights_kernel(dims, routes_ref, probs_ref, combine_ref):
-    for m in range(routes_ref.shape[0]):
-        hits, _, here = places(dims, routes_ref, m)
-        picked = [jnp.sum(probs_ref[m] * hit, axis=0, keepdims=True) for hit in hits]
-        total = picked[0] + picked[1]
-        combine_ref[m] = here[0] * (picked[0] / total) + here[1] * (picked[1] / total)
-
-
-def repack_kernel(dims, arrived_ref, *refs):
-    dp, cap2, blocks, micro, experts, tokens_all = dims
-    xs, loss_ref = refs[:-1], refs[-1]
-    per = blocks // len(xs)
+        sent[d][blocks * cap2 :, :] = aux
+
+
+def weights_kernel(dims, where_ref, routes_ref, probs_ref, *orders):
+    dp, cap2, experts = dims
+    micro, _, rows = routes_ref.shape
+    for shifted, pieces_ref in enumerate(orders):
+        device = block_device(dims, rows, where_ref[0] if shifted else None)
+        for m in range(micro):
+            hits, _, here = places(dims, device, routes_ref, m)
+            picked = [jnp.sum(probs_ref[m] * hit, axis=0, keepdims=True) for hit in hits]
+            total = picked[0] + picked[1]
+            left = (here[0] * (picked[0] / total) + here[1] * (picked[1] / total)).T
+            for piece in range(3):
+                part = left.astype(jnp.bfloat16)
+                at = (piece * micro + m) * rows
+                pieces_ref[at : at + rows, :] = part
+                left = left - part.astype(jnp.float32)
+
+
+def repack_kernel(dims, where_ref, *refs):
+    dp, blocks, tokens_all, count = dims
+    arrived, refs = refs[:dp], refs[dp:]
+    xs, loss_ref, aux_ref = refs[:count], refs[count], refs[count + 1]
+    experts, micro = loss_ref.shape
+    cap2 = xs[0].shape[1]
+    per = blocks // count
+    for shift in range(dp):
+        group = lax.rem(where_ref[0] + (dp - shift), dp)
+        for b in range(blocks):
+            xs[b // per][group, :, b % per * LANES : (b % per + 1) * LANES] = arrived[shift][
+                b * cap2 : (b + 1) * cap2, :
+            ]
+        aux_ref[group] = arrived[shift][blocks * cap2 :, :].astype(jnp.float32)
     total = jnp.zeros((experts, LANES), jnp.float32)
-    for d in range(dp):
-        for b in range(blocks):
-            xs[b // per][
-                d * cap2 : (d + 1) * cap2, b % per * LANES : (b % per + 1) * LANES
-            ] = arrived_ref[d, b * cap2 : (b + 1) * cap2, :]
-        total = total + arrived_ref[d, blocks * cap2 :, :].astype(jnp.float32)
+    for group in range(dp):
+        total = total + aux_ref[group]
     count = total[:, 0:micro]
     prob = total[:, 3 * micro : 4 * micro] + total[:, 2 * micro : 3 * micro]
     prob = prob + total[:, micro : 2 * micro]
@@ -195,7 +222,7 @@
     width = w_gate.shape[2]
     return pl.pallas_call(
         functools.partial(first_kernel, pieces),
-        in_specs=[SMEM, HBM, HBM, HBM],
+        in_specs=[SMEM, pl.BlockSpec(memory_space=pl.ANY), HBM, HBM],
         out_specs=[VMEM] * 2,
         out_shape=[pltpu.VMEM((depth, width), jnp.bfloat16)] * 2,
         scratch_shapes=[pltpu.SemaphoreType.DMA((2, 2 * len(pieces)))],
@@ -216,7 +243,7 @@
         sources = [w_gate, w_up]
         out_shape = [pltpu.VMEM((rows, width), jnp.float32)] * 2
         out_shape += [pltpu.VMEM((depth, width), jnp.bfloat16)] * 2
-    plan = (len(xs), totals is None, following, tile_of(width, 512))
+    plan = (len(xs), totals is None, following, tile_of(width, (5 << 20) // (8 * rows)))
     totals = totals or []
     at = 1 + len(xs) + 2
     return pl.pallas_call(
@@ -244,15 +271,19 @@
         finish = run_copies(down_copies(0, (part,), here, w_down, (next_ref,), sems))
     quarter = columns * OUT_CHUNKS
     half = w_a.shape[0]
-    for p, out_ref in enumerate((keep_ref, send_ref)):
-        start = ((here & 1) ^ p) * quarter + c * columns
-        for j in range(columns // tile):
+
+    def step(j, carry):
+        for p, out_ref in enumerate((keep_ref, send_ref)):
+            start = ((here & 1) ^ p) * quarter + c * columns
             at = pl.ds(pl.multiple_of(start + j * tile, tile), tile)
             total = jnp.dot(h_ref[:, :half], w_a[:, at], preferred_element_type=jnp.float32)
             total = total + jnp.dot(
                 h_ref[:, half:], w_b[:, at], preferred_element_type=jnp.float32
             )
-            out_ref[:, j * tile : (j + 1) * tile] = total.astype(out_ref.dtype)
+            out_ref[:, pl.ds(pl.multiple_of(j * tile, tile), tile)] = total.astype(out_ref.dtype)
+        return carry
+
+    lax.fori_loop(0, columns // tile, step, 0)
     token_ref[...] = jnp.zeros_like(token_ref)
     if finish is not None:
         finish()
@@ -271,7 +302,7 @@
     if more:
         out_shape.append(pltpu.VMEM((half, both), jnp.bfloat16))
     return pl.pallas_call(
-        functools.partial(down_kernel, (c, part, tile_of(columns, 512), columns)),
+        functools.partial(down_kernel, (c, part, tile_of(columns, 256), columns)),
         in_specs=[SMEM, VMEM, VMEM, VMEM, HBM] + [HBM] * more,
         out_specs=[VMEM] * len(out_shape),
         out_shape=out_shape,
@@ -283,24 +314,30 @@
     )(where, h, *weights, after, *([w_down] * more))
 
 
-def combine_kernel(combine_ref, *refs):
-    parts, out_ref = refs[:-1], refs[-1]
-    micro, _, rows = combine_ref.shape
-    left = jnp.concatenate([combine_ref[m].T for m in range(micro)], axis=0)
-    pieces = []
-    for _ in range(3):
-        piece = left.astype(jnp.bfloat16)
-        pieces.append(piece)
-        left = left - piece.astype(jnp.float32)
-    pieces = jnp.concatenate(pieces, axis=0)
+def spread_kernel(dp, where_ref, keep_ref, got_ref, crossed_ref, *outs):
+    for shift in range(dp):
+        group = lax.rem(where_ref[0] + (dp - shift), dp)
+        total = keep_ref[group] + got_ref[group].astype(jnp.float32)
+        total = total + crossed_ref[group].astype(jnp.float32)
+        outs[shift][...] = total.astype(jnp.bfloat16)
+
+
+def combine_kernel(whole_ref, shifted_ref, first_ref, *refs):
+    blocks, out_ref, rows_ref = refs[:-2], refs[-2], refs[-1]
+    micro, rows, _ = out_ref.shape
     each = micro * rows
-    for at, part in enumerate(parts):
+    cap2 = blocks[0].shape[0]
+    for shift, block in enumerate(blocks):
+        rows_ref[shift * cap2 : (shift + 1) * cap2, :] = block[...]
+    at = 0
+    for pieces, part in ((whole_ref, first_ref), (shifted_ref, rows_ref)):
         width = part.shape[1]
-        total = jnp.dot(pieces, part[...], preferred_element_type=jnp.float32)
+        total = jnp.dot(pieces[...], part[...], preferred_element_type=jnp.float32)
         total = (total[2 * each :] + total[each : 2 * each]) + total[:each]
         total = total.astype(jnp.bfloat16)
         for m in range(micro):
-            out_ref[m, :, at * width : (at + 1) * width] = total[m * rows : (m + 1) * rows]
+            out_ref[m, :, at : at + width] = total[m * rows : (m + 1) * rows]
+        at += width
 
 
 def local(dp, tensor, tokens, routes, probs, w_gate, w_up, w_down):
@@ -319,37 +356,47 @@
     width = features // IN_CHUNKS
     dims = (dp, cap2, experts)
     routes, probs = routes.transpose(0, 2, 1), probs.transpose(0, 2, 1)
+    place = lax.axis_index("dp")[None]
+    inputs = (pltpu.with_memory_space_constraint(a, pltpu.HBM) for a in (routes, probs, tokens))
     sent = pl.pallas_call(
         functools.partial(tables_kernel, dims),
-        out_shape=pltpu.VMEM((dp, blocks * cap2 + experts, LANES), jnp.bfloat16),
+        in_specs=[SMEM] + [VMEM] * 3,
+        out_shape=[pltpu.VMEM((blocks * cap2 + experts, LANES), jnp.bfloat16)] * dp,
         scratch_shapes=[pltpu.VMEM((experts, LANES), jnp.float32)],
-        compiler_params=pltpu.CompilerParams(vmem_limit_bytes=24 << 20),
+        compiler_params=pltpu.CompilerParams(vmem_limit_bytes=48 << 20),
         name="tables",
-    )(*(pltpu.with_memory_space_constraint(a, pltpu.HBM) for a in (routes, probs, tokens)))
-    arrived = lax.all_to_all(sent, "dp", split_axis=0, concat_axis=0, tiled=True)
+    )(place, *inputs)
+    arrived = [sent[0]]
+    for shift in range(1, dp):
+        onward = [(i, (i + shift) % dp) for i in range(dp)]
+        arrived.append(lax.ppermute(sent[shift], "dp", onward))
     combine = pl.pallas_call(
         functools.partial(weights_kernel, dims),
-        out_shape=jax.ShapeDtypeStruct((micro, slots_all, rows), jnp.float32),
+        in_specs=[SMEM] + [VMEM] * 2,
+        out_shape=[jax.ShapeDtypeStruct((3 * micro * rows, slots_all), jnp.bfloat16)] * 2,
         compiler_params=pltpu.CompilerParams(vmem_limit_bytes=8 << 20),
         name="weights",
-    )(routes, probs)
+    )(place, routes, probs)
+    chunks = range(IN_CHUNKS)
+    stages = [[(q, c) for c in chunks] for q in range(2)] + [[(2, c), (3, c)] for c in chunks]
+    weights = first_weights(where, stages[0], sent[0], w_gate, w_up, features)
     *xs, loss = pl.pallas_call(
-        functools.partial(repack_kernel, (dp, cap2, blocks, micro, experts, rows * dp)),
-        out_shape=[pltpu.VMEM((slots_all, width), jnp.bfloat16)] * IN_CHUNKS
+        functools.partial(repack_kernel, (dp, blocks, rows * dp, IN_CHUNKS)),
+        in_specs=[SMEM] + [VMEM] * dp,
+        out_shape=[pltpu.VMEM((dp, cap2, width), jnp.bfloat16)] * IN_CHUNKS
         + [jax.ShapeDtypeStruct((experts, micro), jnp.float32)],
-        compiler_params=pltpu.CompilerParams(vmem_limit_bytes=4 << 20),
+        scratch_shapes=[pltpu.VMEM((dp, experts, LANES), jnp.float32)],
+        compiler_params=pltpu.CompilerParams(vmem_limit_bytes=12 << 20),
         name="repack",
-    )(pltpu.with_memory_space_constraint(arrived, pltpu.VMEM))
+    )(place, *arrived)
+    xs = [x.reshape(slots_all, width) for x in xs]
     paired, crossed = [], []
     for x in xs:
         paired.append(lax.ppermute(x, "tensor", core))
         crossed.append(lax.ppermute(x, "tensor", row))
-    chunks = range(IN_CHUNKS)
-    stages = [[(q, c) for c in chunks] for q in range(2)] + [[(2, c), (3, c)] for c in chunks]
     operands = [xs, paired]
     for c in chunks:
         operands.append([crossed[c], lax.ppermute(crossed[c], "tensor", core)])
-    weights = first_weights(where, stages[0], loss, w_gate, w_up, features)
     totals = None
     for at, pieces in enumerate(operands):
         following = stages[at + 1] if at + 1 < len(stages) else None
@@ -375,19 +422,31 @@
         keep, got = kept[1, c]
         total = (keep + got.astype(jnp.float32)).astype(jnp.bfloat16)
         crossed.append(lax.ppermute(total, "tensor", row))
-    for c in range(OUT_CHUNKS):
-        keep, got = kept[0, c]
-        total = keep + got.astype(jnp.float32) + crossed[c].astype(jnp.float32)
-        total = total.astype(jnp.bfloat16).reshape(dp, cap2, width)
-        back = lax.all_to_all(total, "dp", split_axis=0, concat_axis=0, tiled=True)
-        back = pltpu.with_memory_space_constraint(back.reshape(slots_all, width), pltpu.VMEM)
-        returned.append(back)
+    keep, got = kept[0, 0]
+    total = keep + got.astype(jnp.float32) + crossed[0].astype(jnp.float32)
+    total = total.astype(jnp.bfloat16).reshape(dp, cap2, width)
+    back = lax.all_to_all(total, "dp", split_axis=0, concat_axis=0, tiled=True)
+    returned.append(
+        pltpu.with_memory_space_constraint(back.reshape(slots_all, width), pltpu.VMEM)
+    )
+    blocks = pl.pallas_call(
+        functools.partial(spread_kernel, dp),
+        in_specs=[SMEM] + [VMEM] * 3,
+        out_shape=[jax.ShapeDtypeStruct((cap2, width), jnp.bfloat16)] * dp,
+        compiler_params=pltpu.CompilerParams(vmem_limit_bytes=12 << 20),
+        name="spread",
+    )(place, *(a.reshape(dp, cap2, width) for a in (*kept[0, 1], crossed[1])))
+    returned.append(blocks[0])
+    for shift in range(1, dp):
+        home = [(i, (i - shift) % dp) for i in range(dp)]
+        returned.append(lax.ppermute(blocks[shift], "dp", home))
     mixed = pl.pallas_call(
         combine_kernel,
         out_shape=jax.ShapeDtypeStruct((micro, rows, features), jnp.bfloat16),
+        scratch_shapes=[pltpu.VMEM((slots_all, width), jnp.bfloat16)],
         compiler_params=pltpu.CompilerParams(vmem_limit_bytes=16 << 20),
         name="combine",
-    )(combine, *returned)
+    )(*combine, *returned)
     return mixed, loss.T
 
 

time: 125 us -> 119 us (0.952)
  starting transfers between devices: 20.2 us -> 39.5 us
  waiting for transfers between devices: 45.5 us -> 26.5 us
  Pallas kernels: 49.8 us -> 44.6 us
    ppermute x0 -> x14, starting transfers between devices: none -> 24.7 us  [the longest x7 13.8 us: local(): arrived.append(lax.ppermute(sent[shift], 'dp', onward))]
    all_to_all x1 -> x0, waiting for transfers between devices: 17.6 us -> none  [local(): lax.all_to_all(sent, 'dp', split_axis=0, concat_axis=0, tiled=True)]
    all_to_all x2 -> x1, waiting for transfers between devices: 14.5 us -> 0.01 us  [local(): back = lax.all_to_all(total, 'dp', split_axis=0, concat_axis=0, tiled=True)]
    all_to_all x1 -> x0, starting transfers between devices: 7.28 us -> none  [local(): lax.all_to_all(sent, 'dp', split_axis=0, concat_axis=0, tiled=True)]
    ppermute x2, waiting for transfers between devices: 3.34 us -> 9.57 us  [local(): crossed.append(lax.ppermute(x, 'tensor', row))]
    ppermute x0 -> x14, waiting for transfers between devices: none -> 4.72 us  [the longest x7 4.71 us: local(): returned.append(lax.ppermute(blocks[shift], 'dp', home))]
    pallas_call x4, Pallas kernels: 14.9 us -> 12.3 us  [down(): pl.pallas_call(functools.partial(down_kernel, (c, part, tile_of(columns,...]
    ppermute x2, waiting for transfers between devices: 9.98 us -> 12.2 us  [local(): crossed.append(lax.ppermute(total, 'tensor', row))]
  transfers between devices with their start and end apart: 15 -> 27, of which waited for: 6 -> 7; matrix products, arithmetic and copies ran while one was open for 2% -> 1% of each run, Pallas kernels for 24% -> 27%
where the time goes in v2:
time: 119 us
  Pallas kernels  44.6 us (37%)
  starting transfers between devices  39.5 us (33%)
  waiting for transfers between devices  26.5 us (22%)
  local copies, waits for them, and re-layouts  6.62 us (6%)
    pallas_call x4, Pallas kernels, gate_up(): pl.pallas_call(functools.partial(gate_up_kernel, plan), in_specs=[SMEM] +...  23.3 us
    ppermute x7, starting transfers between devices, local(): arrived.append(lax.ppermute(sent[shift], 'dp', onward))  13.8 us
    pallas_call x4, Pallas kernels, down(): pl.pallas_call(functools.partial(down_kernel, (c, part, tile_of(columns,...  12.3 us
    ppermute x2, waiting for transfers between devices, local(): crossed.append(lax.ppermute(total, 'tensor', row))  12.2 us
    ppermute x7, starting transfers between devices, local(): returned.append(lax.ppermute(blocks[shift], 'dp', home))  10.9 us
    ppermute x2, waiting for transfers between devices, local(): crossed.append(lax.ppermute(x, 'tensor', row))  9.57 us
    all_to_all x1, starting transfers between devices, local(): back = lax.all_to_all(total, 'dp', split_axis=0, concat_axis=0, tiled=True)  8.15 us
    unnamed x9, local copies, waits for them, and re-layouts  6.62 us
  transfers between devices with their start and end apart: 27, of which 7 were waited for; matrix products, arithmetic and copies ran while one was open for 1% of the time, Pallas kernels for 27%

profile of v2, /device:TPU:0, one launch (start us, length us, event | category | flops | bytes accessed | tf_op | source)
XLA Modules:
  0.0 119.1 jit_solution(1821820989381166957)
XLA Ops:
  0.6 1.6 %tables.1 = (bf16[328,128]{1,0:T(8,128)(2,1)S(1)}, bf16[328,128]{1,0:T(8,128)(2,1)S(1)}, bf16[328,128]{1,0:T(8,128)(2,1)S(1)}, bf16[328,128]{1,0:T(8,128)(2,1)S(...) custom-call(s32[1]{0:T(128)} %bitcast.where_ref, ...), custom_call_target="tpu_custom_call" | custom-call | tf_op jit(solution)/shard_map/tables/pallas_call | solution.py:361
  2.2 3.0 %collective-permute-start = (bf16[328,128]{1,0:T(8,128)(2,1)S(1)}, bf16[328,128]{1,0:T(8,128)(2,1)S(1)}, u32[]{:S(2)}, u32[]{:S(2)}) collective-permute-start(bf16[328,128]{1,0:T(8,128)(2,1)S(1)} %get-tuple-element.56), channel_id=1, source_target_pairs={{0,4},{4,8},{8,12},{12,16},{16,20},{20,24},{24,28},{28,0},{1,5},{5... | collective-permute-start | bytes 251912 | tf_op jit(solution)/shard_map/ppermute | solution.py:372
  5.3 1.6 %collective-permute-start.1 = (bf16[328,128]{1,0:T(8,128)(2,1)S(1)}, bf16[328,128]{1,0:T(8,128)(2,1)S(1)}, u32[]{:S(2)}, u32[]{:S(2)}) collective-permute-start(bf16[328,128]{1,0:T(8,128)(2,1)S(1)} %get-tuple-element.57), channel_id=1, source_target_pairs={{0,8},{4,12},{8,16},{12,20},{16,24},{20,28},{24,0},{28,4},{1,9},{5... | collective-permute-start | bytes 251912 | tf_op jit(solution)/shard_map/ppermute | solution.py:372
  6.8 2.6 %collective-permute-start.2 = (bf16[328,128]{1,0:T(8,128)(2,1)S(1)}, bf16[328,128]{1,0:T(8,128)(2,1)S(1)}, u32[]{:S(2)}, u32[]{:S(2)}) collective-permute-start(bf16[328,128]{1,0:T(8,128)(2,1)S(1)} %get-tuple-element.58), channel_id=1, source_target_pairs={{0,12},{4,16},{8,20},{12,24},{16,28},{20,0},{24,4},{28,8},{1,13},{... | collective-permute-start | bytes 251912 | tf_op jit(solution)/shard_map/ppermute | solution.py:372
  9.4 1.2 %collective-permute-start.3 = (bf16[328,128]{1,0:T(8,128)(2,1)S(1)}, bf16[328,128]{1,0:T(8,128)(2,1)S(1)}, u32[]{:S(2)}, u32[]{:S(2)}) collective-permute-start(bf16[328,128]{1,0:T(8,128)(2,1)S(1)} %get-tuple-element.59), channel_id=1, source_target_pairs={{0,16},{4,20},{8,24},{12,28},{16,0},{20,4},{24,8},{28,12},{1,17},{... | collective-permute-start | bytes 251912 | tf_op jit(solution)/shard_map/ppermute | solution.py:372
  10.6 2.6 %collective-permute-start.4 = (bf16[328,128]{1,0:T(8,128)(2,1)S(1)}, bf16[328,128]{1,0:T(8,128)(2,1)S(1)}, u32[]{:S(2)}, u32[]{:S(2)}) collective-permute-start(bf16[328,128]{1,0:T(8,128)(2,1)S(1)} %get-tuple-element.60), channel_id=1, source_target_pairs={{0,20},{4,24},{8,28},{12,0},{16,4},{20,8},{24,12},{28,16},{1,21},{... | collective-permute-start | bytes 251912 | tf_op jit(solution)/shard_map/ppermute | solution.py:372
  13.2 1.4 %collective-permute-start.5 = (bf16[328,128]{1,0:T(8,128)(2,1)S(1)}, bf16[328,128]{1,0:T(8,128)(2,1)S(1)}, u32[]{:S(2)}, u32[]{:S(2)}) collective-permute-start(bf16[328,128]{1,0:T(8,128)(2,1)S(1)} %get-tuple-element.61), channel_id=1, source_target_pairs={{0,24},{4,28},{8,0},{12,4},{16,8},{20,12},{24,16},{28,20},{1,25},{... | collective-permute-start | bytes 251912 | tf_op jit(solution)/shard_map/ppermute | solution.py:372
  14.6 1.4 %collective-permute-start.6 = (bf16[328,128]{1,0:T(8,128)(2,1)S(1)}, bf16[328,128]{1,0:T(8,128)(2,1)S(1)}, u32[]{:S(2)}, u32[]{:S(2)}) collective-permute-start(bf16[328,128]{1,0:T(8,128)(2,1)S(1)} %get-tuple-element.62), channel_id=1, source_target_pairs={{0,28},{4,0},{8,4},{12,8},{16,12},{20,16},{24,20},{28,24},{1,29},{... | collective-permute-start | bytes 251912 | tf_op jit(solution)/shard_map/ppermute | solution.py:372
  16.0 5.3 %first.1 = (bf16[1024,3584]{1,0:T(8,128)(2,1)S(1)}, bf16[1024,3584]{1,0:T(8,128)(2,1)S(1)}) custom-call(s32[1]{0:T(128)} %bitcast.3.where_ref, bf16[328,128]{1,0:T(8,128)(2,1)S(1)} %get-tuple-element.55.refs_0_.after_ref, bf16[1,4096,3584]{2,1,0:T(8,128)(2,1)} %refs_6_.4, bf16[1,4096,3584]{2,1,0:T(8,128)(2,1)} %refs_7_.3), custom_call_target="tpu_custom_call" | custom-call | tf_op jit(solution)/shard_map/first/pallas_call | solution.py:223
  21.4 0.2 repack.1
  21.7 1.6 %collective-permute-start.9 = (bf16[320,512]{1,0:T(8,128)(2,1)S(1)}, bf16[320,512]{1,0:T(8,128)(2,1)S(1)}, u32[]{:S(2)}, u32[]{:S(2)}) collective-permute-start(bf16[320,512]{1,0:T(8,128)(2,1)S(1)} %bitcast.20), channel_id=1, source_target_pairs={{0,2},{1,3},{2,0},{3,1},{4,6},{5,7},{6,4},{7,5},{8,10},{9,11},{10,... | collective-permute-start | bytes 983048 | tf_op jit(solution)/shard_map/ppermute | solution.py:396
  23.3 0.2 collective-permute-start.12
  23.4 0.5 collective-permute-start.7
  23.9 5.3 %shard_map.77 = (f32[320,3584]{1,0:T(8,128)S(1)}, f32[320,3584]{1,0:T(8,128)S(1)}, bf16[1024,3584]{1,0:T(8,128)(2,1)S(1)}, bf16[1024,3584]{1,0:T(8,128)(2,1)S(1)}) custom-call(s32[1]{0:T(128)} %bitcast.3.where_ref, bf16[320,512]{1,0:T(8,128)(2,1)S(1)} %bitcast.21, bf16[320,512]{1,0:T(8,128)(2,1)S(1)} %bitcast.18, ...), custom_call_target="tpu_custom_call" | custom-call | flops 4697620480 | bytes 14680064 | tf_op jit(solution)/shard_map/pallas_call | solution.py:249
  29.2 3.1 %collective-permute-done.9.refs_0_ = bf16[320,512]{1,0:T(8,128)(2,1)S(1)} collective-permute-done((bf16[320,512]{1,0:T(8,128)(2,1)S(1)}, bf16[320,512]{1,0:T(8,128)(2,1)S(1)}, u32[]{:S(2)}, u32[]{:S(2)}) %collective-permute-start.9) | collective-permute-done | bytes 327712 | tf_op jit(solution)/shard_map/ppermute | solution.py:396
  32.3 6.5 %collective-permute-done.7.refs_0_ = bf16[320,512]{1,0:T(8,128)(2,1)S(1)} collective-permute-done((bf16[320,512]{1,0:T(8,128)(2,1)S(1)}, bf16[320,512]{1,0:T(8,128)(2,1)S(1)}, u32[]{:S(2)}, u32[]{:S(2)}) %collective-permute-start.7) | collective-permute-done | bytes 327712 | tf_op jit(solution)/shard_map/ppermute | solution.py:396
  38.8 5.8 %shard_map.78 = (f32[320,3584]{1,0:T(8,128)S(1)}, f32[320,3584]{1,0:T(8,128)S(1)}, bf16[1024,3584]{1,0:T(8,128)(2,1)S(1)}, bf16[1024,3584]{1,0:T(8,128)(2,1)S(1)}) custom-call(s32[1]{0:T(128)} %bitcast.3.where_ref, bf16[320,512]{1,0:T(8,128)(2,1)S(1)} %collective-permute-done.11.refs_0_, ...), custom_call_target="tpu_custom_call", output_to_operand_aliasing={{0}: (5, {}), {1}: (6, {})} | custom-call | flops 4697620480 | bytes 14680064 | tf_op jit(solution)/shard_map/pallas_call | solution.py:249
  44.6 5.8 %shard_map.79 = (f32[320,3584]{1,0:T(8,128)S(1)}, f32[320,3584]{1,0:T(8,128)S(1)}, bf16[1024,3584]{1,0:T(8,128)(2,1)S(1)}, bf16[1024,3584]{1,0:T(8,128)(2,1)S(1)}) custom-call(s32[1]{0:T(128)} %bitcast.3.where_ref, bf16[320,512]{1,0:T(8,128)(2,1)S(1)} %collective-permute-done.9.refs_0_, ...), custom_call_target="tpu_custom_call", output_to_operand_aliasing={{0}: (5, {}), {1}: (6, {})} | custom-call | flops 4697620480 | bytes 14680064 | tf_op jit(solution)/shard_map/pallas_call | solution.py:249
  50.5 2.9 %copy-done = bf16[1024,3584]{1,0:T(8,128)(2,1)} copy-done((bf16[1024,3584]{1,0:T(8,128)(2,1)}, bf16[1024,3584]{1,0:T(8,128)(2,1)S(1)}, u32[]{:S(2)}) %copy-start) | copy-done | bytes 7340056
  53.4 3.1 %copy-done.1 = bf16[1024,3584]{1,0:T(8,128)(2,1)S(1)} copy-done((bf16[1024,3584]{1,0:T(8,128)(2,1)S(1)}, bf16[1024,3584]{1,0:T(8,128)(2,1)}, u32[]{:S(2)}) %copy-start.1) | copy-done | bytes 7340056
  56.4 6.4 %shard_map.80 = (bf16[320,3584]{1,0:T(8,128)(2,1)S(1)}, bf16[1792,2048]{1,0:T(8,128)(2,1)S(1)}, bf16[1792,2048]{1,0:T(8,128)(2,1)S(1)}) custom-call(s32[1]{0:T(128)} %bitcast.3.where_ref, bf16[320,512]{1,0:T(8,128)(2,1)S(1)} %collective-permute-done.7.refs_0_, bf16[320,512]{1,0:T(8,128)(2,1)S(1)} %collective-permute-done.8.refs_1_, ...), custom_call_target="tpu_custom_call" | custom-call | flops 4697620480 | bytes 14680064 | tf_op jit(solution)/shard_map/pallas_call | solution.py:249
  62.9 3.1 %shard_map.81 = (f32[320,512]{1,0:T(8,128)S(1)}, bf16[320,512]{1,0:T(8,128)(2,1)S(1)}, f32[8,128]{1,0:T(8,128)S(1)}, bf16[1792,2048]{1,0:T(8,128)(2,1)S(1)}) custom-call(s32[1]{0:T(128)} %bitcast.3.where_ref, bf16[320,3584]{1,0:T(8,128)(2,1)S(1)} %get-tuple-element.79.h_ref, bf16[1792,2048]{1,0:T(8,128)(2,1)S(1)} %get-tuple-element.80.w_a, ...), custom_call_target="tpu_custom_call" | custom-call | flops 2348810240 | bytes 7340032 | tf_op jit(solution)/shard_map/pallas_call | solution.py:304
  66.0 0.6 collective-permute-start.14
  66.6 3.1 %shard_map.82 = (f32[320,512]{1,0:T(8,128)S(1)}, bf16[320,512]{1,0:T(8,128)(2,1)S(1)}, f32[8,128]{1,0:T(8,128)S(1)}, bf16[1792,2048]{1,0:T(8,128)(2,1)S(1)}) custom-call(s32[1]{0:T(128)} %bitcast.3.where_ref, bf16[320,3584]{1,0:T(8,128)(2,1)S(1)} %get-tuple-element.79.h_ref, bf16[1792,2048]{1,0:T(8,128)(2,1)S(1)} %get-tuple-element.80.w_a, ...), custom_call_target="tpu_custom_call" | custom-call | flops 2348810240 | bytes 7340032 | tf_op jit(solution)/shard_map/pallas_call | solution.py:304
  69.7 2.8 %shard_map.83 = (f32[320,512]{1,0:T(8,128)S(1)}, bf16[320,512]{1,0:T(8,128)(2,1)S(1)}, f32[8,128]{1,0:T(8,128)S(1)}) custom-call(s32[1]{0:T(128)} %bitcast.3.where_ref, bf16[320,3584]{1,0:T(8,128)(2,1)S(1)} %get-tuple-element.79.h_ref, bf16[1792,2048]{1,0:T(8,128)(2,1)S(1)} %get-tuple-element.83.w_a, bf16[1792,2048]{1,0:T(8,128)(2,1)S(1)} %get-tuple-element.85.w_b, ...), custom_call_target="tpu_custom_call" | custom-call | flops 2348810240 | bytes 7340032 | tf_op jit(solution)/shard_map/pallas_call | solution.py:304
  72.5 0.1 add_convert_fusion.2
  72.6 1.6 %collective-permute-start.15 = (bf16[320,512]{1,0:T(8,128)(2,1)S(1)}, bf16[320,512]{1,0:T(8,128)(2,1)S(1)}, u32[]{:S(2)}, u32[]{:S(2)}) collective-permute-start(bf16[320,512]{1,0:T(8,128)(2,1)S(1)} %add_convert_fusion.2), channel_id=1, source_target_pairs={{0,2},{1,3},{2,0},{3,1},{4,6},{5,7},{6,4},{7,5},{8,10},{9,11},{10,... | collective-permute-start | bytes 983048 | tf_op jit(solution)/shard_map/ppermute | solution.py:424
  74.2 0.2 collective-permute-start.17
  74.4 3.3 %shard_map.84 = (f32[320,512]{1,0:T(8,128)S(1)}, bf16[320,512]{1,0:T(8,128)(2,1)S(1)}, f32[8,128]{1,0:T(8,128)}) custom-call(s32[1]{0:T(128)} %bitcast.3.where_ref, bf16[320,3584]{1,0:T(8,128)(2,1)S(1)} %get-tuple-element.79.h_ref, bf16[1792,2048]{1,0:T(8,128)(2,1)S(1)} %get-tuple-element.83.w_a, bf16[1792,2048]{1,0:T(8,128)(2,1)S(1)} %get-tuple-element.85.w_b, ...), custom_call_target="tpu_custom_call" | custom-call | flops 2348810240 | bytes 7340032 | tf_op jit(solution)/shard_map/pallas_call | solution.py:304
  77.8 0.3 collective-permute-start.16
  78.1 4.7 %collective-permute-done.15 = bf16[320,512]{1,0:T(8,128)(2,1)S(1)} collective-permute-done((bf16[320,512]{1,0:T(8,128)(2,1)S(1)}, bf16[320,512]{1,0:T(8,128)(2,1)S(1)}, u32[]{:S(2)}, u32[]{:S(2)}) %collective-permute-start.15) | collective-permute-done | bytes 327712 | tf_op jit(solution)/shard_map/ppermute | solution.py:424
  82.8 0.9 add_convert_fusion.1
  83.7 8.1 %all-to-all-start = ((bf16[8,40,512]{2,1,0:T(8,128)(2,1)}), bf16[8,40,512]{2,1,0:T(8,128)(2,1)S(1)}, u32[]{:S(2)}, u32[]{:S(2)}) async-start(bf16[8,40,512]{2,1,0:T(8,128)(2,1)} %bitcast.6), calls=%async_computation | async-start | bytes 655360 | tf_op jit(solution)/shard_map/all_to_all | solution.py:428
  91.8 0.1 add_convert_fusion
  91.9 1.6 %collective-permute-start.18 = (bf16[320,512]{1,0:T(8,128)(2,1)S(1)}, bf16[320,512]{1,0:T(8,128)(2,1)S(1)}, u32[]{:S(2)}, u32[]{:S(2)}) collective-permute-start(bf16[320,512]{1,0:T(8,128)(2,1)S(1)} %add_convert_fusion), channel_id=1, source_target_pairs={{0,2},{1,3},{2,0},{3,1},{4,6},{5,7},{6,4},{7,5},{8,10},{9,11},{10,... | collective-permute-start | bytes 983048 | tf_op jit(solution)/shard_map/ppermute | solution.py:424
  93.5 7.4 %collective-permute-done.18 = bf16[320,512]{1,0:T(8,128)(2,1)S(1)} collective-permute-done((bf16[320,512]{1,0:T(8,128)(2,1)S(1)}, bf16[320,512]{1,0:T(8,128)(2,1)S(1)}, u32[]{:S(2)}, u32[]{:S(2)}) %collective-permute-start.18) | collective-permute-done | bytes 327712 | tf_op jit(solution)/shard_map/ppermute | solution.py:424
  101.0 0.1 spread.1
  101.1 4.5 %collective-permute-start.19 = (bf16[40,512]{1,0:T(8,128)(2,1)S(1)}, bf16[40,512]{1,0:T(8,128)(2,1)S(1)}, u32[]{:S(2)}, u32[]{:S(2)}) collective-permute-start(bf16[40,512]{1,0:T(8,128)(2,1)S(1)} %get-tuple-element.97), channel_id=1, source_target_pairs={{0,28},{4,0},{8,4},{12,8},{16,12},{20,16},{24,20},{28,24},{1,29},{... | collective-permute-start | bytes 122888 | tf_op jit(solution)/shard_map/ppermute | solution.py:442
  105.6 0.6 collective-permute-start.20
  106.1 2.9 %collective-permute-start.22 = (bf16[40,512]{1,0:T(8,128)(2,1)S(1)}, bf16[40,512]{1,0:T(8,128)(2,1)S(1)}, u32[]{:S(2)}, u32[]{:S(2)}) collective-permute-start(bf16[40,512]{1,0:T(8,128)(2,1)S(1)} %get-tuple-element.100), channel_id=1, source_target_pairs={{0,16},{4,20},{8,24},{12,28},{16,0},{20,4},{24,8},{28,12},{1,17},{... | collective-permute-start | bytes 122888 | tf_op jit(solution)/shard_map/ppermute | solution.py:442
  109.1 2.0 %collective-permute-start.24 = (bf16[40,512]{1,0:T(8,128)(2,1)S(1)}, bf16[40,512]{1,0:T(8,128)(2,1)S(1)}, u32[]{:S(2)}, u32[]{:S(2)}) collective-permute-start(bf16[40,512]{1,0:T(8,128)(2,1)S(1)} %get-tuple-element.102), channel_id=1, source_target_pairs={{0,8},{4,12},{8,16},{12,20},{16,24},{20,28},{24,0},{28,4},{1,9},{5... | collective-permute-start | bytes 122888 | tf_op jit(solution)/shard_map/ppermute | solution.py:442
  111.1 0.9 collective-permute-start.25
  112.0 0.4 weights.1
  112.4 0.6 copy.12
  113.1 1.8 %collective-permute-done.23.refs_5_ = bf16[40,512]{1,0:T(8,128)(2,1)S(1)} collective-permute-done((bf16[40,512]{1,0:T(8,128)(2,1)S(1)}, bf16[40,512]{1,0:T(8,128)(2,1)S(1)}, u32[]{:S(2)}, u32[]{:S(2)}) %collective-permute-start.23) | collective-permute-done | bytes 40992 | tf_op jit(solution)/shard_map/ppermute | solution.py:442
  114.9 1.3 %collective-permute-done.24.refs_6_ = bf16[40,512]{1,0:T(8,128)(2,1)S(1)} collective-permute-done((bf16[40,512]{1,0:T(8,128)(2,1)S(1)}, bf16[40,512]{1,0:T(8,128)(2,1)S(1)}, u32[]{:S(2)}, u32[]{:S(2)}) %collective-permute-start.24) | collective-permute-done | bytes 40992 | tf_op jit(solution)/shard_map/ppermute | solution.py:442
  116.2 1.6 %collective-permute-done.25.refs_7_ = bf16[40,512]{1,0:T(8,128)(2,1)S(1)} collective-permute-done((bf16[40,512]{1,0:T(8,128)(2,1)S(1)}, bf16[40,512]{1,0:T(8,128)(2,1)S(1)}, u32[]{:S(2)}, u32[]{:S(2)}) %collective-permute-start.25) | collective-permute-done | bytes 40992 | tf_op jit(solution)/shard_map/ppermute | solution.py:442
  117.8 1.3 %combine.1 = bf16[2,64,1024]{2,1,0:T(8,128)(2,1)} custom-call(bf16[384,320]{1,0:T(8,128)(2,1)S(1)} %get-tuple-element.53.whole_ref, bf16[384,320]{1,0:T(8,128)(2,1)S(1)} %get-tuple-element.54.shifted_ref, bf16[320,512]{1,0:T(8,128)(2,1)S(1)} %bitcast.12, bf16[40,512]{1,0:T(8,128)(2,1)S(1)} %get-tuple-element.96.refs_0_, ...), custom_call_target="tpu_custom_call" | custom-call | tf_op jit(solution)/shard_map/combine/pallas_call | solution.py:443
  (32 shorter events, 0.2 us)
Async XLA Ops:
  2.2 11.0 %collective-permute-start = (bf16[328,128]{1,0:T(8,128)(2,1)S(1)}, bf16[328,128]{1,0:T(8,128)(2,1)S(1)}, u32[]{:S(2)}, u32[]{:S(2)}) collective-permute-start(bf16[328,128]{1,0:T(8,128)(2,1)S(1)} %get-tuple-element.56), channel_id=1, source_target_pairs={{0,4},{4,8},{8,12},{12,16},{16,20},{20,24},{24,28},{28,0},{1,5},{5... | collective-permute-start | bytes 251912 | tf_op jit(solution)/shard_map/ppermute | solution.py:372
  5.3 9.3 %collective-permute-start.1 = (bf16[328,128]{1,0:T(8,128)(2,1)S(1)}, bf16[328,128]{1,0:T(8,128)(2,1)S(1)}, u32[]{:S(2)}, u32[]{:S(2)}) collective-permute-start(bf16[328,128]{1,0:T(8,128)(2,1)S(1)} %get-tuple-element.57), channel_id=1, source_target_pairs={{0,8},{4,12},{8,16},{12,20},{16,24},{20,28},{24,0},{28,4},{1,9},{5... | collective-permute-start | bytes 251912 | tf_op jit(solution)/shard_map/ppermute | solution.py:372
  6.8 14.5 %collective-permute-start.2 = (bf16[328,128]{1,0:T(8,128)(2,1)S(1)}, bf16[328,128]{1,0:T(8,128)(2,1)S(1)}, u32[]{:S(2)}, u32[]{:S(2)}) collective-permute-start(bf16[328,128]{1,0:T(8,128)(2,1)S(1)} %get-tuple-element.58), channel_id=1, source_target_pairs={{0,12},{4,16},{8,20},{12,24},{16,28},{20,0},{24,4},{28,8},{1,13},{... | collective-permute-start | bytes 251912 | tf_op jit(solution)/shard_map/ppermute | solution.py:372
  9.4 12.0 %collective-permute-start.3 = (bf16[328,128]{1,0:T(8,128)(2,1)S(1)}, bf16[328,128]{1,0:T(8,128)(2,1)S(1)}, u32[]{:S(2)}, u32[]{:S(2)}) collective-permute-start(bf16[328,128]{1,0:T(8,128)(2,1)S(1)} %get-tuple-element.59), channel_id=1, source_target_pairs={{0,16},{4,20},{8,24},{12,28},{16,0},{20,4},{24,8},{28,12},{1,17},{... | collective-permute-start | bytes 251912 | tf_op jit(solution)/shard_map/ppermute | solution.py:372
  10.6 10.7 %collective-permute-start.4 = (bf16[328,128]{1,0:T(8,128)(2,1)S(1)}, bf16[328,128]{1,0:T(8,128)(2,1)S(1)}, u32[]{:S(2)}, u32[]{:S(2)}) collective-permute-start(bf16[328,128]{1,0:T(8,128)(2,1)S(1)} %get-tuple-element.60), channel_id=1, source_target_pairs={{0,20},{4,24},{8,28},{12,0},{16,4},{20,8},{24,12},{28,16},{1,21},{... | collective-permute-start | bytes 251912 | tf_op jit(solution)/shard_map/ppermute | solution.py:372
  13.2 8.1 %collective-permute-start.5 = (bf16[328,128]{1,0:T(8,128)(2,1)S(1)}, bf16[328,128]{1,0:T(8,128)(2,1)S(1)}, u32[]{:S(2)}, u32[]{:S(2)}) collective-permute-start(bf16[328,128]{1,0:T(8,128)(2,1)S(1)} %get-tuple-element.61), channel_id=1, source_target_pairs={{0,24},{4,28},{8,0},{12,4},{16,8},{20,12},{24,16},{28,20},{1,25},{... | collective-permute-start | bytes 251912 | tf_op jit(solution)/shard_map/ppermute | solution.py:372
  14.6 6.8 %collective-permute-start.6 = (bf16[328,128]{1,0:T(8,128)(2,1)S(1)}, bf16[328,128]{1,0:T(8,128)(2,1)S(1)}, u32[]{:S(2)}, u32[]{:S(2)}) collective-permute-start(bf16[328,128]{1,0:T(8,128)(2,1)S(1)} %get-tuple-element.62), channel_id=1, source_target_pairs={{0,28},{4,0},{8,4},{12,8},{16,12},{20,16},{24,20},{28,24},{1,29},{... | collective-permute-start | bytes 251912 | tf_op jit(solution)/shard_map/ppermute | solution.py:372
  21.6 17.2 %collective-permute-start.11 = (bf16[320,512]{1,0:T(8,128)(2,1)S(1)}, bf16[320,512]{1,0:T(8,128)(2,1)S(1)}, u32[]{:S(2)}, u32[]{:S(2)}) collective-permute-start(bf16[320,512]{1,0:T(8,128)(2,1)S(1)} %bitcast.19), channel_id=1, source_target_pairs={{0,1},{1,0},{2,3},{3,2},{4,5},{5,4},{6,7},{7,6},{8,9},{9,8},{10,11... | collective-permute-start | bytes 983048 | tf_op jit(solution)/shard_map/ppermute | solution.py:395
  21.7 10.7 %collective-permute-start.9 = (bf16[320,512]{1,0:T(8,128)(2,1)S(1)}, bf16[320,512]{1,0:T(8,128)(2,1)S(1)}, u32[]{:S(2)}, u32[]{:S(2)}) collective-permute-start(bf16[320,512]{1,0:T(8,128)(2,1)S(1)} %bitcast.20), channel_id=1, source_target_pairs={{0,2},{1,3},{2,0},{3,1},{4,6},{5,7},{6,4},{7,5},{8,10},{9,11},{10,... | collective-permute-start | bytes 983048 | tf_op jit(solution)/shard_map/ppermute | solution.py:396
  23.3 15.6 %collective-permute-start.12 = (bf16[320,512]{1,0:T(8,128)(2,1)S(1)}, bf16[320,512]{1,0:T(8,128)(2,1)S(1)}, u32[]{:S(2)}, u32[]{:S(2)}) collective-permute-start(bf16[320,512]{1,0:T(8,128)(2,1)S(1)} %bitcast.16), channel_id=1, source_target_pairs={{0,1},{1,0},{2,3},{3,2},{4,5},{5,4},{6,7},{7,6},{8,9},{9,8},{10,11... | collective-permute-start | bytes 983048 | tf_op jit(solution)/shard_map/ppermute | solution.py:395
  23.4 15.4 %collective-permute-start.7 = (bf16[320,512]{1,0:T(8,128)(2,1)S(1)}, bf16[320,512]{1,0:T(8,128)(2,1)S(1)}, u32[]{:S(2)}, u32[]{:S(2)}) collective-permute-start(bf16[320,512]{1,0:T(8,128)(2,1)S(1)} %bitcast.17), channel_id=1, source_target_pairs={{0,2},{1,3},{2,0},{3,1},{4,6},{5,7},{6,4},{7,5},{8,10},{9,11},{10,... | collective-permute-start | bytes 983048 | tf_op jit(solution)/shard_map/ppermute | solution.py:396
  32.3 12.3 %collective-permute-start.10 = (bf16[320,512]{1,0:T(8,128)(2,1)S(1)}, bf16[320,512]{1,0:T(8,128)(2,1)S(1)}, u32[]{:S(2)}, u32[]{:S(2)}) collective-permute-start(bf16[320,512]{1,0:T(8,128)(2,1)S(1)} %collective-permute-done.9.refs_0_), channel_id=1, source_target_pairs={{0,1},{1,0},{2,3},{3,2},{4,5},{5,4},{6,7},{7,6},{8,9},{9,8},{10,11... | collective-permute-start | bytes 983048 | tf_op jit(solution)/shard_map/ppermute | solution.py:399
  38.8 14.5 %collective-permute-start.8 = (bf16[320,512]{1,0:T(8,128)(2,1)S(1)}, bf16[320,512]{1,0:T(8,128)(2,1)S(1)}, u32[]{:S(2)}, u32[]{:S(2)}) collective-permute-start(bf16[320,512]{1,0:T(8,128)(2,1)S(1)} %collective-permute-done.7.refs_0_), channel_id=1, source_target_pairs={{0,1},{1,0},{2,3},{3,2},{4,5},{5,4},{6,7},{7,6},{8,9},{9,8},{10,11... | collective-permute-start | bytes 983048 | tf_op jit(solution)/shard_map/ppermute | solution.py:399
  50.5 2.9 %copy-start = (bf16[1024,3584]{1,0:T(8,128)(2,1)}, bf16[1024,3584]{1,0:T(8,128)(2,1)S(1)}, u32[]{:S(2)}) copy-start(bf16[1024,3584]{1,0:T(8,128)(2,1)S(1)} %get-tuple-element.75.refs_2_) | copy-start | bytes 22020100
  53.4 3.1 %copy-start.1 = (bf16[1024,3584]{1,0:T(8,128)(2,1)S(1)}, bf16[1024,3584]{1,0:T(8,128)(2,1)}, u32[]{:S(2)}) copy-start(bf16[1024,3584]{1,0:T(8,128)(2,1)} %copy-done) | copy-start | bytes 22020100
  66.0 6.5 %collective-permute-start.14 = (bf16[320,512]{1,0:T(8,128)(2,1)S(1)}, bf16[320,512]{1,0:T(8,128)(2,1)S(1)}, u32[]{:S(2)}, u32[]{:S(2)}) collective-permute-start(bf16[320,512]{1,0:T(8,128)(2,1)S(1)} %get-tuple-element.90), channel_id=1, source_target_pairs={{0,1},{1,0},{2,3},{3,2},{4,5},{5,4},{6,7},{7,6},{8,9},{9,8},{10,11... | collective-permute-start | bytes 983048 | tf_op jit(solution)/shard_map/ppermute | solution.py:418
  72.4 5.6 %collective-permute-start.13 = (bf16[320,512]{1,0:T(8,128)(2,1)S(1)}, bf16[320,512]{1,0:T(8,128)(2,1)S(1)}, u32[]{:S(2)}, u32[]{:S(2)}) collective-permute-start(bf16[320,512]{1,0:T(8,128)(2,1)S(1)} %get-tuple-element.88), channel_id=1, source_target_pairs={{0,1},{1,0},{2,3},{3,2},{4,5},{5,4},{6,7},{7,6},{8,9},{9,8},{10,11... | collective-permute-start | bytes 983048 | tf_op jit(solution)/shard_map/ppermute | solution.py:418
  72.6 10.2 %collective-permute-start.15 = (bf16[320,512]{1,0:T(8,128)(2,1)S(1)}, bf16[320,512]{1,0:T(8,128)(2,1)S(1)}, u32[]{:S(2)}, u32[]{:S(2)}) collective-permute-start(bf16[320,512]{1,0:T(8,128)(2,1)S(1)} %add_convert_fusion.2), channel_id=1, source_target_pairs={{0,2},{1,3},{2,0},{3,1},{4,6},{5,7},{6,4},{7,5},{8,10},{9,11},{10,... | collective-permute-start | bytes 983048 | tf_op jit(solution)/shard_map/ppermute | solution.py:424
  74.2 17.6 %collective-permute-start.17 = (bf16[320,512]{1,0:T(8,128)(2,1)S(1)}, bf16[320,512]{1,0:T(8,128)(2,1)S(1)}, u32[]{:S(2)}, u32[]{:S(2)}) collective-permute-start(bf16[320,512]{1,0:T(8,128)(2,1)S(1)} %get-tuple-element.95), channel_id=1, source_target_pairs={{0,1},{1,0},{2,3},{3,2},{4,5},{5,4},{6,7},{7,6},{8,9},{9,8},{10,11... | collective-permute-start | bytes 983048 | tf_op jit(solution)/shard_map/ppermute | solution.py:418
  74.4 37.6 %copy-start.2 = (f32[2,64,8]{1,2,0:T(8,128)S(1)}, f32[2,64,8]{1,2,0:T(8,128)}, u32[]{:S(2)}) copy-start(f32[2,64,8]{1,2,0:T(8,128)} %param.8) | copy-start | bytes 12292
  74.4 37.6 %copy-start.3 = (s32[2,64,2]{1,2,0:T(2,128)S(1)}, s32[2,64,2]{1,2,0:T(2,128)}, u32[]{:S(2)}) copy-start(s32[2,64,2]{1,2,0:T(2,128)} %param.7) | copy-start | bytes 3076
  77.8 15.7 %collective-permute-start.16 = (bf16[320,512]{1,0:T(8,128)(2,1)S(1)}, bf16[320,512]{1,0:T(8,128)(2,1)S(1)}, u32[]{:S(2)}, u32[]{:S(2)}) collective-permute-start(bf16[320,512]{1,0:T(8,128)(2,1)S(1)} %get-tuple-element.93), channel_id=1, source_target_pairs={{0,1},{1,0},{2,3},{3,2},{4,5},{5,4},{6,7},{7,6},{8,9},{9,8},{10,11... | collective-permute-start | bytes 983048 | tf_op jit(solution)/shard_map/ppermute | solution.py:418
  83.7 34.1 %all-to-all-start = ((bf16[8,40,512]{2,1,0:T(8,128)(2,1)}), bf16[8,40,512]{2,1,0:T(8,128)(2,1)S(1)}, u32[]{:S(2)}, u32[]{:S(2)}) async-start(bf16[8,40,512]{2,1,0:T(8,128)(2,1)} %bitcast.6), calls=%async_computation | async-start | bytes 655360 | tf_op jit(solution)/shard_map/all_to_all | solution.py:428
  91.9 9.0 %collective-permute-start.18 = (bf16[320,512]{1,0:T(8,128)(2,1)S(1)}, bf16[320,512]{1,0:T(8,128)(2,1)S(1)}, u32[]{:S(2)}, u32[]{:S(2)}) collective-permute-start(bf16[320,512]{1,0:T(8,128)(2,1)S(1)} %add_convert_fusion), channel_id=1, source_target_pairs={{0,2},{1,3},{2,0},{3,1},{4,6},{5,7},{6,4},{7,5},{8,10},{9,11},{10,... | collective-permute-start | bytes 983048 | tf_op jit(solution)/shard_map/ppermute | solution.py:424
  101.1 8.0 %collective-permute-start.19 = (bf16[40,512]{1,0:T(8,128)(2,1)S(1)}, bf16[40,512]{1,0:T(8,128)(2,1)S(1)}, u32[]{:S(2)}, u32[]{:S(2)}) collective-permute-start(bf16[40,512]{1,0:T(8,128)(2,1)S(1)} %get-tuple-element.97), channel_id=1, source_target_pairs={{0,28},{4,0},{8,4},{12,8},{16,12},{20,16},{24,20},{28,24},{1,29},{... | collective-permute-start | bytes 122888 | tf_op jit(solution)/shard_map/ppermute | solution.py:442
  105.6 5.5 %collective-permute-start.20 = (bf16[40,512]{1,0:T(8,128)(2,1)S(1)}, bf16[40,512]{1,0:T(8,128)(2,1)S(1)}, u32[]{:S(2)}, u32[]{:S(2)}) collective-permute-start(bf16[40,512]{1,0:T(8,128)(2,1)S(1)} %get-tuple-element.98), channel_id=1, source_target_pairs={{0,24},{4,28},{8,0},{12,4},{16,8},{20,12},{24,16},{28,20},{1,25},{... | collective-permute-start | bytes 122888 | tf_op jit(solution)/shard_map/ppermute | solution.py:442
  106.1 7.0 %collective-permute-start.21 = (bf16[40,512]{1,0:T(8,128)(2,1)S(1)}, bf16[40,512]{1,0:T(8,128)(2,1)S(1)}, u32[]{:S(2)}, u32[]{:S(2)}) collective-permute-start(bf16[40,512]{1,0:T(8,128)(2,1)S(1)} %get-tuple-element.99), channel_id=1, source_target_pairs={{0,20},{4,24},{8,28},{12,0},{16,4},{20,8},{24,12},{28,16},{1,21},{... | collective-permute-start | bytes 122888 | tf_op jit(solution)/shard_map/ppermute | solution.py:442
  106.1 7.0 %collective-permute-start.22 = (bf16[40,512]{1,0:T(8,128)(2,1)S(1)}, bf16[40,512]{1,0:T(8,128)(2,1)S(1)}, u32[]{:S(2)}, u32[]{:S(2)}) collective-permute-start(bf16[40,512]{1,0:T(8,128)(2,1)S(1)} %get-tuple-element.100), channel_id=1, source_target_pairs={{0,16},{4,20},{8,24},{12,28},{16,0},{20,4},{24,8},{28,12},{1,17},{... | collective-permute-start | bytes 122888 | tf_op jit(solution)/shard_map/ppermute | solution.py:442
  109.0 5.8 %collective-permute-start.23 = (bf16[40,512]{1,0:T(8,128)(2,1)S(1)}, bf16[40,512]{1,0:T(8,128)(2,1)S(1)}, u32[]{:S(2)}, u32[]{:S(2)}) collective-permute-start(bf16[40,512]{1,0:T(8,128)(2,1)S(1)} %get-tuple-element.101), channel_id=1, source_target_pairs={{0,12},{4,16},{8,20},{12,24},{16,28},{20,0},{24,4},{28,8},{1,13},{... | collective-permute-start | bytes 122888 | tf_op jit(solution)/shard_map/ppermute | solution.py:442
  109.1 7.1 %collective-permute-start.24 = (bf16[40,512]{1,0:T(8,128)(2,1)S(1)}, bf16[40,512]{1,0:T(8,128)(2,1)S(1)}, u32[]{:S(2)}, u32[]{:S(2)}) collective-permute-start(bf16[40,512]{1,0:T(8,128)(2,1)S(1)} %get-tuple-element.102), channel_id=1, source_target_pairs={{0,8},{4,12},{8,16},{12,20},{16,24},{20,28},{24,0},{28,4},{1,9},{5... | collective-permute-start | bytes 122888 | tf_op jit(solution)/shard_map/ppermute | solution.py:442
  111.1 6.7 %collective-permute-start.25 = (bf16[40,512]{1,0:T(8,128)(2,1)S(1)}, bf16[40,512]{1,0:T(8,128)(2,1)S(1)}, u32[]{:S(2)}, u32[]{:S(2)}) collective-permute-start(bf16[40,512]{1,0:T(8,128)(2,1)S(1)} %get-tuple-element.103), channel_id=1, source_target_pairs={{0,4},{4,8},{8,12},{12,16},{16,20},{20,24},{24,28},{28,0},{1,5},{5... | collective-permute-start | bytes 122888 | tf_op jit(solution)/shard_map/ppermute | solution.py:442

commit v3 on v2

--- a/solution.py
+++ b/solution.py
@@ -26,8 +26,7 @@
     device = jnp.floor((device + 0.5) * (1.0 / cap2))
     if first is None:
         return device
-    device = device + first.astype(jnp.float32)
-    return device - jnp.floor((device + 0.5) * (1.0 / dp)) * dp
+    return (device.astype(jnp.int32) ^ first).astype(jnp.float32)
 
 
 def places(dims, device, routes_ref, m):
@@ -81,7 +80,7 @@
         sent[d][blocks * cap2 :, :] = aux
 
 
-def weights_kernel(dims, where_ref, routes_ref, probs_ref, *orders):
+def weights_kernel(dims, where_ref, routes_ref, probs_ref, after_ref, *orders):
     dp, cap2, experts = dims
     micro, _, rows = routes_ref.shape
     for shifted, pieces_ref in enumerate(orders):
@@ -106,7 +105,7 @@
     cap2 = xs[0].shape[1]
     per = blocks // count
     for shift in range(dp):
-        group = lax.rem(where_ref[0] + (dp - shift), dp)
+        group = where_ref[0] ^ shift
         for b in range(blocks):
             xs[b // per][group, :, b % per * LANES : (b % per + 1) * LANES] = arrived[shift][
                 b * cap2 : (b + 1) * cap2, :
@@ -316,7 +315,7 @@
 
 def spread_kernel(dp, where_ref, keep_ref, got_ref, crossed_ref, *outs):
     for shift in range(dp):
-        group = lax.rem(where_ref[0] + (dp - shift), dp)
+        group = where_ref[0] ^ shift
         total = keep_ref[group] + got_ref[group].astype(jnp.float32)
         total = total + crossed_ref[group].astype(jnp.float32)
         outs[shift][...] = total.astype(jnp.bfloat16)
@@ -366,17 +365,10 @@
         compiler_params=pltpu.CompilerParams(vmem_limit_bytes=48 << 20),
         name="tables",
     )(place, *inputs)
-    arrived = [sent[0]]
-    for shift in range(1, dp):
-        onward = [(i, (i + shift) % dp) for i in range(dp)]
-        arrived.append(lax.ppermute(sent[shift], "dp", onward))
-    combine = pl.pallas_call(
-        functools.partial(weights_kernel, dims),
-        in_specs=[SMEM] + [VMEM] * 2,
-        out_shape=[jax.ShapeDtypeStruct((3 * micro * rows, slots_all), jnp.bfloat16)] * 2,
-        compiler_params=pltpu.CompilerParams(vmem_limit_bytes=8 << 20),
-        name="weights",
-    )(place, routes, probs)
+    arrived = [sent[0]] * dp
+    for shift in reversed(range(1, dp)):
+        swap = [(i, i ^ shift) for i in range(dp)]
+        arrived[shift] = lax.ppermute(sent[shift], "dp", swap)
     chunks = range(IN_CHUNKS)
     stages = [[(q, c) for c in chunks] for q in range(2)] + [[(2, c), (3, c)] for c in chunks]
     weights = first_weights(where, stages[0], sent[0], w_gate, w_up, features)
@@ -417,6 +409,13 @@
             upcoming += more
             kept[side, c] = (keep, lax.ppermute(send, "tensor", core))
         weights = upcoming
+    combine = pl.pallas_call(
+        functools.partial(weights_kernel, dims),
+        in_specs=[SMEM] + [VMEM] * 2 + [pl.BlockSpec(memory_space=pl.ANY)],
+        out_shape=[jax.ShapeDtypeStruct((3 * micro * rows, slots_all), jnp.bfloat16)] * 2,
+        compiler_params=pltpu.CompilerParams(vmem_limit_bytes=8 << 20),
+        name="weights",
+    )(place, routes, probs, token)
     crossed = []
     for c in range(OUT_CHUNKS):
         keep, got = kept[1, c]
@@ -436,17 +435,17 @@
         compiler_params=pltpu.CompilerParams(vmem_limit_bytes=12 << 20),
         name="spread",
     )(place, *(a.reshape(dp, cap2, width) for a in (*kept[0, 1], crossed[1])))
-    returned.append(blocks[0])
-    for shift in range(1, dp):
-        home = [(i, (i - shift) % dp) for i in range(dp)]
-        returned.append(lax.ppermute(blocks[shift], "dp", home))
+    home = [blocks[0]] * dp
+    for shift in reversed(range(1, dp)):
+        swap = [(i, i ^ shift) for i in range(dp)]
+        home[shift] = lax.ppermute(blocks[shift], "dp", swap)
     mixed = pl.pallas_call(
         combine_kernel,
         out_shape=jax.ShapeDtypeStruct((micro, rows, features), jnp.bfloat16),
         scratch_shapes=[pltpu.VMEM((slots_all, width), jnp.bfloat16)],
         compiler_params=pltpu.CompilerParams(vmem_limit_bytes=16 << 20),
         name="combine",
-    )(*combine, *returned)
+    )(*combine, *returned, *home)
     return mixed, loss.T
 
 

time: 119 us -> 120 us (level)
  waiting for transfers between devices: 26.5 us -> 30.9 us
  starting transfers between devices: 39.5 us -> 36 us
    ppermute x14, waiting for transfers between devices: 4.72 us -> 8.63 us  [the longest x7 5.32 us: local(): home[shift] = lax.ppermute(blocks[shift], 'dp', swap)]
    all_to_all x1, starting transfers between devices: 8.15 us -> 5.6 us  [local(): back = lax.all_to_all(total, 'dp', split_axis=0, concat_axis=0, tiled=True)]
  transfers between devices with their start and end apart: 27 -> 27, of which waited for: 7 -> 7; matrix products, arithmetic and copies ran while one was open for 1% -> 1% of each run, Pallas kernels for 27% -> 26%
where the time goes in v3:
time: 120 us; the launch traced here: 119 us
  Pallas kernels  44 us (37%)
  starting transfers between devices  36 us (30%)
  waiting for transfers between devices  30.9 us (26%)
  local copies, waits for them, and re-layouts  6.62 us (6%)
    pallas_call x4, Pallas kernels, gate_up(): pl.pallas_call(functools.partial(gate_up_kernel, plan), in_specs=[SMEM] +...  23.3 us
    ppermute x2, waiting for transfers between devices, local(): crossed.append(lax.ppermute(total, 'tensor', row))  12.7 us
    ppermute x7, starting transfers between devices, local(): arrived[shift] = lax.ppermute(sent[shift], 'dp', swap)  12.5 us
    pallas_call x4, Pallas kernels, down(): pl.pallas_call(functools.partial(down_kernel, (c, part, tile_of(columns,...  11.7 us
    ppermute x7, starting transfers between devices, local(): home[shift] = lax.ppermute(blocks[shift], 'dp', swap)  11.2 us
    ppermute x2, waiting for transfers between devices, local(): crossed.append(lax.ppermute(x, 'tensor', row))  9.57 us
    unnamed x9, local copies, waits for them, and re-layouts  6.62 us
    all_to_all x1, starting transfers between devices, local(): back = lax.all_to_all(total, 'dp', split_axis=0, concat_axis=0, tiled=True)  5.6 us
  transfers between devices with their start and end apart: 27, of which 7 were waited for; matrix products, arithmetic and copies ran while one was open for 1% of the time, Pallas kernels for 26%

profile of v3, /device:TPU:0, one launch (start us, length us, event | category | flops | bytes accessed | tf_op | source)
XLA Modules:
  0.0 119.4 jit_solution(15103275512281718485)
XLA Ops:
  0.6 1.6 %tables.1 = (bf16[328,128]{1,0:T(8,128)(2,1)S(1)}, bf16[328,128]{1,0:T(8,128)(2,1)S(1)}, bf16[328,128]{1,0:T(8,128)(2,1)S(1)}, bf16[328,128]{1,0:T(8,128)(2,1)S(...) custom-call(s32[1]{0:T(128)} %bitcast.where_ref, ...), custom_call_target="tpu_custom_call" | custom-call | tf_op jit(solution)/shard_map/tables/pallas_call | solution.py:360
  2.2 3.0 %collective-permute-start = (bf16[328,128]{1,0:T(8,128)(2,1)S(1)}, bf16[328,128]{1,0:T(8,128)(2,1)S(1)}, u32[]{:S(2)}, u32[]{:S(2)}) collective-permute-start(bf16[328,128]{1,0:T(8,128)(2,1)S(1)} %get-tuple-element.55), channel_id=1, source_target_pairs={{0,4},{4,0},{8,12},{12,8},{16,20},{20,16},{24,28},{28,24},{1,5},{5... | collective-permute-start | bytes 251912 | tf_op jit(solution)/shard_map/ppermute | solution.py:371
  5.3 1.6 %collective-permute-start.1 = (bf16[328,128]{1,0:T(8,128)(2,1)S(1)}, bf16[328,128]{1,0:T(8,128)(2,1)S(1)}, u32[]{:S(2)}, u32[]{:S(2)}) collective-permute-start(bf16[328,128]{1,0:T(8,128)(2,1)S(1)} %get-tuple-element.56), channel_id=1, source_target_pairs={{0,8},{4,12},{8,0},{12,4},{16,24},{20,28},{24,16},{28,20},{1,9},{5... | collective-permute-start | bytes 251912 | tf_op jit(solution)/shard_map/ppermute | solution.py:371
  6.8 3.0 %collective-permute-start.3 = (bf16[328,128]{1,0:T(8,128)(2,1)S(1)}, bf16[328,128]{1,0:T(8,128)(2,1)S(1)}, u32[]{:S(2)}, u32[]{:S(2)}) collective-permute-start(bf16[328,128]{1,0:T(8,128)(2,1)S(1)} %get-tuple-element.58), channel_id=1, source_target_pairs={{0,16},{4,20},{8,24},{12,28},{16,0},{20,4},{24,8},{28,12},{1,17},{... | collective-permute-start | bytes 251912 | tf_op jit(solution)/shard_map/ppermute | solution.py:371
  9.9 1.3 %collective-permute-start.4 = (bf16[328,128]{1,0:T(8,128)(2,1)S(1)}, bf16[328,128]{1,0:T(8,128)(2,1)S(1)}, u32[]{:S(2)}, u32[]{:S(2)}) collective-permute-start(bf16[328,128]{1,0:T(8,128)(2,1)S(1)} %get-tuple-element.59), channel_id=1, source_target_pairs={{0,20},{4,16},{8,28},{12,24},{16,4},{20,0},{24,12},{28,8},{1,21},{... | collective-permute-start | bytes 251912 | tf_op jit(solution)/shard_map/ppermute | solution.py:371
  11.1 3.6 %collective-permute-start.5 = (bf16[328,128]{1,0:T(8,128)(2,1)S(1)}, bf16[328,128]{1,0:T(8,128)(2,1)S(1)}, u32[]{:S(2)}, u32[]{:S(2)}) collective-permute-start(bf16[328,128]{1,0:T(8,128)(2,1)S(1)} %get-tuple-element.60), channel_id=1, source_target_pairs={{0,24},{4,28},{8,16},{12,20},{16,8},{20,12},{24,0},{28,4},{1,25},{... | collective-permute-start | bytes 251912 | tf_op jit(solution)/shard_map/ppermute | solution.py:371
  14.8 5.3 %first.1 = (bf16[1024,3584]{1,0:T(8,128)(2,1)S(1)}, bf16[1024,3584]{1,0:T(8,128)(2,1)S(1)}) custom-call(s32[1]{0:T(128)} %bitcast.3.where_ref, bf16[328,128]{1,0:T(8,128)(2,1)S(1)} %get-tuple-element.54.refs_0_.after_ref, bf16[1,4096,3584]{2,1,0:T(8,128)(2,1)} %refs_6_.4, bf16[1,4096,3584]{2,1,0:T(8,128)(2,1)} %refs_7_.3), custom_call_target="tpu_custom_call" | custom-call | tf_op jit(solution)/shard_map/first/pallas_call | solution.py:222
  20.1 3.3 %collective-permute-done.4.refs_5_ = bf16[328,128]{1,0:T(8,128)(2,1)S(1)} collective-permute-done((bf16[328,128]{1,0:T(8,128)(2,1)S(1)}, bf16[328,128]{1,0:T(8,128)(2,1)S(1)}, u32[]{:S(2)}, u32[]{:S(2)}) %collective-permute-start.4) | collective-permute-done | bytes 84000 | tf_op jit(solution)/shard_map/ppermute | solution.py:371
  23.4 0.2 repack.1
  23.7 1.6 %collective-permute-start.9 = (bf16[320,512]{1,0:T(8,128)(2,1)S(1)}, bf16[320,512]{1,0:T(8,128)(2,1)S(1)}, u32[]{:S(2)}, u32[]{:S(2)}) collective-permute-start(bf16[320,512]{1,0:T(8,128)(2,1)S(1)} %bitcast.20), channel_id=1, source_target_pairs={{0,2},{1,3},{2,0},{3,1},{4,6},{5,7},{6,4},{7,5},{8,10},{9,11},{10,... | collective-permute-start | bytes 983048 | tf_op jit(solution)/shard_map/ppermute | solution.py:388
  25.2 0.2 collective-permute-start.12
  25.4 0.5 collective-permute-start.7
  25.9 5.3 %shard_map.77 = (f32[320,3584]{1,0:T(8,128)S(1)}, f32[320,3584]{1,0:T(8,128)S(1)}, bf16[1024,3584]{1,0:T(8,128)(2,1)S(1)}, bf16[1024,3584]{1,0:T(8,128)(2,1)S(1)}) custom-call(s32[1]{0:T(128)} %bitcast.3.where_ref, bf16[320,512]{1,0:T(8,128)(2,1)S(1)} %bitcast.21, bf16[320,512]{1,0:T(8,128)(2,1)S(1)} %bitcast.18, ...), custom_call_target="tpu_custom_call" | custom-call | flops 4697620480 | bytes 14680064 | tf_op jit(solution)/shard_map/pallas_call | solution.py:248
  31.2 3.1 %collective-permute-done.9.refs_0_ = bf16[320,512]{1,0:T(8,128)(2,1)S(1)} collective-permute-done((bf16[320,512]{1,0:T(8,128)(2,1)S(1)}, bf16[320,512]{1,0:T(8,128)(2,1)S(1)}, u32[]{:S(2)}, u32[]{:S(2)}) %collective-permute-start.9) | collective-permute-done | bytes 327712 | tf_op jit(solution)/shard_map/ppermute | solution.py:388
  34.3 6.5 %collective-permute-done.7.refs_0_ = bf16[320,512]{1,0:T(8,128)(2,1)S(1)} collective-permute-done((bf16[320,512]{1,0:T(8,128)(2,1)S(1)}, bf16[320,512]{1,0:T(8,128)(2,1)S(1)}, u32[]{:S(2)}, u32[]{:S(2)}) %collective-permute-start.7) | collective-permute-done | bytes 327712 | tf_op jit(solution)/shard_map/ppermute | solution.py:388
  40.8 5.8 %shard_map.78 = (f32[320,3584]{1,0:T(8,128)S(1)}, f32[320,3584]{1,0:T(8,128)S(1)}, bf16[1024,3584]{1,0:T(8,128)(2,1)S(1)}, bf16[1024,3584]{1,0:T(8,128)(2,1)S(1)}) custom-call(s32[1]{0:T(128)} %bitcast.3.where_ref, bf16[320,512]{1,0:T(8,128)(2,1)S(1)} %collective-permute-done.11.refs_0_, ...), custom_call_target="tpu_custom_call", output_to_operand_aliasing={{0}: (5, {}), {1}: (6, {})} | custom-call | flops 4697620480 | bytes 14680064 | tf_op jit(solution)/shard_map/pallas_call | solution.py:248
  46.6 5.8 %shard_map.79 = (f32[320,3584]{1,0:T(8,128)S(1)}, f32[320,3584]{1,0:T(8,128)S(1)}, bf16[1024,3584]{1,0:T(8,128)(2,1)S(1)}, bf16[1024,3584]{1,0:T(8,128)(2,1)S(1)}) custom-call(s32[1]{0:T(128)} %bitcast.3.where_ref, bf16[320,512]{1,0:T(8,128)(2,1)S(1)} %collective-permute-done.9.refs_0_, ...), custom_call_target="tpu_custom_call", output_to_operand_aliasing={{0}: (5, {}), {1}: (6, {})} | custom-call | flops 4697620480 | bytes 14680064 | tf_op jit(solution)/shard_map/pallas_call | solution.py:248
  52.4 2.9 %copy-done = bf16[1024,3584]{1,0:T(8,128)(2,1)} copy-done((bf16[1024,3584]{1,0:T(8,128)(2,1)}, bf16[1024,3584]{1,0:T(8,128)(2,1)S(1)}, u32[]{:S(2)}) %copy-start) | copy-done | bytes 7340056
  55.3 3.1 %copy-done.1 = bf16[1024,3584]{1,0:T(8,128)(2,1)S(1)} copy-done((bf16[1024,3584]{1,0:T(8,128)(2,1)S(1)}, bf16[1024,3584]{1,0:T(8,128)(2,1)}, u32[]{:S(2)}) %copy-start.1) | copy-done | bytes 7340056
  58.4 6.4 %shard_map.80 = (bf16[320,3584]{1,0:T(8,128)(2,1)S(1)}, bf16[1792,2048]{1,0:T(8,128)(2,1)S(1)}, bf16[1792,2048]{1,0:T(8,128)(2,1)S(1)}) custom-call(s32[1]{0:T(128)} %bitcast.3.where_ref, bf16[320,512]{1,0:T(8,128)(2,1)S(1)} %collective-permute-done.7.refs_0_, bf16[320,512]{1,0:T(8,128)(2,1)S(1)} %collective-permute-done.8.refs_1_, ...), custom_call_target="tpu_custom_call" | custom-call | flops 4697620480 | bytes 14680064 | tf_op jit(solution)/shard_map/pallas_call | solution.py:248
  64.9 3.1 %shard_map.81 = (f32[320,512]{1,0:T(8,128)S(1)}, bf16[320,512]{1,0:T(8,128)(2,1)S(1)}, f32[8,128]{1,0:T(8,128)S(1)}, bf16[1792,2048]{1,0:T(8,128)(2,1)S(1)}) custom-call(s32[1]{0:T(128)} %bitcast.3.where_ref, bf16[320,3584]{1,0:T(8,128)(2,1)S(1)} %get-tuple-element.78.h_ref, bf16[1792,2048]{1,0:T(8,128)(2,1)S(1)} %get-tuple-element.79.w_a, ...), custom_call_target="tpu_custom_call" | custom-call | flops 2348810240 | bytes 7340032 | tf_op jit(solution)/shard_map/pallas_call | solution.py:303
  68.0 0.6 collective-permute-start.14
  68.5 3.1 %shard_map.82 = (f32[320,512]{1,0:T(8,128)S(1)}, bf16[320,512]{1,0:T(8,128)(2,1)S(1)}, f32[8,128]{1,0:T(8,128)S(1)}, bf16[1792,2048]{1,0:T(8,128)(2,1)S(1)}) custom-call(s32[1]{0:T(128)} %bitcast.3.where_ref, bf16[320,3584]{1,0:T(8,128)(2,1)S(1)} %get-tuple-element.78.h_ref, bf16[1792,2048]{1,0:T(8,128)(2,1)S(1)} %get-tuple-element.79.w_a, ...), custom_call_target="tpu_custom_call" | custom-call | flops 2348810240 | bytes 7340032 | tf_op jit(solution)/shard_map/pallas_call | solution.py:303
  71.6 2.8 %shard_map.83 = (f32[320,512]{1,0:T(8,128)S(1)}, bf16[320,512]{1,0:T(8,128)(2,1)S(1)}, f32[8,128]{1,0:T(8,128)S(1)}) custom-call(s32[1]{0:T(128)} %bitcast.3.where_ref, bf16[320,3584]{1,0:T(8,128)(2,1)S(1)} %get-tuple-element.78.h_ref, bf16[1792,2048]{1,0:T(8,128)(2,1)S(1)} %get-tuple-element.82.w_a, bf16[1792,2048]{1,0:T(8,128)(2,1)S(1)} %get-tuple-element.84.w_b, ...), custom_call_target="tpu_custom_call" | custom-call | flops 2348810240 | bytes 7340032 | tf_op jit(solution)/shard_map/pallas_call | solution.py:303
  74.5 0.1 add_convert_fusion.2
  74.6 1.6 %collective-permute-start.15 = (bf16[320,512]{1,0:T(8,128)(2,1)S(1)}, bf16[320,512]{1,0:T(8,128)(2,1)S(1)}, u32[]{:S(2)}, u32[]{:S(2)}) collective-permute-start(bf16[320,512]{1,0:T(8,128)(2,1)S(1)} %add_convert_fusion.2), channel_id=1, source_target_pairs={{0,2},{1,3},{2,0},{3,1},{4,6},{5,7},{6,4},{7,5},{8,10},{9,11},{10,... | collective-permute-start | bytes 983048 | tf_op jit(solution)/shard_map/ppermute | solution.py:423
  76.2 0.2 collective-permute-start.17
  76.4 2.8 %shard_map.84 = (f32[320,512]{1,0:T(8,128)S(1)}, bf16[320,512]{1,0:T(8,128)(2,1)S(1)}, f32[8,128]{1,0:T(8,128)S(1)}) custom-call(s32[1]{0:T(128)} %bitcast.3.where_ref, bf16[320,3584]{1,0:T(8,128)(2,1)S(1)} %get-tuple-element.78.h_ref, bf16[1792,2048]{1,0:T(8,128)(2,1)S(1)} %get-tuple-element.82.w_a, bf16[1792,2048]{1,0:T(8,128)(2,1)S(1)} %get-tuple-element.84.w_b, ...), custom_call_target="tpu_custom_call" | custom-call | flops 2348810240 | bytes 7340032 | tf_op jit(solution)/shard_map/pallas_call | solution.py:303
  79.2 0.4 collective-permute-start.16
  79.5 5.2 %collective-permute-done.15 = bf16[320,512]{1,0:T(8,128)(2,1)S(1)} collective-permute-done((bf16[320,512]{1,0:T(8,128)(2,1)S(1)}, bf16[320,512]{1,0:T(8,128)(2,1)S(1)}, u32[]{:S(2)}, u32[]{:S(2)}) %collective-permute-start.15) | collective-permute-done | bytes 327712 | tf_op jit(solution)/shard_map/ppermute | solution.py:423
  84.8 0.9 add_convert_fusion.1
  85.6 5.6 %all-to-all-start = ((bf16[8,40,512]{2,1,0:T(8,128)(2,1)}), bf16[8,40,512]{2,1,0:T(8,128)(2,1)S(1)}, u32[]{:S(2)}, u32[]{:S(2)}) async-start(bf16[8,40,512]{2,1,0:T(8,128)(2,1)} %bitcast.6), calls=%async_computation | async-start | bytes 655360 | tf_op jit(solution)/shard_map/all_to_all | solution.py:427
  91.2 0.1 add_convert_fusion
  91.3 1.6 %collective-permute-start.18 = (bf16[320,512]{1,0:T(8,128)(2,1)S(1)}, bf16[320,512]{1,0:T(8,128)(2,1)S(1)}, u32[]{:S(2)}, u32[]{:S(2)}) collective-permute-start(bf16[320,512]{1,0:T(8,128)(2,1)S(1)} %add_convert_fusion), channel_id=1, source_target_pairs={{0,2},{1,3},{2,0},{3,1},{4,6},{5,7},{6,4},{7,5},{8,10},{9,11},{10,... | collective-permute-start | bytes 983048 | tf_op jit(solution)/shard_map/ppermute | solution.py:423
  92.9 7.5 %collective-permute-done.18 = bf16[320,512]{1,0:T(8,128)(2,1)S(1)} collective-permute-done((bf16[320,512]{1,0:T(8,128)(2,1)S(1)}, bf16[320,512]{1,0:T(8,128)(2,1)S(1)}, u32[]{:S(2)}, u32[]{:S(2)}) %collective-permute-start.18) | collective-permute-done | bytes 327712 | tf_op jit(solution)/shard_map/ppermute | solution.py:423
  100.4 0.1 spread.1
  100.5 1.8 %collective-permute-start.19 = (bf16[40,512]{1,0:T(8,128)(2,1)S(1)}, bf16[40,512]{1,0:T(8,128)(2,1)S(1)}, u32[]{:S(2)}, u32[]{:S(2)}) collective-permute-start(bf16[40,512]{1,0:T(8,128)(2,1)S(1)} %get-tuple-element.99), channel_id=1, source_target_pairs={{0,4},{4,0},{8,12},{12,8},{16,20},{20,16},{24,28},{28,24},{1,5},{5... | collective-permute-start | bytes 122888 | tf_op jit(solution)/shard_map/ppermute | solution.py:441
  102.3 1.5 %collective-permute-start.20 = (bf16[40,512]{1,0:T(8,128)(2,1)S(1)}, bf16[40,512]{1,0:T(8,128)(2,1)S(1)}, u32[]{:S(2)}, u32[]{:S(2)}) collective-permute-start(bf16[40,512]{1,0:T(8,128)(2,1)S(1)} %get-tuple-element.100), channel_id=1, source_target_pairs={{0,8},{4,12},{8,0},{12,4},{16,24},{20,28},{24,16},{28,20},{1,9},{5... | collective-permute-start | bytes 122888 | tf_op jit(solution)/shard_map/ppermute | solution.py:441
  103.8 0.3 collective-permute-start.21
  104.0 2.6 %collective-permute-start.22 = (bf16[40,512]{1,0:T(8,128)(2,1)S(1)}, bf16[40,512]{1,0:T(8,128)(2,1)S(1)}, u32[]{:S(2)}, u32[]{:S(2)}) collective-permute-start(bf16[40,512]{1,0:T(8,128)(2,1)S(1)} %get-tuple-element.102), channel_id=1, source_target_pairs={{0,16},{4,20},{8,24},{12,28},{16,0},{20,4},{24,8},{28,12},{1,17},{... | collective-permute-start | bytes 122888 | tf_op jit(solution)/shard_map/ppermute | solution.py:441
  106.7 1.5 %collective-permute-start.23 = (bf16[40,512]{1,0:T(8,128)(2,1)S(1)}, bf16[40,512]{1,0:T(8,128)(2,1)S(1)}, u32[]{:S(2)}, u32[]{:S(2)}) collective-permute-start(bf16[40,512]{1,0:T(8,128)(2,1)S(1)} %get-tuple-element.103), channel_id=1, source_target_pairs={{0,20},{4,16},{8,28},{12,24},{16,4},{20,0},{24,12},{28,8},{1,21},{... | collective-permute-start | bytes 122888 | tf_op jit(solution)/shard_map/ppermute | solution.py:441
  108.2 3.3 %collective-permute-start.24 = (bf16[40,512]{1,0:T(8,128)(2,1)S(1)}, bf16[40,512]{1,0:T(8,128)(2,1)S(1)}, u32[]{:S(2)}, u32[]{:S(2)}) collective-permute-start(bf16[40,512]{1,0:T(8,128)(2,1)S(1)} %get-tuple-element.104), channel_id=1, source_target_pairs={{0,24},{4,28},{8,16},{12,20},{16,8},{20,12},{24,0},{28,4},{1,25},{... | collective-permute-start | bytes 122888 | tf_op jit(solution)/shard_map/ppermute | solution.py:441
  111.4 0.3 collective-permute-start.25
  111.7 0.6 copy.12
  112.3 0.4 weights.1
  112.8 1.1 collective-permute-done.24.refs_6_
  114.0 4.2 %collective-permute-done.25.refs_7_ = bf16[40,512]{1,0:T(8,128)(2,1)S(1)} collective-permute-done((bf16[40,512]{1,0:T(8,128)(2,1)S(1)}, bf16[40,512]{1,0:T(8,128)(2,1)S(1)}, u32[]{:S(2)}, u32[]{:S(2)}) %collective-permute-start.25) | collective-permute-done | bytes 40992 | tf_op jit(solution)/shard_map/ppermute | solution.py:441
  118.1 1.3 %combine.1 = bf16[2,64,1024]{2,1,0:T(8,128)(2,1)} custom-call(bf16[384,320]{1,0:T(8,128)(2,1)S(1)} %get-tuple-element.88.whole_ref, bf16[384,320]{1,0:T(8,128)(2,1)S(1)} %get-tuple-element.89.shifted_ref, bf16[320,512]{1,0:T(8,128)(2,1)S(1)} %bitcast.12, bf16[40,512]{1,0:T(8,128)(2,1)S(1)} %get-tuple-element.98.refs_0_, ...), custom_call_target="tpu_custom_call" | custom-call | tf_op jit(solution)/shard_map/combine/pallas_call | solution.py:442
  (32 shorter events, 0.3 us)
Async XLA Ops:
  2.2 8.9 %collective-permute-start = (bf16[328,128]{1,0:T(8,128)(2,1)S(1)}, bf16[328,128]{1,0:T(8,128)(2,1)S(1)}, u32[]{:S(2)}, u32[]{:S(2)}) collective-permute-start(bf16[328,128]{1,0:T(8,128)(2,1)S(1)} %get-tuple-element.55), channel_id=1, source_target_pairs={{0,4},{4,0},{8,12},{12,8},{16,20},{20,16},{24,28},{28,24},{1,5},{5... | collective-permute-start | bytes 251912 | tf_op jit(solution)/shard_map/ppermute | solution.py:371
  5.3 9.5 %collective-permute-start.1 = (bf16[328,128]{1,0:T(8,128)(2,1)S(1)}, bf16[328,128]{1,0:T(8,128)(2,1)S(1)}, u32[]{:S(2)}, u32[]{:S(2)}) collective-permute-start(bf16[328,128]{1,0:T(8,128)(2,1)S(1)} %get-tuple-element.56), channel_id=1, source_target_pairs={{0,8},{4,12},{8,0},{12,4},{16,24},{20,28},{24,16},{28,20},{1,9},{5... | collective-permute-start | bytes 251912 | tf_op jit(solution)/shard_map/ppermute | solution.py:371
  6.8 13.2 %collective-permute-start.2 = (bf16[328,128]{1,0:T(8,128)(2,1)S(1)}, bf16[328,128]{1,0:T(8,128)(2,1)S(1)}, u32[]{:S(2)}, u32[]{:S(2)}) collective-permute-start(bf16[328,128]{1,0:T(8,128)(2,1)S(1)} %get-tuple-element.57), channel_id=1, source_target_pairs={{0,12},{4,8},{8,4},{12,0},{16,28},{20,24},{24,20},{28,16},{1,13},{... | collective-permute-start | bytes 251912 | tf_op jit(solution)/shard_map/ppermute | solution.py:371
  6.8 13.3 %collective-permute-start.3 = (bf16[328,128]{1,0:T(8,128)(2,1)S(1)}, bf16[328,128]{1,0:T(8,128)(2,1)S(1)}, u32[]{:S(2)}, u32[]{:S(2)}) collective-permute-start(bf16[328,128]{1,0:T(8,128)(2,1)S(1)} %get-tuple-element.58), channel_id=1, source_target_pairs={{0,16},{4,20},{8,24},{12,28},{16,0},{20,4},{24,8},{28,12},{1,17},{... | collective-permute-start | bytes 251912 | tf_op jit(solution)/shard_map/ppermute | solution.py:371
  9.9 13.5 %collective-permute-start.4 = (bf16[328,128]{1,0:T(8,128)(2,1)S(1)}, bf16[328,128]{1,0:T(8,128)(2,1)S(1)}, u32[]{:S(2)}, u32[]{:S(2)}) collective-permute-start(bf16[328,128]{1,0:T(8,128)(2,1)S(1)} %get-tuple-element.59), channel_id=1, source_target_pairs={{0,20},{4,16},{8,28},{12,24},{16,4},{20,0},{24,12},{28,8},{1,21},{... | collective-permute-start | bytes 251912 | tf_op jit(solution)/shard_map/ppermute | solution.py:371
  11.1 12.3 %collective-permute-start.5 = (bf16[328,128]{1,0:T(8,128)(2,1)S(1)}, bf16[328,128]{1,0:T(8,128)(2,1)S(1)}, u32[]{:S(2)}, u32[]{:S(2)}) collective-permute-start(bf16[328,128]{1,0:T(8,128)(2,1)S(1)} %get-tuple-element.60), channel_id=1, source_target_pairs={{0,24},{4,28},{8,16},{12,20},{16,8},{20,12},{24,0},{28,4},{1,25},{... | collective-permute-start | bytes 251912 | tf_op jit(solution)/shard_map/ppermute | solution.py:371
  14.7 8.7 %collective-permute-start.6 = (bf16[328,128]{1,0:T(8,128)(2,1)S(1)}, bf16[328,128]{1,0:T(8,128)(2,1)S(1)}, u32[]{:S(2)}, u32[]{:S(2)}) collective-permute-start(bf16[328,128]{1,0:T(8,128)(2,1)S(1)} %get-tuple-element.61), channel_id=1, source_target_pairs={{0,28},{4,24},{8,20},{12,16},{16,12},{20,8},{24,4},{28,0},{1,29},{... | collective-permute-start | bytes 251912 | tf_op jit(solution)/shard_map/ppermute | solution.py:371
  23.6 17.2 %collective-permute-start.11 = (bf16[320,512]{1,0:T(8,128)(2,1)S(1)}, bf16[320,512]{1,0:T(8,128)(2,1)S(1)}, u32[]{:S(2)}, u32[]{:S(2)}) collective-permute-start(bf16[320,512]{1,0:T(8,128)(2,1)S(1)} %bitcast.19), channel_id=1, source_target_pairs={{0,1},{1,0},{2,3},{3,2},{4,5},{5,4},{6,7},{7,6},{8,9},{9,8},{10,11... | collective-permute-start | bytes 983048 | tf_op jit(solution)/shard_map/ppermute | solution.py:387
  23.7 10.7 %collective-permute-start.9 = (bf16[320,512]{1,0:T(8,128)(2,1)S(1)}, bf16[320,512]{1,0:T(8,128)(2,1)S(1)}, u32[]{:S(2)}, u32[]{:S(2)}) collective-permute-start(bf16[320,512]{1,0:T(8,128)(2,1)S(1)} %bitcast.20), channel_id=1, source_target_pairs={{0,2},{1,3},{2,0},{3,1},{4,6},{5,7},{6,4},{7,5},{8,10},{9,11},{10,... | collective-permute-start | bytes 983048 | tf_op jit(solution)/shard_map/ppermute | solution.py:388
  25.2 15.6 %collective-permute-start.12 = (bf16[320,512]{1,0:T(8,128)(2,1)S(1)}, bf16[320,512]{1,0:T(8,128)(2,1)S(1)}, u32[]{:S(2)}, u32[]{:S(2)}) collective-permute-start(bf16[320,512]{1,0:T(8,128)(2,1)S(1)} %bitcast.16), channel_id=1, source_target_pairs={{0,1},{1,0},{2,3},{3,2},{4,5},{5,4},{6,7},{7,6},{8,9},{9,8},{10,11... | collective-permute-start | bytes 983048 | tf_op jit(solution)/shard_map/ppermute | solution.py:387
  25.4 15.4 %collective-permute-start.7 = (bf16[320,512]{1,0:T(8,128)(2,1)S(1)}, bf16[320,512]{1,0:T(8,128)(2,1)S(1)}, u32[]{:S(2)}, u32[]{:S(2)}) collective-permute-start(bf16[320,512]{1,0:T(8,128)(2,1)S(1)} %bitcast.17), channel_id=1, source_target_pairs={{0,2},{1,3},{2,0},{3,1},{4,6},{5,7},{6,4},{7,5},{8,10},{9,11},{10,... | collective-permute-start | bytes 983048 | tf_op jit(solution)/shard_map/ppermute | solution.py:388
  34.3 12.3 %collective-permute-start.10 = (bf16[320,512]{1,0:T(8,128)(2,1)S(1)}, bf16[320,512]{1,0:T(8,128)(2,1)S(1)}, u32[]{:S(2)}, u32[]{:S(2)}) collective-permute-start(bf16[320,512]{1,0:T(8,128)(2,1)S(1)} %collective-permute-done.9.refs_0_), channel_id=1, source_target_pairs={{0,1},{1,0},{2,3},{3,2},{4,5},{5,4},{6,7},{7,6},{8,9},{9,8},{10,11... | collective-permute-start | bytes 983048 | tf_op jit(solution)/shard_map/ppermute | solution.py:391
  40.8 14.6 %collective-permute-start.8 = (bf16[320,512]{1,0:T(8,128)(2,1)S(1)}, bf16[320,512]{1,0:T(8,128)(2,1)S(1)}, u32[]{:S(2)}, u32[]{:S(2)}) collective-permute-start(bf16[320,512]{1,0:T(8,128)(2,1)S(1)} %collective-permute-done.7.refs_0_), channel_id=1, source_target_pairs={{0,1},{1,0},{2,3},{3,2},{4,5},{5,4},{6,7},{7,6},{8,9},{9,8},{10,11... | collective-permute-start | bytes 983048 | tf_op jit(solution)/shard_map/ppermute | solution.py:391
  52.4 2.9 %copy-start = (bf16[1024,3584]{1,0:T(8,128)(2,1)}, bf16[1024,3584]{1,0:T(8,128)(2,1)S(1)}, u32[]{:S(2)}) copy-start(bf16[1024,3584]{1,0:T(8,128)(2,1)S(1)} %get-tuple-element.74.refs_2_) | copy-start | bytes 22020100
  55.3 3.1 %copy-start.1 = (bf16[1024,3584]{1,0:T(8,128)(2,1)S(1)}, bf16[1024,3584]{1,0:T(8,128)(2,1)}, u32[]{:S(2)}) copy-start(bf16[1024,3584]{1,0:T(8,128)(2,1)} %copy-done) | copy-start | bytes 22020100
  68.0 6.5 %collective-permute-start.14 = (bf16[320,512]{1,0:T(8,128)(2,1)S(1)}, bf16[320,512]{1,0:T(8,128)(2,1)S(1)}, u32[]{:S(2)}, u32[]{:S(2)}) collective-permute-start(bf16[320,512]{1,0:T(8,128)(2,1)S(1)} %get-tuple-element.93), channel_id=1, source_target_pairs={{0,1},{1,0},{2,3},{3,2},{4,5},{5,4},{6,7},{7,6},{8,9},{9,8},{10,11... | collective-permute-start | bytes 983048 | tf_op jit(solution)/shard_map/ppermute | solution.py:410
  74.4 5.1 %collective-permute-start.13 = (bf16[320,512]{1,0:T(8,128)(2,1)S(1)}, bf16[320,512]{1,0:T(8,128)(2,1)S(1)}, u32[]{:S(2)}, u32[]{:S(2)}) collective-permute-start(bf16[320,512]{1,0:T(8,128)(2,1)S(1)} %get-tuple-element.91), channel_id=1, source_target_pairs={{0,1},{1,0},{2,3},{3,2},{4,5},{5,4},{6,7},{7,6},{8,9},{9,8},{10,11... | collective-permute-start | bytes 983048 | tf_op jit(solution)/shard_map/ppermute | solution.py:410
  74.6 10.2 %collective-permute-start.15 = (bf16[320,512]{1,0:T(8,128)(2,1)S(1)}, bf16[320,512]{1,0:T(8,128)(2,1)S(1)}, u32[]{:S(2)}, u32[]{:S(2)}) collective-permute-start(bf16[320,512]{1,0:T(8,128)(2,1)S(1)} %add_convert_fusion.2), channel_id=1, source_target_pairs={{0,2},{1,3},{2,0},{3,1},{4,6},{5,7},{6,4},{7,5},{8,10},{9,11},{10,... | collective-permute-start | bytes 983048 | tf_op jit(solution)/shard_map/ppermute | solution.py:423
  76.2 15.0 %collective-permute-start.17 = (bf16[320,512]{1,0:T(8,128)(2,1)S(1)}, bf16[320,512]{1,0:T(8,128)(2,1)S(1)}, u32[]{:S(2)}, u32[]{:S(2)}) collective-permute-start(bf16[320,512]{1,0:T(8,128)(2,1)S(1)} %get-tuple-element.97), channel_id=1, source_target_pairs={{0,1},{1,0},{2,3},{3,2},{4,5},{5,4},{6,7},{7,6},{8,9},{9,8},{10,11... | collective-permute-start | bytes 983048 | tf_op jit(solution)/shard_map/ppermute | solution.py:410
  76.4 35.9 %copy-start.2 = (f32[2,64,8]{1,2,0:T(8,128)S(1)}, f32[2,64,8]{1,2,0:T(8,128)}, u32[]{:S(2)}) copy-start(f32[2,64,8]{1,2,0:T(8,128)} %param.8) | copy-start | bytes 12292
  76.4 35.9 %copy-start.3 = (s32[2,64,2]{1,2,0:T(2,128)S(1)}, s32[2,64,2]{1,2,0:T(2,128)}, u32[]{:S(2)}) copy-start(s32[2,64,2]{1,2,0:T(2,128)} %param.7) | copy-start | bytes 3076
  79.2 13.8 %collective-permute-start.16 = (bf16[320,512]{1,0:T(8,128)(2,1)S(1)}, bf16[320,512]{1,0:T(8,128)(2,1)S(1)}, u32[]{:S(2)}, u32[]{:S(2)}) collective-permute-start(bf16[320,512]{1,0:T(8,128)(2,1)S(1)} %get-tuple-element.95), channel_id=1, source_target_pairs={{0,1},{1,0},{2,3},{3,2},{4,5},{5,4},{6,7},{7,6},{8,9},{9,8},{10,11... | collective-permute-start | bytes 983048 | tf_op jit(solution)/shard_map/ppermute | solution.py:410
  85.6 32.5 %all-to-all-start = ((bf16[8,40,512]{2,1,0:T(8,128)(2,1)}), bf16[8,40,512]{2,1,0:T(8,128)(2,1)S(1)}, u32[]{:S(2)}, u32[]{:S(2)}) async-start(bf16[8,40,512]{2,1,0:T(8,128)(2,1)} %bitcast.6), calls=%async_computation | async-start | bytes 655360 | tf_op jit(solution)/shard_map/all_to_all | solution.py:427
  91.3 9.0 %collective-permute-start.18 = (bf16[320,512]{1,0:T(8,128)(2,1)S(1)}, bf16[320,512]{1,0:T(8,128)(2,1)S(1)}, u32[]{:S(2)}, u32[]{:S(2)}) collective-permute-start(bf16[320,512]{1,0:T(8,128)(2,1)S(1)} %add_convert_fusion), channel_id=1, source_target_pairs={{0,2},{1,3},{2,0},{3,1},{4,6},{5,7},{6,4},{7,5},{8,10},{9,11},{10,... | collective-permute-start | bytes 983048 | tf_op jit(solution)/shard_map/ppermute | solution.py:423
  100.5 7.7 %collective-permute-start.19 = (bf16[40,512]{1,0:T(8,128)(2,1)S(1)}, bf16[40,512]{1,0:T(8,128)(2,1)S(1)}, u32[]{:S(2)}, u32[]{:S(2)}) collective-permute-start(bf16[40,512]{1,0:T(8,128)(2,1)S(1)} %get-tuple-element.99), channel_id=1, source_target_pairs={{0,4},{4,0},{8,12},{12,8},{16,20},{20,16},{24,28},{28,24},{1,5},{5... | collective-permute-start | bytes 122888 | tf_op jit(solution)/shard_map/ppermute | solution.py:441
  102.3 9.1 %collective-permute-start.20 = (bf16[40,512]{1,0:T(8,128)(2,1)S(1)}, bf16[40,512]{1,0:T(8,128)(2,1)S(1)}, u32[]{:S(2)}, u32[]{:S(2)}) collective-permute-start(bf16[40,512]{1,0:T(8,128)(2,1)S(1)} %get-tuple-element.100), channel_id=1, source_target_pairs={{0,8},{4,12},{8,0},{12,4},{16,24},{20,28},{24,16},{28,20},{1,9},{5... | collective-permute-start | bytes 122888 | tf_op jit(solution)/shard_map/ppermute | solution.py:441
  103.8 9.0 %collective-permute-start.21 = (bf16[40,512]{1,0:T(8,128)(2,1)S(1)}, bf16[40,512]{1,0:T(8,128)(2,1)S(1)}, u32[]{:S(2)}, u32[]{:S(2)}) collective-permute-start(bf16[40,512]{1,0:T(8,128)(2,1)S(1)} %get-tuple-element.101), channel_id=1, source_target_pairs={{0,12},{4,8},{8,4},{12,0},{16,28},{20,24},{24,20},{28,16},{1,13},{... | collective-permute-start | bytes 122888 | tf_op jit(solution)/shard_map/ppermute | solution.py:441
  104.0 8.8 %collective-permute-start.22 = (bf16[40,512]{1,0:T(8,128)(2,1)S(1)}, bf16[40,512]{1,0:T(8,128)(2,1)S(1)}, u32[]{:S(2)}, u32[]{:S(2)}) collective-permute-start(bf16[40,512]{1,0:T(8,128)(2,1)S(1)} %get-tuple-element.102), channel_id=1, source_target_pairs={{0,16},{4,20},{8,24},{12,28},{16,0},{20,4},{24,8},{28,12},{1,17},{... | collective-permute-start | bytes 122888 | tf_op jit(solution)/shard_map/ppermute | solution.py:441
  106.7 6.1 %collective-permute-start.23 = (bf16[40,512]{1,0:T(8,128)(2,1)S(1)}, bf16[40,512]{1,0:T(8,128)(2,1)S(1)}, u32[]{:S(2)}, u32[]{:S(2)}) collective-permute-start(bf16[40,512]{1,0:T(8,128)(2,1)S(1)} %get-tuple-element.103), channel_id=1, source_target_pairs={{0,20},{4,16},{8,28},{12,24},{16,4},{20,0},{24,12},{28,8},{1,21},{... | collective-permute-start | bytes 122888 | tf_op jit(solution)/shard_map/ppermute | solution.py:441
  108.2 5.8 %collective-permute-start.24 = (bf16[40,512]{1,0:T(8,128)(2,1)S(1)}, bf16[40,512]{1,0:T(8,128)(2,1)S(1)}, u32[]{:S(2)}, u32[]{:S(2)}) collective-permute-start(bf16[40,512]{1,0:T(8,128)(2,1)S(1)} %get-tuple-element.104), channel_id=1, source_target_pairs={{0,24},{4,28},{8,16},{12,20},{16,8},{20,12},{24,0},{28,4},{1,25},{... | collective-permute-start | bytes 122888 | tf_op jit(solution)/shard_map/ppermute | solution.py:441
  111.4 6.7 %collective-permute-start.25 = (bf16[40,512]{1,0:T(8,128)(2,1)S(1)}, bf16[40,512]{1,0:T(8,128)(2,1)S(1)}, u32[]{:S(2)}, u32[]{:S(2)}) collective-permute-start(bf16[40,512]{1,0:T(8,128)(2,1)S(1)} %get-tuple-element.105), channel_id=1, source_target_pairs={{0,28},{4,24},{8,20},{12,16},{16,12},{20,8},{24,4},{28,0},{1,29},{... | collective-permute-start | bytes 122888 | tf_op jit(solution)/shard_map/ppermute | solution.py:441

commit v4 on v3

--- a/solution.py
+++ b/solution.py
@@ -321,22 +321,29 @@
         outs[shift][...] = total.astype(jnp.bfloat16)
 
 
-def combine_kernel(whole_ref, shifted_ref, first_ref, *refs):
-    blocks, out_ref, rows_ref = refs[:-2], refs[-2], refs[-1]
+def combine_rows(pieces, part, out_ref, at):
     micro, rows, _ = out_ref.shape
     each = micro * rows
+    width = part.shape[1]
+    total = jnp.dot(pieces[...], part[...], preferred_element_type=jnp.float32)
+    total = (total[2 * each :] + total[each : 2 * each]) + total[:each]
+    total = total.astype(jnp.bfloat16)
+    for m in range(micro):
+        out_ref[m, :, at : at + width] = total[m * rows : (m + 1) * rows]
+
+
+def half_kernel(pieces_ref, part_ref, out_ref):
+    combine_rows(pieces_ref, part_ref, out_ref, 0)
+
+
+def combine_kernel(half_ref, pieces_ref, *refs):
+    blocks, out_ref, rows_ref = refs[:-2], refs[-2], refs[-1]
     cap2 = blocks[0].shape[0]
+    width = half_ref.shape[2]
+    out_ref[:, :, :width] = half_ref[...]
     for shift, block in enumerate(blocks):
         rows_ref[shift * cap2 : (shift + 1) * cap2, :] = block[...]
-    at = 0
-    for pieces, part in ((whole_ref, first_ref), (shifted_ref, rows_ref)):
-        width = part.shape[1]
-        total = jnp.dot(pieces[...], part[...], preferred_element_type=jnp.float32)
-        total = (total[2 * each :] + total[each : 2 * each]) + total[:each]
-        total = total.astype(jnp.bfloat16)
-        for m in range(micro):
-            out_ref[m, :, at : at + width] = total[m * rows : (m + 1) * rows]
-        at += width
+    combine_rows(pieces_ref, rows_ref, out_ref, width)
 
 
 def local(dp, tensor, tokens, routes, probs, w_gate, w_up, w_down):
@@ -439,13 +446,19 @@
     for shift in reversed(range(1, dp)):
         swap = [(i, i ^ shift) for i in range(dp)]
         home[shift] = lax.ppermute(blocks[shift], "dp", swap)
+    half = pl.pallas_call(
+        half_kernel,
+        out_shape=jax.ShapeDtypeStruct((micro, rows, width), jnp.bfloat16),
+        compiler_params=pltpu.CompilerParams(vmem_limit_bytes=16 << 20),
+        name="half",
+    )(combine[0], *returned)
     mixed = pl.pallas_call(
         combine_kernel,
         out_shape=jax.ShapeDtypeStruct((micro, rows, features), jnp.bfloat16),
         scratch_shapes=[pltpu.VMEM((slots_all, width), jnp.bfloat16)],
         compiler_params=pltpu.CompilerParams(vmem_limit_bytes=16 << 20),
         name="combine",
-    )(*combine, *returned, *home)
+    )(half, combine[1], *home)
     return mixed, loss.T
 
 

time: 120 us -> 120 us (level)
  transfers between devices with their start and end apart: 27 -> 27, of which waited for: 7 -> 7; matrix products, arithmetic and copies ran while one was open for 1% -> 1% of each run, Pallas kernels for 26% -> 27%
where the time goes in v4:
time: 120 us; the launch traced here: 119 us
  Pallas kernels  44.1 us (37%)
  starting transfers between devices  36 us (30%)
  waiting for transfers between devices  30.5 us (25%)
  local copies, waits for them, and re-layouts  6.62 us (6%)
    pallas_call x4, Pallas kernels, gate_up(): pl.pallas_call(functools.partial(gate_up_kernel, plan), in_specs=[SMEM] +...  23.3 us
    ppermute x2, waiting for transfers between devices, local(): crossed.append(lax.ppermute(total, 'tensor', row))  12.7 us
    ppermute x7, starting transfers between devices, local(): arrived[shift] = lax.ppermute(sent[shift], 'dp', swap)  12.5 us
    pallas_call x4, Pallas kernels, down(): pl.pallas_call(functools.partial(down_kernel, (c, part, tile_of(columns,...  11.7 us
    ppermute x7, starting transfers between devices, local(): home[shift] = lax.ppermute(blocks[shift], 'dp', swap)  11.2 us
    ppermute x2, waiting for transfers between devices, local(): crossed.append(lax.ppermute(x, 'tensor', row))  9.57 us
    unnamed x9, local copies, waits for them, and re-layouts  6.62 us
    all_to_all x1, starting transfers between devices, local(): back = lax.all_to_all(total, 'dp', split_axis=0, concat_axis=0, tiled=True)  5.6 us
  transfers between devices with their start and end apart: 27, of which 7 were waited for; matrix products, arithmetic and copies ran while one was open for 1% of the time, Pallas kernels for 27%

profile of v4, /device:TPU:0, one launch (start us, length us, event | category | flops | bytes accessed | tf_op | source)
XLA Modules:
  0.0 119.2 jit_solution(5254773732160329317)
XLA Ops:
  0.6 1.6 %tables.1 = (bf16[328,128]{1,0:T(8,128)(2,1)S(1)}, bf16[328,128]{1,0:T(8,128)(2,1)S(1)}, bf16[328,128]{1,0:T(8,128)(2,1)S(1)}, bf16[328,128]{1,0:T(8,128)(2,1)S(...) custom-call(s32[1]{0:T(128)} %bitcast.where_ref, ...), custom_call_target="tpu_custom_call" | custom-call | tf_op jit(solution)/shard_map/tables/pallas_call | solution.py:367
  2.2 3.0 %collective-permute-start = (bf16[328,128]{1,0:T(8,128)(2,1)S(1)}, bf16[328,128]{1,0:T(8,128)(2,1)S(1)}, u32[]{:S(2)}, u32[]{:S(2)}) collective-permute-start(bf16[328,128]{1,0:T(8,128)(2,1)S(1)} %get-tuple-element.55), channel_id=1, source_target_pairs={{0,4},{4,0},{8,12},{12,8},{16,20},{20,16},{24,28},{28,24},{1,5},{5... | collective-permute-start | bytes 251912 | tf_op jit(solution)/shard_map/ppermute | solution.py:378
  5.3 1.6 %collective-permute-start.1 = (bf16[328,128]{1,0:T(8,128)(2,1)S(1)}, bf16[328,128]{1,0:T(8,128)(2,1)S(1)}, u32[]{:S(2)}, u32[]{:S(2)}) collective-permute-start(bf16[328,128]{1,0:T(8,128)(2,1)S(1)} %get-tuple-element.56), channel_id=1, source_target_pairs={{0,8},{4,12},{8,0},{12,4},{16,24},{20,28},{24,16},{28,20},{1,9},{5... | collective-permute-start | bytes 251912 | tf_op jit(solution)/shard_map/ppermute | solution.py:378
  6.8 3.0 %collective-permute-start.3 = (bf16[328,128]{1,0:T(8,128)(2,1)S(1)}, bf16[328,128]{1,0:T(8,128)(2,1)S(1)}, u32[]{:S(2)}, u32[]{:S(2)}) collective-permute-start(bf16[328,128]{1,0:T(8,128)(2,1)S(1)} %get-tuple-element.58), channel_id=1, source_target_pairs={{0,16},{4,20},{8,24},{12,28},{16,0},{20,4},{24,8},{28,12},{1,17},{... | collective-permute-start | bytes 251912 | tf_op jit(solution)/shard_map/ppermute | solution.py:378
  9.9 1.3 %collective-permute-start.4 = (bf16[328,128]{1,0:T(8,128)(2,1)S(1)}, bf16[328,128]{1,0:T(8,128)(2,1)S(1)}, u32[]{:S(2)}, u32[]{:S(2)}) collective-permute-start(bf16[328,128]{1,0:T(8,128)(2,1)S(1)} %get-tuple-element.59), channel_id=1, source_target_pairs={{0,20},{4,16},{8,28},{12,24},{16,4},{20,0},{24,12},{28,8},{1,21},{... | collective-permute-start | bytes 251912 | tf_op jit(solution)/shard_map/ppermute | solution.py:378
  11.1 3.6 %collective-permute-start.5 = (bf16[328,128]{1,0:T(8,128)(2,1)S(1)}, bf16[328,128]{1,0:T(8,128)(2,1)S(1)}, u32[]{:S(2)}, u32[]{:S(2)}) collective-permute-start(bf16[328,128]{1,0:T(8,128)(2,1)S(1)} %get-tuple-element.60), channel_id=1, source_target_pairs={{0,24},{4,28},{8,16},{12,20},{16,8},{20,12},{24,0},{28,4},{1,25},{... | collective-permute-start | bytes 251912 | tf_op jit(solution)/shard_map/ppermute | solution.py:378
  14.8 5.3 %first.1 = (bf16[1024,3584]{1,0:T(8,128)(2,1)S(1)}, bf16[1024,3584]{1,0:T(8,128)(2,1)S(1)}) custom-call(s32[1]{0:T(128)} %bitcast.3.where_ref, bf16[328,128]{1,0:T(8,128)(2,1)S(1)} %get-tuple-element.54.refs_0_.after_ref, bf16[1,4096,3584]{2,1,0:T(8,128)(2,1)} %refs_6_.4, bf16[1,4096,3584]{2,1,0:T(8,128)(2,1)} %refs_7_.3), custom_call_target="tpu_custom_call" | custom-call | tf_op jit(solution)/shard_map/first/pallas_call | solution.py:222
  20.1 3.3 %collective-permute-done.4.refs_5_ = bf16[328,128]{1,0:T(8,128)(2,1)S(1)} collective-permute-done((bf16[328,128]{1,0:T(8,128)(2,1)S(1)}, bf16[328,128]{1,0:T(8,128)(2,1)S(1)}, u32[]{:S(2)}, u32[]{:S(2)}) %collective-permute-start.4) | collective-permute-done | bytes 84000 | tf_op jit(solution)/shard_map/ppermute | solution.py:378
  23.4 0.2 repack.1
  23.7 1.6 %collective-permute-start.9 = (bf16[320,512]{1,0:T(8,128)(2,1)S(1)}, bf16[320,512]{1,0:T(8,128)(2,1)S(1)}, u32[]{:S(2)}, u32[]{:S(2)}) collective-permute-start(bf16[320,512]{1,0:T(8,128)(2,1)S(1)} %bitcast.20), channel_id=1, source_target_pairs={{0,2},{1,3},{2,0},{3,1},{4,6},{5,7},{6,4},{7,5},{8,10},{9,11},{10,... | collective-permute-start | bytes 983048 | tf_op jit(solution)/shard_map/ppermute | solution.py:395
  25.2 0.2 collective-permute-start.12
  25.4 0.5 collective-permute-start.7
  25.9 5.3 %shard_map.77 = (f32[320,3584]{1,0:T(8,128)S(1)}, f32[320,3584]{1,0:T(8,128)S(1)}, bf16[1024,3584]{1,0:T(8,128)(2,1)S(1)}, bf16[1024,3584]{1,0:T(8,128)(2,1)S(1)}) custom-call(s32[1]{0:T(128)} %bitcast.3.where_ref, bf16[320,512]{1,0:T(8,128)(2,1)S(1)} %bitcast.21, bf16[320,512]{1,0:T(8,128)(2,1)S(1)} %bitcast.18, ...), custom_call_target="tpu_custom_call" | custom-call | flops 4697620480 | bytes 14680064 | tf_op jit(solution)/shard_map/pallas_call | solution.py:248
  31.2 3.1 %collective-permute-done.9.refs_0_ = bf16[320,512]{1,0:T(8,128)(2,1)S(1)} collective-permute-done((bf16[320,512]{1,0:T(8,128)(2,1)S(1)}, bf16[320,512]{1,0:T(8,128)(2,1)S(1)}, u32[]{:S(2)}, u32[]{:S(2)}) %collective-permute-start.9) | collective-permute-done | bytes 327712 | tf_op jit(solution)/shard_map/ppermute | solution.py:395
  34.3 6.5 %collective-permute-done.7.refs_0_ = bf16[320,512]{1,0:T(8,128)(2,1)S(1)} collective-permute-done((bf16[320,512]{1,0:T(8,128)(2,1)S(1)}, bf16[320,512]{1,0:T(8,128)(2,1)S(1)}, u32[]{:S(2)}, u32[]{:S(2)}) %collective-permute-start.7) | collective-permute-done | bytes 327712 | tf_op jit(solution)/shard_map/ppermute | solution.py:395
  40.8 5.8 %shard_map.78 = (f32[320,3584]{1,0:T(8,128)S(1)}, f32[320,3584]{1,0:T(8,128)S(1)}, bf16[1024,3584]{1,0:T(8,128)(2,1)S(1)}, bf16[1024,3584]{1,0:T(8,128)(2,1)S(1)}) custom-call(s32[1]{0:T(128)} %bitcast.3.where_ref, bf16[320,512]{1,0:T(8,128)(2,1)S(1)} %collective-permute-done.11.refs_0_, ...), custom_call_target="tpu_custom_call", output_to_operand_aliasing={{0}: (5, {}), {1}: (6, {})} | custom-call | flops 4697620480 | bytes 14680064 | tf_op jit(solution)/shard_map/pallas_call | solution.py:248
  46.6 5.8 %shard_map.79 = (f32[320,3584]{1,0:T(8,128)S(1)}, f32[320,3584]{1,0:T(8,128)S(1)}, bf16[1024,3584]{1,0:T(8,128)(2,1)S(1)}, bf16[1024,3584]{1,0:T(8,128)(2,1)S(1)}) custom-call(s32[1]{0:T(128)} %bitcast.3.where_ref, bf16[320,512]{1,0:T(8,128)(2,1)S(1)} %collective-permute-done.9.refs_0_, ...), custom_call_target="tpu_custom_call", output_to_operand_aliasing={{0}: (5, {}), {1}: (6, {})} | custom-call | flops 4697620480 | bytes 14680064 | tf_op jit(solution)/shard_map/pallas_call | solution.py:248
  52.4 2.9 %copy-done = bf16[1024,3584]{1,0:T(8,128)(2,1)} copy-done((bf16[1024,3584]{1,0:T(8,128)(2,1)}, bf16[1024,3584]{1,0:T(8,128)(2,1)S(1)}, u32[]{:S(2)}) %copy-start) | copy-done | bytes 7340056
  55.3 3.1 %copy-done.1 = bf16[1024,3584]{1,0:T(8,128)(2,1)S(1)} copy-done((bf16[1024,3584]{1,0:T(8,128)(2,1)S(1)}, bf16[1024,3584]{1,0:T(8,128)(2,1)}, u32[]{:S(2)}) %copy-start.1) | copy-done | bytes 7340056
  58.4 6.4 %shard_map.80 = (bf16[320,3584]{1,0:T(8,128)(2,1)S(1)}, bf16[1792,2048]{1,0:T(8,128)(2,1)S(1)}, bf16[1792,2048]{1,0:T(8,128)(2,1)S(1)}) custom-call(s32[1]{0:T(128)} %bitcast.3.where_ref, bf16[320,512]{1,0:T(8,128)(2,1)S(1)} %collective-permute-done.7.refs_0_, bf16[320,512]{1,0:T(8,128)(2,1)S(1)} %collective-permute-done.8.refs_1_, ...), custom_call_target="tpu_custom_call" | custom-call | flops 4697620480 | bytes 14680064 | tf_op jit(solution)/shard_map/pallas_call | solution.py:248
  64.9 3.1 %shard_map.81 = (f32[320,512]{1,0:T(8,128)S(1)}, bf16[320,512]{1,0:T(8,128)(2,1)S(1)}, f32[8,128]{1,0:T(8,128)S(1)}, bf16[1792,2048]{1,0:T(8,128)(2,1)S(1)}) custom-call(s32[1]{0:T(128)} %bitcast.3.where_ref, bf16[320,3584]{1,0:T(8,128)(2,1)S(1)} %get-tuple-element.78.h_ref, bf16[1792,2048]{1,0:T(8,128)(2,1)S(1)} %get-tuple-element.79.w_a, ...), custom_call_target="tpu_custom_call" | custom-call | flops 2348810240 | bytes 7340032 | tf_op jit(solution)/shard_map/pallas_call | solution.py:303
  68.0 0.6 collective-permute-start.14
  68.5 3.1 %shard_map.82 = (f32[320,512]{1,0:T(8,128)S(1)}, bf16[320,512]{1,0:T(8,128)(2,1)S(1)}, f32[8,128]{1,0:T(8,128)S(1)}, bf16[1792,2048]{1,0:T(8,128)(2,1)S(1)}) custom-call(s32[1]{0:T(128)} %bitcast.3.where_ref, bf16[320,3584]{1,0:T(8,128)(2,1)S(1)} %get-tuple-element.78.h_ref, bf16[1792,2048]{1,0:T(8,128)(2,1)S(1)} %get-tuple-element.79.w_a, ...), custom_call_target="tpu_custom_call" | custom-call | flops 2348810240 | bytes 7340032 | tf_op jit(solution)/shard_map/pallas_call | solution.py:303
  71.6 2.8 %shard_map.83 = (f32[320,512]{1,0:T(8,128)S(1)}, bf16[320,512]{1,0:T(8,128)(2,1)S(1)}, f32[8,128]{1,0:T(8,128)S(1)}) custom-call(s32[1]{0:T(128)} %bitcast.3.where_ref, bf16[320,3584]{1,0:T(8,128)(2,1)S(1)} %get-tuple-element.78.h_ref, bf16[1792,2048]{1,0:T(8,128)(2,1)S(1)} %get-tuple-element.82.w_a, bf16[1792,2048]{1,0:T(8,128)(2,1)S(1)} %get-tuple-element.84.w_b, ...), custom_call_target="tpu_custom_call" | custom-call | flops 2348810240 | bytes 7340032 | tf_op jit(solution)/shard_map/pallas_call | solution.py:303
  74.6 1.6 %collective-permute-start.15 = (bf16[320,512]{1,0:T(8,128)(2,1)S(1)}, bf16[320,512]{1,0:T(8,128)(2,1)S(1)}, u32[]{:S(2)}, u32[]{:S(2)}) collective-permute-start(bf16[320,512]{1,0:T(8,128)(2,1)S(1)} %add_convert_fusion.2), channel_id=1, source_target_pairs={{0,2},{1,3},{2,0},{3,1},{4,6},{5,7},{6,4},{7,5},{8,10},{9,11},{10,... | collective-permute-start | bytes 983048 | tf_op jit(solution)/shard_map/ppermute | solution.py:430
  76.2 0.2 collective-permute-start.17
  76.4 2.8 %shard_map.84 = (f32[320,512]{1,0:T(8,128)S(1)}, bf16[320,512]{1,0:T(8,128)(2,1)S(1)}, f32[8,128]{1,0:T(8,128)S(1)}) custom-call(s32[1]{0:T(128)} %bitcast.3.where_ref, bf16[320,3584]{1,0:T(8,128)(2,1)S(1)} %get-tuple-element.78.h_ref, bf16[1792,2048]{1,0:T(8,128)(2,1)S(1)} %get-tuple-element.82.w_a, bf16[1792,2048]{1,0:T(8,128)(2,1)S(1)} %get-tuple-element.84.w_b, ...), custom_call_target="tpu_custom_call" | custom-call | flops 2348810240 | bytes 7340032 | tf_op jit(solution)/shard_map/pallas_call | solution.py:303
  79.2 0.4 collective-permute-start.16
  79.5 5.2 %collective-permute-done.15 = bf16[320,512]{1,0:T(8,128)(2,1)S(1)} collective-permute-done((bf16[320,512]{1,0:T(8,128)(2,1)S(1)}, bf16[320,512]{1,0:T(8,128)(2,1)S(1)}, u32[]{:S(2)}, u32[]{:S(2)}) %collective-permute-start.15) | collective-permute-done | bytes 327712 | tf_op jit(solution)/shard_map/ppermute | solution.py:430
  84.8 0.9 add_convert_fusion.1
  85.6 5.6 %all-to-all-start = ((bf16[8,40,512]{2,1,0:T(8,128)(2,1)}), bf16[8,40,512]{2,1,0:T(8,128)(2,1)S(1)}, u32[]{:S(2)}, u32[]{:S(2)}) async-start(bf16[8,40,512]{2,1,0:T(8,128)(2,1)} %bitcast.6), calls=%async_computation | async-start | bytes 655360 | tf_op jit(solution)/shard_map/all_to_all | solution.py:434
  91.2 0.1 add_convert_fusion
  91.3 1.6 %collective-permute-start.18 = (bf16[320,512]{1,0:T(8,128)(2,1)S(1)}, bf16[320,512]{1,0:T(8,128)(2,1)S(1)}, u32[]{:S(2)}, u32[]{:S(2)}) collective-permute-start(bf16[320,512]{1,0:T(8,128)(2,1)S(1)} %add_convert_fusion), channel_id=1, source_target_pairs={{0,2},{1,3},{2,0},{3,1},{4,6},{5,7},{6,4},{7,5},{8,10},{9,11},{10,... | collective-permute-start | bytes 983048 | tf_op jit(solution)/shard_map/ppermute | solution.py:430
  92.9 7.5 %collective-permute-done.18 = bf16[320,512]{1,0:T(8,128)(2,1)S(1)} collective-permute-done((bf16[320,512]{1,0:T(8,128)(2,1)S(1)}, bf16[320,512]{1,0:T(8,128)(2,1)S(1)}, u32[]{:S(2)}, u32[]{:S(2)}) %collective-permute-start.18) | collective-permute-done | bytes 327712 | tf_op jit(solution)/shard_map/ppermute | solution.py:430
  100.4 0.1 spread.1
  100.5 1.8 %collective-permute-start.19 = (bf16[40,512]{1,0:T(8,128)(2,1)S(1)}, bf16[40,512]{1,0:T(8,128)(2,1)S(1)}, u32[]{:S(2)}, u32[]{:S(2)}) collective-permute-start(bf16[40,512]{1,0:T(8,128)(2,1)S(1)} %get-tuple-element.99), channel_id=1, source_target_pairs={{0,4},{4,0},{8,12},{12,8},{16,20},{20,16},{24,28},{28,24},{1,5},{5... | collective-permute-start | bytes 122888 | tf_op jit(solution)/shard_map/ppermute | solution.py:448
  102.3 1.5 %collective-permute-start.20 = (bf16[40,512]{1,0:T(8,128)(2,1)S(1)}, bf16[40,512]{1,0:T(8,128)(2,1)S(1)}, u32[]{:S(2)}, u32[]{:S(2)}) collective-permute-start(bf16[40,512]{1,0:T(8,128)(2,1)S(1)} %get-tuple-element.100), channel_id=1, source_target_pairs={{0,8},{4,12},{8,0},{12,4},{16,24},{20,28},{24,16},{28,20},{1,9},{5... | collective-permute-start | bytes 122888 | tf_op jit(solution)/shard_map/ppermute | solution.py:448
  103.8 0.3 collective-permute-start.21
  104.0 2.6 %collective-permute-start.22 = (bf16[40,512]{1,0:T(8,128)(2,1)S(1)}, bf16[40,512]{1,0:T(8,128)(2,1)S(1)}, u32[]{:S(2)}, u32[]{:S(2)}) collective-permute-start(bf16[40,512]{1,0:T(8,128)(2,1)S(1)} %get-tuple-element.102), channel_id=1, source_target_pairs={{0,16},{4,20},{8,24},{12,28},{16,0},{20,4},{24,8},{28,12},{1,17},{... | collective-permute-start | bytes 122888 | tf_op jit(solution)/shard_map/ppermute | solution.py:448
  106.7 1.5 %collective-permute-start.23 = (bf16[40,512]{1,0:T(8,128)(2,1)S(1)}, bf16[40,512]{1,0:T(8,128)(2,1)S(1)}, u32[]{:S(2)}, u32[]{:S(2)}) collective-permute-start(bf16[40,512]{1,0:T(8,128)(2,1)S(1)} %get-tuple-element.103), channel_id=1, source_target_pairs={{0,20},{4,16},{8,28},{12,24},{16,4},{20,0},{24,12},{28,8},{1,21},{... | collective-permute-start | bytes 122888 | tf_op jit(solution)/shard_map/ppermute | solution.py:448
  108.2 3.3 %collective-permute-start.24 = (bf16[40,512]{1,0:T(8,128)(2,1)S(1)}, bf16[40,512]{1,0:T(8,128)(2,1)S(1)}, u32[]{:S(2)}, u32[]{:S(2)}) collective-permute-start(bf16[40,512]{1,0:T(8,128)(2,1)S(1)} %get-tuple-element.104), channel_id=1, source_target_pairs={{0,24},{4,28},{8,16},{12,20},{16,8},{20,12},{24,0},{28,4},{1,25},{... | collective-permute-start | bytes 122888 | tf_op jit(solution)/shard_map/ppermute | solution.py:448
  111.4 0.3 collective-permute-start.25
  111.7 0.6 copy.12
  112.3 0.4 weights.1
  112.8 0.4 half.1.half_ref
  113.2 0.8 collective-permute-done.24.refs_6_
  114.0 4.2 %collective-permute-done.25.refs_7_ = bf16[40,512]{1,0:T(8,128)(2,1)S(1)} collective-permute-done((bf16[40,512]{1,0:T(8,128)(2,1)S(1)}, bf16[40,512]{1,0:T(8,128)(2,1)S(1)}, u32[]{:S(2)}, u32[]{:S(2)}) %collective-permute-start.25) | collective-permute-done | bytes 40992 | tf_op jit(solution)/shard_map/ppermute | solution.py:448
  118.1 1.1 combine.1
  (33 shorter events, 0.4 us)
Async XLA Ops:
  2.2 8.9 %collective-permute-start = (bf16[328,128]{1,0:T(8,128)(2,1)S(1)}, bf16[328,128]{1,0:T(8,128)(2,1)S(1)}, u32[]{:S(2)}, u32[]{:S(2)}) collective-permute-start(bf16[328,128]{1,0:T(8,128)(2,1)S(1)} %get-tuple-element.55), channel_id=1, source_target_pairs={{0,4},{4,0},{8,12},{12,8},{16,20},{20,16},{24,28},{28,24},{1,5},{5... | collective-permute-start | bytes 251912 | tf_op jit(solution)/shard_map/ppermute | solution.py:378
  5.3 9.5 %collective-permute-start.1 = (bf16[328,128]{1,0:T(8,128)(2,1)S(1)}, bf16[328,128]{1,0:T(8,128)(2,1)S(1)}, u32[]{:S(2)}, u32[]{:S(2)}) collective-permute-start(bf16[328,128]{1,0:T(8,128)(2,1)S(1)} %get-tuple-element.56), channel_id=1, source_target_pairs={{0,8},{4,12},{8,0},{12,4},{16,24},{20,28},{24,16},{28,20},{1,9},{5... | collective-permute-start | bytes 251912 | tf_op jit(solution)/shard_map/ppermute | solution.py:378
  6.8 13.2 %collective-permute-start.2 = (bf16[328,128]{1,0:T(8,128)(2,1)S(1)}, bf16[328,128]{1,0:T(8,128)(2,1)S(1)}, u32[]{:S(2)}, u32[]{:S(2)}) collective-permute-start(bf16[328,128]{1,0:T(8,128)(2,1)S(1)} %get-tuple-element.57), channel_id=1, source_target_pairs={{0,12},{4,8},{8,4},{12,0},{16,28},{20,24},{24,20},{28,16},{1,13},{... | collective-permute-start | bytes 251912 | tf_op jit(solution)/shard_map/ppermute | solution.py:378
  6.8 13.3 %collective-permute-start.3 = (bf16[328,128]{1,0:T(8,128)(2,1)S(1)}, bf16[328,128]{1,0:T(8,128)(2,1)S(1)}, u32[]{:S(2)}, u32[]{:S(2)}) collective-permute-start(bf16[328,128]{1,0:T(8,128)(2,1)S(1)} %get-tuple-element.58), channel_id=1, source_target_pairs={{0,16},{4,20},{8,24},{12,28},{16,0},{20,4},{24,8},{28,12},{1,17},{... | collective-permute-start | bytes 251912 | tf_op jit(solution)/shard_map/ppermute | solution.py:378
  9.9 13.5 %collective-permute-start.4 = (bf16[328,128]{1,0:T(8,128)(2,1)S(1)}, bf16[328,128]{1,0:T(8,128)(2,1)S(1)}, u32[]{:S(2)}, u32[]{:S(2)}) collective-permute-start(bf16[328,128]{1,0:T(8,128)(2,1)S(1)} %get-tuple-element.59), channel_id=1, source_target_pairs={{0,20},{4,16},{8,28},{12,24},{16,4},{20,0},{24,12},{28,8},{1,21},{... | collective-permute-start | bytes 251912 | tf_op jit(solution)/shard_map/ppermute | solution.py:378
  11.1 12.3 %collective-permute-start.5 = (bf16[328,128]{1,0:T(8,128)(2,1)S(1)}, bf16[328,128]{1,0:T(8,128)(2,1)S(1)}, u32[]{:S(2)}, u32[]{:S(2)}) collective-permute-start(bf16[328,128]{1,0:T(8,128)(2,1)S(1)} %get-tuple-element.60), channel_id=1, source_target_pairs={{0,24},{4,28},{8,16},{12,20},{16,8},{20,12},{24,0},{28,4},{1,25},{... | collective-permute-start | bytes 251912 | tf_op jit(solution)/shard_map/ppermute | solution.py:378
  14.7 8.7 %collective-permute-start.6 = (bf16[328,128]{1,0:T(8,128)(2,1)S(1)}, bf16[328,128]{1,0:T(8,128)(2,1)S(1)}, u32[]{:S(2)}, u32[]{:S(2)}) collective-permute-start(bf16[328,128]{1,0:T(8,128)(2,1)S(1)} %get-tuple-element.61), channel_id=1, source_target_pairs={{0,28},{4,24},{8,20},{12,16},{16,12},{20,8},{24,4},{28,0},{1,29},{... | collective-permute-start | bytes 251912 | tf_op jit(solution)/shard_map/ppermute | solution.py:378
  23.6 17.2 %collective-permute-start.11 = (bf16[320,512]{1,0:T(8,128)(2,1)S(1)}, bf16[320,512]{1,0:T(8,128)(2,1)S(1)}, u32[]{:S(2)}, u32[]{:S(2)}) collective-permute-start(bf16[320,512]{1,0:T(8,128)(2,1)S(1)} %bitcast.19), channel_id=1, source_target_pairs={{0,1},{1,0},{2,3},{3,2},{4,5},{5,4},{6,7},{7,6},{8,9},{9,8},{10,11... | collective-permute-start | bytes 983048 | tf_op jit(solution)/shard_map/ppermute | solution.py:394
  23.7 10.7 %collective-permute-start.9 = (bf16[320,512]{1,0:T(8,128)(2,1)S(1)}, bf16[320,512]{1,0:T(8,128)(2,1)S(1)}, u32[]{:S(2)}, u32[]{:S(2)}) collective-permute-start(bf16[320,512]{1,0:T(8,128)(2,1)S(1)} %bitcast.20), channel_id=1, source_target_pairs={{0,2},{1,3},{2,0},{3,1},{4,6},{5,7},{6,4},{7,5},{8,10},{9,11},{10,... | collective-permute-start | bytes 983048 | tf_op jit(solution)/shard_map/ppermute | solution.py:395
  25.2 15.6 %collective-permute-start.12 = (bf16[320,512]{1,0:T(8,128)(2,1)S(1)}, bf16[320,512]{1,0:T(8,128)(2,1)S(1)}, u32[]{:S(2)}, u32[]{:S(2)}) collective-permute-start(bf16[320,512]{1,0:T(8,128)(2,1)S(1)} %bitcast.16), channel_id=1, source_target_pairs={{0,1},{1,0},{2,3},{3,2},{4,5},{5,4},{6,7},{7,6},{8,9},{9,8},{10,11... | collective-permute-start | bytes 983048 | tf_op jit(solution)/shard_map/ppermute | solution.py:394
  25.4 15.4 %collective-permute-start.7 = (bf16[320,512]{1,0:T(8,128)(2,1)S(1)}, bf16[320,512]{1,0:T(8,128)(2,1)S(1)}, u32[]{:S(2)}, u32[]{:S(2)}) collective-permute-start(bf16[320,512]{1,0:T(8,128)(2,1)S(1)} %bitcast.17), channel_id=1, source_target_pairs={{0,2},{1,3},{2,0},{3,1},{4,6},{5,7},{6,4},{7,5},{8,10},{9,11},{10,... | collective-permute-start | bytes 983048 | tf_op jit(solution)/shard_map/ppermute | solution.py:395
  34.3 12.3 %collective-permute-start.10 = (bf16[320,512]{1,0:T(8,128)(2,1)S(1)}, bf16[320,512]{1,0:T(8,128)(2,1)S(1)}, u32[]{:S(2)}, u32[]{:S(2)}) collective-permute-start(bf16[320,512]{1,0:T(8,128)(2,1)S(1)} %collective-permute-done.9.refs_0_), channel_id=1, source_target_pairs={{0,1},{1,0},{2,3},{3,2},{4,5},{5,4},{6,7},{7,6},{8,9},{9,8},{10,11... | collective-permute-start | bytes 983048 | tf_op jit(solution)/shard_map/ppermute | solution.py:398
  40.8 14.6 %collective-permute-start.8 = (bf16[320,512]{1,0:T(8,128)(2,1)S(1)}, bf16[320,512]{1,0:T(8,128)(2,1)S(1)}, u32[]{:S(2)}, u32[]{:S(2)}) collective-permute-start(bf16[320,512]{1,0:T(8,128)(2,1)S(1)} %collective-permute-done.7.refs_0_), channel_id=1, source_target_pairs={{0,1},{1,0},{2,3},{3,2},{4,5},{5,4},{6,7},{7,6},{8,9},{9,8},{10,11... | collective-permute-start | bytes 983048 | tf_op jit(solution)/shard_map/ppermute | solution.py:398
  52.4 2.9 %copy-start = (bf16[1024,3584]{1,0:T(8,128)(2,1)}, bf16[1024,3584]{1,0:T(8,128)(2,1)S(1)}, u32[]{:S(2)}) copy-start(bf16[1024,3584]{1,0:T(8,128)(2,1)S(1)} %get-tuple-element.74.refs_2_) | copy-start | bytes 22020100
  55.3 3.1 %copy-start.1 = (bf16[1024,3584]{1,0:T(8,128)(2,1)S(1)}, bf16[1024,3584]{1,0:T(8,128)(2,1)}, u32[]{:S(2)}) copy-start(bf16[1024,3584]{1,0:T(8,128)(2,1)} %copy-done) | copy-start | bytes 22020100
  68.0 6.5 %collective-permute-start.14 = (bf16[320,512]{1,0:T(8,128)(2,1)S(1)}, bf16[320,512]{1,0:T(8,128)(2,1)S(1)}, u32[]{:S(2)}, u32[]{:S(2)}) collective-permute-start(bf16[320,512]{1,0:T(8,128)(2,1)S(1)} %get-tuple-element.92), channel_id=1, source_target_pairs={{0,1},{1,0},{2,3},{3,2},{4,5},{5,4},{6,7},{7,6},{8,9},{9,8},{10,11... | collective-permute-start | bytes 983048 | tf_op jit(solution)/shard_map/ppermute | solution.py:417
  74.4 5.1 %collective-permute-start.13 = (bf16[320,512]{1,0:T(8,128)(2,1)S(1)}, bf16[320,512]{1,0:T(8,128)(2,1)S(1)}, u32[]{:S(2)}, u32[]{:S(2)}) collective-permute-start(bf16[320,512]{1,0:T(8,128)(2,1)S(1)} %get-tuple-element.90), channel_id=1, source_target_pairs={{0,1},{1,0},{2,3},{3,2},{4,5},{5,4},{6,7},{7,6},{8,9},{9,8},{10,11... | collective-permute-start | bytes 983048 | tf_op jit(solution)/shard_map/ppermute | solution.py:417
  74.6 10.2 %collective-permute-start.15 = (bf16[320,512]{1,0:T(8,128)(2,1)S(1)}, bf16[320,512]{1,0:T(8,128)(2,1)S(1)}, u32[]{:S(2)}, u32[]{:S(2)}) collective-permute-start(bf16[320,512]{1,0:T(8,128)(2,1)S(1)} %add_convert_fusion.2), channel_id=1, source_target_pairs={{0,2},{1,3},{2,0},{3,1},{4,6},{5,7},{6,4},{7,5},{8,10},{9,11},{10,... | collective-permute-start | bytes 983048 | tf_op jit(solution)/shard_map/ppermute | solution.py:430
  76.2 15.0 %collective-permute-start.17 = (bf16[320,512]{1,0:T(8,128)(2,1)S(1)}, bf16[320,512]{1,0:T(8,128)(2,1)S(1)}, u32[]{:S(2)}, u32[]{:S(2)}) collective-permute-start(bf16[320,512]{1,0:T(8,128)(2,1)S(1)} %get-tuple-element.97), channel_id=1, source_target_pairs={{0,1},{1,0},{2,3},{3,2},{4,5},{5,4},{6,7},{7,6},{8,9},{9,8},{10,11... | collective-permute-start | bytes 983048 | tf_op jit(solution)/shard_map/ppermute | solution.py:417
  76.4 35.9 %copy-start.2 = (f32[2,64,8]{1,2,0:T(8,128)S(1)}, f32[2,64,8]{1,2,0:T(8,128)}, u32[]{:S(2)}) copy-start(f32[2,64,8]{1,2,0:T(8,128)} %param.8) | copy-start | bytes 12292
  76.4 35.9 %copy-start.3 = (s32[2,64,2]{1,2,0:T(2,128)S(1)}, s32[2,64,2]{1,2,0:T(2,128)}, u32[]{:S(2)}) copy-start(s32[2,64,2]{1,2,0:T(2,128)} %param.7) | copy-start | bytes 3076
  79.2 13.8 %collective-permute-start.16 = (bf16[320,512]{1,0:T(8,128)(2,1)S(1)}, bf16[320,512]{1,0:T(8,128)(2,1)S(1)}, u32[]{:S(2)}, u32[]{:S(2)}) collective-permute-start(bf16[320,512]{1,0:T(8,128)(2,1)S(1)} %get-tuple-element.95), channel_id=1, source_target_pairs={{0,1},{1,0},{2,3},{3,2},{4,5},{5,4},{6,7},{7,6},{8,9},{9,8},{10,11... | collective-permute-start | bytes 983048 | tf_op jit(solution)/shard_map/ppermute | solution.py:417
  85.6 27.2 %all-to-all-start = ((bf16[8,40,512]{2,1,0:T(8,128)(2,1)}), bf16[8,40,512]{2,1,0:T(8,128)(2,1)S(1)}, u32[]{:S(2)}, u32[]{:S(2)}) async-start(bf16[8,40,512]{2,1,0:T(8,128)(2,1)} %bitcast.6), calls=%async_computation | async-start | bytes 655360 | tf_op jit(solution)/shard_map/all_to_all | solution.py:434
  91.3 9.0 %collective-permute-start.18 = (bf16[320,512]{1,0:T(8,128)(2,1)S(1)}, bf16[320,512]{1,0:T(8,128)(2,1)S(1)}, u32[]{:S(2)}, u32[]{:S(2)}) collective-permute-start(bf16[320,512]{1,0:T(8,128)(2,1)S(1)} %add_convert_fusion), channel_id=1, source_target_pairs={{0,2},{1,3},{2,0},{3,1},{4,6},{5,7},{6,4},{7,5},{8,10},{9,11},{10,... | collective-permute-start | bytes 983048 | tf_op jit(solution)/shard_map/ppermute | solution.py:430
  100.5 7.7 %collective-permute-start.19 = (bf16[40,512]{1,0:T(8,128)(2,1)S(1)}, bf16[40,512]{1,0:T(8,128)(2,1)S(1)}, u32[]{:S(2)}, u32[]{:S(2)}) collective-permute-start(bf16[40,512]{1,0:T(8,128)(2,1)S(1)} %get-tuple-element.99), channel_id=1, source_target_pairs={{0,4},{4,0},{8,12},{12,8},{16,20},{20,16},{24,28},{28,24},{1,5},{5... | collective-permute-start | bytes 122888 | tf_op jit(solution)/shard_map/ppermute | solution.py:448
  102.3 9.1 %collective-permute-start.20 = (bf16[40,512]{1,0:T(8,128)(2,1)S(1)}, bf16[40,512]{1,0:T(8,128)(2,1)S(1)}, u32[]{:S(2)}, u32[]{:S(2)}) collective-permute-start(bf16[40,512]{1,0:T(8,128)(2,1)S(1)} %get-tuple-element.100), channel_id=1, source_target_pairs={{0,8},{4,12},{8,0},{12,4},{16,24},{20,28},{24,16},{28,20},{1,9},{5... | collective-permute-start | bytes 122888 | tf_op jit(solution)/shard_map/ppermute | solution.py:448
  103.8 9.4 %collective-permute-start.21 = (bf16[40,512]{1,0:T(8,128)(2,1)S(1)}, bf16[40,512]{1,0:T(8,128)(2,1)S(1)}, u32[]{:S(2)}, u32[]{:S(2)}) collective-permute-start(bf16[40,512]{1,0:T(8,128)(2,1)S(1)} %get-tuple-element.101), channel_id=1, source_target_pairs={{0,12},{4,8},{8,4},{12,0},{16,28},{20,24},{24,20},{28,16},{1,13},{... | collective-permute-start | bytes 122888 | tf_op jit(solution)/shard_map/ppermute | solution.py:448
  104.0 9.1 %collective-permute-start.22 = (bf16[40,512]{1,0:T(8,128)(2,1)S(1)}, bf16[40,512]{1,0:T(8,128)(2,1)S(1)}, u32[]{:S(2)}, u32[]{:S(2)}) collective-permute-start(bf16[40,512]{1,0:T(8,128)(2,1)S(1)} %get-tuple-element.102), channel_id=1, source_target_pairs={{0,16},{4,20},{8,24},{12,28},{16,0},{20,4},{24,8},{28,12},{1,17},{... | collective-permute-start | bytes 122888 | tf_op jit(solution)/shard_map/ppermute | solution.py:448
  106.7 6.5 %collective-permute-start.23 = (bf16[40,512]{1,0:T(8,128)(2,1)S(1)}, bf16[40,512]{1,0:T(8,128)(2,1)S(1)}, u32[]{:S(2)}, u32[]{:S(2)}) collective-permute-start(bf16[40,512]{1,0:T(8,128)(2,1)S(1)} %get-tuple-element.103), channel_id=1, source_target_pairs={{0,20},{4,16},{8,28},{12,24},{16,4},{20,0},{24,12},{28,8},{1,21},{... | collective-permute-start | bytes 122888 | tf_op jit(solution)/shard_map/ppermute | solution.py:448
  108.2 5.8 %collective-permute-start.24 = (bf16[40,512]{1,0:T(8,128)(2,1)S(1)}, bf16[40,512]{1,0:T(8,128)(2,1)S(1)}, u32[]{:S(2)}, u32[]{:S(2)}) collective-permute-start(bf16[40,512]{1,0:T(8,128)(2,1)S(1)} %get-tuple-element.104), channel_id=1, source_target_pairs={{0,24},{4,28},{8,16},{12,20},{16,8},{20,12},{24,0},{28,4},{1,25},{... | collective-permute-start | bytes 122888 | tf_op jit(solution)/shard_map/ppermute | solution.py:448
  111.4 6.7 %collective-permute-start.25 = (bf16[40,512]{1,0:T(8,128)(2,1)S(1)}, bf16[40,512]{1,0:T(8,128)(2,1)S(1)}, u32[]{:S(2)}, u32[]{:S(2)}) collective-permute-start(bf16[40,512]{1,0:T(8,128)(2,1)S(1)} %get-tuple-element.105), channel_id=1, source_target_pairs={{0,28},{4,24},{8,20},{12,16},{16,12},{20,8},{24,4},{28,0},{1,29},{... | collective-permute-start | bytes 122888 | tf_op jit(solution)/shard_map/ppermute | solution.py:448
